TPU v7x, 256 devices: a whole 4x4x8 slice. The times are simulated.
256 devices in a mesh: gx: 16 (over z, core), gy: 8 (over x_hi, y), gz: 2 (over x_lo).
Axes of the slice: x: 4 (x_hi: 2, x_lo: 2; x = x_hi * 2 + x_lo), y: 4, z: 8, core: 2. Of those that a mesh axis runs over, the one named last changes fastest.
Arguments:
- load_current: float32 [1536, 8192], P('gy', 'gx'), may hold values from 0 to 90
- sink_mask: int32 [1536, 8192], P('gy', 'gx'), may hold values 0 or 1
- pad_mask: int32 [1536, 8192], P('gy', 'gx'), may hold values from 0 to 1, as said below
- plane_class: int32 [4, 1536, 8192], P('gz', 'gy', 'gx'), may hold values from 0 to 7
- via_class: int32 [4, 1536, 8192], P('gz', 'gy', 'gx'), may hold values from 0 to 7
- plane_table: float32 [4, 8], P('gz'), may hold values from 0.25 to 4
- via_table: float32 [4, 8], P('gz'), may hold values from 0.25 to 4
Outputs:
- voltage: float32 [4, 1536, 8192], P('gz', 'gy', 'gx')
- residual: float32 [4, 1536, 8192], P('gz', 'gy', 'gx')
Inputs may be any that keep to these rules, and one draw needn't show every extreme that they name: `pad_mask`: exactly one pad in each aligned 8 x 8 tile of nodes.
All inputs are finite; a program needn't handle non-finite values. No bound on the sum of `sink_mask` on one device may be relied on, other than what follows from the above.
Results may differ from a plain program's by a relative error of at most 0.00012.
Values sent between devices are 32-bit elements; how exact they have to be, the bound alone decides.
No kernel may reach another device: no remote copies, remote signals or barrier semaphores. Data moves between devices by JAX's collectives and lax.ppermute only.
A program may use at most 64 MiB of HBM per device.

v0:
```python
import jax
import jax.numpy as jnp
from jax import lax
from jax.sharding import Mesh
from jax.sharding import PartitionSpec as P

ITERS = 3
GX = ("gx_0", "gx_1")
GY = ("gy_0", "gy_1")
GX_GY_GZ = ("gx_0", "gx_1", "gy_0", "gy_1", "gz")


PAD_CONDUCTANCE = 20.0


def padded(array, sides, width):
    edges = {}
    for axis, dim in sides:
        peers, length = (lax.axis_size(axis), array.shape[dim])
        up = [(i, (i + 1) % peers) for i in range(peers)]
        last = lax.slice_in_dim(array, length - width, length, axis=dim)
        leading = lax.slice_in_dim(array, 0, width, axis=dim)
        edges[dim] = (
            lax.ppermute(last, axis, up),
            lax.ppermute(leading, axis, [(b, a) for a, b in up]),
        )
    done = []
    for _, dim in sides:
        low, high = edges[dim]
        around = [(width, width) if d in done else (0, 0) for d in range(array.ndim)]
        array = jnp.concatenate([jnp.pad(low, around), array, jnp.pad(high, around)], axis=dim)
        done.append(dim)
    return array


def padded_2(block, sides, width):
    for axis, dim in sides:
        count = lax.axis_size(axis)
        forward = [(i, i + 1) for i in range(count - 1)]
        backward = [(target, source) for source, target in forward]
        low = lax.ppermute(
            lax.slice_in_dim(block, block.shape[dim] - width, None, axis=dim), axis, forward
        )
        high = lax.ppermute(lax.slice_in_dim(block, 0, width, axis=dim), axis, backward)
        block = jnp.concatenate([low, block, high], axis=dim)
    return block


def by_axis(array, axes):
    for axis in axes:
        array = lax.psum(array, axis)
    return array


def lookup(classes, table):
    summed = jnp.zeros(classes.shape, jnp.float32)
    for level in range(table.shape[1]):
        summed = summed + jnp.where(
            classes == level, table[:, level][:, None, None], jnp.float32(0.0)
        )
    return summed


def harmonic(first, second):
    return 2.0 * first * second / (first + second)


def factor(diagonal, up_edge):
    inverses = []
    factors = []
    for level in range(diagonal.shape[0]):
        pivots = diagonal[level]
        if level > 0:
            pivots = pivots + up_edge[level - 1] * factors[level - 1]
        inverse = 1.0 / pivots
        inverses.append(inverse)
        factors.append(-up_edge[level] * inverse)
    return (jnp.stack(inverses), jnp.stack(factors))


def solve_block(inverses, factors, up_edge, source_term):
    forward = []
    for level in range(source_term.shape[0]):
        entries = source_term[level]
        if level > 0:
            entries = entries + up_edge[level - 1] * forward[level - 1]
        forward.append(entries * inverses[level])
    result = [forward[-1]]
    level = 0
    result.insert(0, forward[level] - factors[level] * result[0])
    return jnp.stack(result)


def plane_extend(field):
    return padded(field, ((GX, 2), (GY, 1)), 1)


def layer_extend(field):
    return padded_2(field, (("gz", 0),), 1)


def merged_sums(residual, precond, image_field):
    return (
        by_axis(jnp.sum(residual * precond), GX_GY_GZ),
        by_axis(jnp.sum(image_field * precond), GX_GY_GZ),
    )


def shards(load_current, sink_mask, pad_mask, plane_class, via_class, plane_table, via_table):
    n_layers, n_rows, n_cols = plane_class.shape
    g_plane = lookup(plane_class, plane_table)
    g_via = lookup(via_class, via_table)
    plane_ext = plane_extend(g_plane)
    middle = plane_ext[:, 1:-1, :]
    across = harmonic(middle[:, :, :-1], middle[:, :, 1:])
    east_edge = across[:, :, 1:]
    west_edge = across[:, :, :-1]
    column = plane_ext[:, :, 1:-1]
    along_rows = harmonic(column[:, :-1], column[:, 1:])
    north_edge = along_rows[:, 1:]
    south_edge = along_rows[:, :-1]
    via_ext = layer_extend(g_via)
    vertical = harmonic(via_ext[:-1], via_ext[1:])
    up_edge = vertical[1:]
    down_edge = vertical[:-1]
    group_index = lax.axis_index("gz")
    is_top = group_index == lax.axis_size("gz") - 1
    is_bottom = group_index == 0
    pad_plane = jnp.where(is_top, PAD_CONDUCTANCE * pad_mask.astype(jnp.float32), jnp.float32(0.0))
    pad_layer = jnp.concatenate(
        [jnp.zeros((n_layers - 1, n_rows, n_cols), jnp.float32), pad_plane[None]], 0
    )
    diagonal = east_edge + west_edge + north_edge + south_edge + up_edge + down_edge + pad_layer
    inverses, factors = factor(diagonal, up_edge)

    def precondition(residual):
        return solve_block(inverses, factors, up_edge, residual)

    def operate(field):
        inner = plane_extend(field)
        layer_ext = layer_extend(field)
        above_field = layer_ext[2:]
        below_field = layer_ext[:-2]
        return (
            diagonal * field
            - east_edge * inner[:, 1:-1, 2:]
            - west_edge * inner[:, 1:-1, :-2]
            - north_edge * inner[:, 2:, 1:-1]
            - south_edge * inner[:, :-2, 1:-1]
            - up_edge * above_field
            - down_edge * below_field
        )

    source = jnp.where(is_bottom, sink_mask.astype(jnp.float32) * load_current, jnp.float32(0.0))
    right_side = jnp.concatenate(
        [source[None], jnp.zeros((n_layers - 1, n_rows, n_cols), jnp.float32)], 0
    )
    voltage = jnp.zeros((n_layers, n_rows, n_cols), jnp.float32)
    residual = right_side
    precond = precondition(residual)
    image_field = operate(precond)
    weight_now, curvature = merged_sums(residual, precond, image_field)
    step_size = weight_now / curvature
    direction = precond
    image_dir = image_field
    for iteration in range(ITERS):
        voltage = voltage + step_size * direction
        residual = residual - step_size * image_dir
        if iteration + 1 < ITERS:
            precond = precondition(residual)
            image_field = operate(precond)
            weight_next, curvature = merged_sums(residual, precond, image_field)
            momentum = weight_next / weight_now
            step_size = weight_next / (curvature - momentum * weight_next / step_size)
            direction = precond + momentum * direction
            image_dir = image_field + momentum * image_dir
            weight_now = weight_next
    return (voltage, residual)


def solution(mesh):
    split = Mesh(
        mesh.devices.reshape(8, 2, 2, 4, mesh.shape["gz"]), ("gx_0", "gx_1", "gy_0", "gy_1", "gz")
    )
    placed = (
        P(GY, GX),
        P(GY, GX),
        P(GY, GX),
        P("gz", GY, GX),
        P("gz", GY, GX),
        P("gz", None),
        P("gz", None),
    )
    return jax.shard_map(
        shards,
        mesh=split,
        in_specs=placed,
        out_specs=(P("gz", GY, GX), P("gz", GY, GX)),
        check_vma=False,
    )
```

profile of v0, /device:TPU:1, one launch (start us, length us, event | category | flops | bytes accessed | tf_op | source)
XLA Modules:
  0.0 243.1 jit_solution(2650260789971561995)
XLA Ops:
  16.5 4.5 %collective-permute-start.3 = (f32[2,1,512]{2,1,0:T(1,128)S(1)}, f32[2,1,512]{2,1,0:T(1,128)S(1)}, u32[]{:S(2)}, u32[]{:S(2)}) collective-permute-start(f32[2,1,512]{2,1,0:T(1,128)S(1)} %get-tuple-element.76), channel_id=1, source_target_pairs={{2,0},{4,2},{6,4},{8,6},{10,8},{12,10},{14,12},{0,14},{3,1},{5,3},... | collective-permute-start | bytes 12296 | tf_op jit(solution)/shard_map/ppermute | solution.py:25
  28.9 4.0 %collective-permute-start.11 = (f32[1,192,512]{2,1,0:T(8,128)S(1)}, f32[1,192,512]{2,1,0:T(8,128)S(1)}, u32[]{:S(2)}, u32[]{:S(2)}) collective-permute-start(f32[1,192,512]{2,1,0:T(8,128)S(1)} %get-tuple-element.61), channel_id=1, source_target_pairs={{0,1},{2,3},{4,5},{6,7},{8,9},{10,11},{12,13},{14,15},{16,17},{18,... | collective-permute-start | bytes 1179656 | tf_op jit(solution)/shard_map/ppermute | solution.py:41
  32.9 5.3 %collective-permute-start.8 = (f32[2,1,512]{2,1,0:T(1,128)S(1)}, f32[2,1,512]{2,1,0:T(1,128)S(1)}, u32[]{:S(2)}, u32[]{:S(2)}) collective-permute-start(f32[2,1,512]{2,1,0:T(1,128)S(1)} %get-tuple-element.71), channel_id=1, source_target_pairs={{2,0},{4,2},{6,4},{8,6},{10,8},{12,10},{14,12},{0,14},{3,1},{5,3},... | collective-permute-start | bytes 12296 | tf_op jit(solution)/shard_map/ppermute | solution.py:25
  38.3 6.7 %collective-permute-start.7 = (f32[2,192,1]{2,1,0:T(8,128)S(1)}, f32[2,192,1]{2,1,0:T(8,128)S(1)}, u32[]{:S(2)}, u32[]{:S(2)}) collective-permute-start(f32[2,192,1]{2,1,0:T(8,128)S(1)} %get-tuple-element.73), channel_id=1, source_target_pairs={{0,16},{16,32},{32,48},{48,64},{64,80},{80,96},{96,112},{112,128},... | collective-permute-start | bytes 4616 | tf_op jit(solution)/shard_map/ppermute | solution.py:24
  56.6 15.4 %all-reduce.12 = (f32[]{:T(128)}, f32[]{:T(128)}) all-reduce(f32[]{:T(128)} %get-tuple-element.7, f32[]{:T(128)} %get-tuple-element.6), channel_id=1, replica_groups=mesh['gx_0'=8,'gx_1'=2,'gy_0'=2,'gy_1'=4,'gz'=2] {'gx_0'}, use_global_device_ids=true, to_apply=%region_1.2 | all-reduce | flops 2 | bytes 16 | tf_op jit(solution)/shard_map/psum | solution.py:51
  71.9 4.9 %all-reduce.24 = (f32[]{:T(128)}, f32[]{:T(128)}) all-reduce(f32[]{:T(128)} %get-tuple-element.28, f32[]{:T(128)} %get-tuple-element.29), channel_id=1, replica_groups=mesh['gx_0'=8,'gx_1'=2,'gy_0'=2,'gy_1'=4,'gz'=2] {'gx_1'}, use_global_device_ids=true, to_apply=%region_2.3 | all-reduce | flops 2 | bytes 16 | tf_op jit(solution)/shard_map/psum | solution.py:51
  76.8 6.0 %all-reduce.21 = (f32[]{:T(128)}, f32[]{:T(128)}) all-reduce(f32[]{:T(128)} %get-tuple-element.52, f32[]{:T(128)} %get-tuple-element.53), channel_id=1, replica_groups=mesh['gx_0'=8,'gx_1'=2,'gy_0'=2,'gy_1'=4,'gz'=2] {'gy_0'}, use_global_device_ids=true, to_apply=%region_3.4 | all-reduce | flops 2 | bytes 16 | tf_op jit(solution)/shard_map/psum | solution.py:51
  82.8 10.5 %all-reduce.15 = (f32[]{:T(128)}, f32[]{:T(128)}) all-reduce(f32[]{:T(128)} %get-tuple-element.46, f32[]{:T(128)} %get-tuple-element.47), channel_id=1, replica_groups=mesh['gx_0'=8,'gx_1'=2,'gy_0'=2,'gy_1'=4,'gz'=2] {'gy_1'}, use_global_device_ids=true, to_apply=%region_4.5 | all-reduce | flops 2 | bytes 16 | tf_op jit(solution)/shard_map/psum | solution.py:51
  93.3 4.4 %all-reduce.18 = (f32[]{:T(128)}, f32[]{:T(128)}) all-reduce(f32[]{:T(128)} %get-tuple-element.34, f32[]{:T(128)} %get-tuple-element.35), channel_id=1, replica_groups=mesh['gx_0'=8,'gx_1'=2,'gy_0'=2,'gy_1'=4,'gz'=2] {'gz'}, use_global_device_ids=true, to_apply=%region_5.6 | all-reduce | flops 2 | bytes 16 | tf_op jit(solution)/shard_map/psum | solution.py:51
  102.1 4.0 %collective-permute-start.17 = (f32[1,192,512]{2,1,0:T(8,128)S(1)}, f32[1,192,512]{2,1,0:T(8,128)S(1)}, u32[]{:S(2)}, u32[]{:S(2)}) collective-permute-start(f32[1,192,512]{2,1,0:T(8,128)S(1)} %get-tuple-element.59), channel_id=1, source_target_pairs={{0,1},{2,3},{4,5},{6,7},{8,9},{10,11},{12,13},{14,15},{16,17},{18,... | collective-permute-start | bytes 1179656 | tf_op jit(solution)/shard_map/ppermute | solution.py:41
  107.9 5.8 %collective-permute-start.13 = (f32[2,192,1]{2,1,0:T(8,128)S(1)}, f32[2,192,1]{2,1,0:T(8,128)S(1)}, u32[]{:S(2)}, u32[]{:S(2)}) collective-permute-start(f32[2,192,1]{2,1,0:T(8,128)S(1)} %get-tuple-element.69), channel_id=1, source_target_pairs={{0,16},{16,32},{32,48},{48,64},{64,80},{80,96},{96,112},{112,128},... | collective-permute-start | bytes 4616 | tf_op jit(solution)/shard_map/ppermute | solution.py:24
  125.4 15.1 %all-reduce.11 = (f32[]{:T(128)}, f32[]{:T(128)}) all-reduce(f32[]{:T(128)} %get-tuple-element.5, f32[]{:T(128)} %get-tuple-element.4), channel_id=1, replica_groups=mesh['gx_0'=8,'gx_1'=2,'gy_0'=2,'gy_1'=4,'gz'=2] {'gx_0'}, use_global_device_ids=true, to_apply=%region_13.14 | all-reduce | flops 2 | bytes 16 | tf_op jit(solution)/shard_map/psum | solution.py:51
  140.5 4.1 %all-reduce.23 = (f32[]{:T(128)}, f32[]{:T(128)}) all-reduce(f32[]{:T(128)} %get-tuple-element.26, f32[]{:T(128)} %get-tuple-element.27), channel_id=1, replica_groups=mesh['gx_0'=8,'gx_1'=2,'gy_0'=2,'gy_1'=4,'gz'=2] {'gx_1'}, use_global_device_ids=true, to_apply=%region_14.15 | all-reduce | flops 2 | bytes 16 | tf_op jit(solution)/shard_map/psum | solution.py:51
  144.6 5.9 %all-reduce.20 = (f32[]{:T(128)}, f32[]{:T(128)}) all-reduce(f32[]{:T(128)} %get-tuple-element.50, f32[]{:T(128)} %get-tuple-element.51), channel_id=1, replica_groups=mesh['gx_0'=8,'gx_1'=2,'gy_0'=2,'gy_1'=4,'gz'=2] {'gy_0'}, use_global_device_ids=true, to_apply=%region_15.16 | all-reduce | flops 2 | bytes 16 | tf_op jit(solution)/shard_map/psum | solution.py:51
  150.5 9.8 %all-reduce.14 = (f32[]{:T(128)}, f32[]{:T(128)}) all-reduce(f32[]{:T(128)} %get-tuple-element.44, f32[]{:T(128)} %get-tuple-element.45), channel_id=1, replica_groups=mesh['gx_0'=8,'gx_1'=2,'gy_0'=2,'gy_1'=4,'gz'=2] {'gy_1'}, use_global_device_ids=true, to_apply=%region_16.17 | all-reduce | flops 2 | bytes 16 | tf_op jit(solution)/shard_map/psum | solution.py:51
  160.3 4.4 %all-reduce.17 = (f32[]{:T(128)}, f32[]{:T(128)}) all-reduce(f32[]{:T(128)} %get-tuple-element.32, f32[]{:T(128)} %get-tuple-element.33), channel_id=1, replica_groups=mesh['gx_0'=8,'gx_1'=2,'gy_0'=2,'gy_1'=4,'gz'=2] {'gz'}, use_global_device_ids=true, to_apply=%region_17.18 | all-reduce | flops 2 | bytes 16 | tf_op jit(solution)/shard_map/psum | solution.py:51
  172.6 4.0 %collective-permute-start.23 = (f32[1,192,512]{2,1,0:T(8,128)S(1)}, f32[1,192,512]{2,1,0:T(8,128)S(1)}, u32[]{:S(2)}, u32[]{:S(2)}) collective-permute-start(f32[1,192,512]{2,1,0:T(8,128)S(1)} %get-tuple-element.56), channel_id=1, source_target_pairs={{0,1},{2,3},{4,5},{6,7},{8,9},{10,11},{12,13},{14,15},{16,17},{18,... | collective-permute-start | bytes 1179656 | tf_op jit(solution)/shard_map/ppermute | solution.py:41
  178.3 7.0 %collective-permute-start.19 = (f32[2,192,1]{2,1,0:T(8,128)S(1)}, f32[2,192,1]{2,1,0:T(8,128)S(1)}, u32[]{:S(2)}, u32[]{:S(2)}) collective-permute-start(f32[2,192,1]{2,1,0:T(8,128)S(1)} %get-tuple-element.65), channel_id=1, source_target_pairs={{0,16},{16,32},{32,48},{48,64},{64,80},{80,96},{96,112},{112,128},... | collective-permute-start | bytes 4616 | tf_op jit(solution)/shard_map/ppermute | solution.py:24
  197.0 13.9 %all-reduce.10 = (f32[]{:T(128)}, f32[]{:T(128)}) all-reduce(f32[]{:T(128)} %get-tuple-element.3, f32[]{:T(128)} %get-tuple-element.2), channel_id=1, replica_groups=mesh['gx_0'=8,'gx_1'=2,'gy_0'=2,'gy_1'=4,'gz'=2] {'gx_0'}, use_global_device_ids=true, to_apply=%region_25.26 | all-reduce | flops 2 | bytes 16 | tf_op jit(solution)/shard_map/psum | solution.py:51
  210.8 4.0 %all-reduce.22 = (f32[]{:T(128)}, f32[]{:T(128)}) all-reduce(f32[]{:T(128)} %get-tuple-element.24, f32[]{:T(128)} %get-tuple-element.25), channel_id=1, replica_groups=mesh['gx_0'=8,'gx_1'=2,'gy_0'=2,'gy_1'=4,'gz'=2] {'gx_1'}, use_global_device_ids=true, to_apply=%region_26.27 | all-reduce | flops 2 | bytes 16 | tf_op jit(solution)/shard_map/psum | solution.py:51
  214.8 5.9 %all-reduce.19 = (f32[]{:T(128)}, f32[]{:T(128)}) all-reduce(f32[]{:T(128)} %get-tuple-element.48, f32[]{:T(128)} %get-tuple-element.49), channel_id=1, replica_groups=mesh['gx_0'=8,'gx_1'=2,'gy_0'=2,'gy_1'=4,'gz'=2] {'gy_0'}, use_global_device_ids=true, to_apply=%region_27.28 | all-reduce | flops 2 | bytes 16 | tf_op jit(solution)/shard_map/psum | solution.py:51
  220.8 9.7 %all-reduce.13 = (f32[]{:T(128)}, f32[]{:T(128)}) all-reduce(f32[]{:T(128)} %get-tuple-element.42, f32[]{:T(128)} %get-tuple-element.43), channel_id=1, replica_groups=mesh['gx_0'=8,'gx_1'=2,'gy_0'=2,'gy_1'=4,'gz'=2] {'gy_1'}, use_global_device_ids=true, to_apply=%region_28.29 | all-reduce | flops 2 | bytes 16 | tf_op jit(solution)/shard_map/psum | solution.py:51
  230.5 4.4 %all-reduce.16 = (f32[]{:T(128)}, f32[]{:T(128)}) all-reduce(f32[]{:T(128)} %get-tuple-element.30, f32[]{:T(128)} %get-tuple-element.31), channel_id=1, replica_groups=mesh['gx_0'=8,'gx_1'=2,'gy_0'=2,'gy_1'=4,'gz'=2] {'gz'}, use_global_device_ids=true, to_apply=%region_29.30 | all-reduce | flops 2 | bytes 16 | tf_op jit(solution)/shard_map/psum | solution.py:51
  238.7 4.4 %multiply_subtract_fusion = (f32[2,192,512]{2,1,0:T(8,128)}, f32[2,192,512]{2,1,0:T(8,128)}) fusion(f32[2,192,512]{2,1,0:T(8,128)} %copy-done.4, f32[2,192,512]{2,1,0:T(8,128)} %get-tuple-element.54, f32[]{:T(128)S(6)} %div.60, f32[]{:T(128)S(6)} %div.62, f32[2,192,512]{2,1,0:T(8,128)} %get-tuple-element.57, f32[2,192,512]{2,1,0:T(8,128)} %get-tuple-element.60, ...), kind=kLoop, calls=%fused_computation.127 | loop fusion | flops 3538944 | bytes 7077908 | tf_op jit(solution)/shard_map/sub | solution.py:168
  (115 shorter events, 68.2 us)
Async XLA Ops:
  3.8 17.5 %collective-permute-start.2 = (f32[2,1,512]{2,1,0:T(1,128)S(1)}, f32[2,1,512]{2,1,0:T(1,128)S(1)}, u32[]{:S(2)}, u32[]{:S(2)}) collective-permute-start(f32[2,1,512]{2,1,0:T(1,128)S(1)} %get-tuple-element.75), channel_id=1, source_target_pairs={{0,2},{2,4},{4,6},{6,8},{8,10},{10,12},{12,14},{14,0},{1,3},{3,5},... | collective-permute-start | bytes 12296 | tf_op jit(solution)/shard_map/ppermute | solution.py:24
  6.8 9.7 %collective-permute-start = (f32[2,192,1]{2,1,0:T(8,128)}, f32[2,192,1]{2,1,0:T(8,128)S(1)}, u32[]{:S(2)}, u32[]{:S(2)}) collective-permute-start(f32[2,192,1]{2,1,0:T(8,128)} %get-tuple-element.77), channel_id=1, source_target_pairs={{0,16},{16,32},{32,48},{48,64},{64,80},{80,96},{96,112},{112,128},... | collective-permute-start | bytes 4616 | tf_op jit(solution)/shard_map/ppermute | solution.py:24
  9.3 11.7 %collective-permute-start.1 = (f32[2,192,1]{2,1,0:T(8,128)S(1)}, f32[2,192,1]{2,1,0:T(8,128)S(1)}, u32[]{:S(2)}, u32[]{:S(2)}) collective-permute-start(f32[2,192,1]{2,1,0:T(8,128)S(1)} %get-tuple-element.78), channel_id=1, source_target_pairs={{16,0},{32,16},{48,32},{64,48},{80,64},{96,80},{112,96},{128,112},... | collective-permute-start | bytes 4616 | tf_op jit(solution)/shard_map/ppermute | solution.py:25
  11.2 11.8 %collective-permute-start.4 = (f32[1,192,512]{2,1,0:T(8,128)}, f32[1,192,512]{2,1,0:T(8,128)}, u32[]{:S(2)}, u32[]{:S(2)}) collective-permute-start(f32[1,192,512]{2,1,0:T(8,128)} %get-tuple-element.79), channel_id=1, source_target_pairs={{0,1},{2,3},{4,5},{6,7},{8,9},{10,11},{12,13},{14,15},{16,17},{18,... | collective-permute-start | bytes 1179656 | tf_op jit(solution)/shard_map/ppermute | solution.py:41
  15.0 8.8 %collective-permute-start.5 = (f32[1,192,512]{2,1,0:T(8,128)}, f32[1,192,512]{2,1,0:T(8,128)}, u32[]{:S(2)}, u32[]{:S(2)}) collective-permute-start(f32[1,192,512]{2,1,0:T(8,128)} %get-tuple-element.80), channel_id=1, source_target_pairs={{1,0},{3,2},{5,4},{7,6},{9,8},{11,10},{13,12},{15,14},{17,16},{19,... | collective-permute-start | bytes 1179656 | tf_op jit(solution)/shard_map/ppermute | solution.py:44
  16.5 5.2 %collective-permute-start.3 = (f32[2,1,512]{2,1,0:T(1,128)S(1)}, f32[2,1,512]{2,1,0:T(1,128)S(1)}, u32[]{:S(2)}, u32[]{:S(2)}) collective-permute-start(f32[2,1,512]{2,1,0:T(1,128)S(1)} %get-tuple-element.76), channel_id=1, source_target_pairs={{2,0},{4,2},{6,4},{8,6},{10,8},{12,10},{14,12},{0,14},{3,1},{5,3},... | collective-permute-start | bytes 12296 | tf_op jit(solution)/shard_map/ppermute | solution.py:25
  27.4 26.0 %collective-permute-start.10 = (f32[1,192,512]{2,1,0:T(8,128)S(1)}, f32[1,192,512]{2,1,0:T(8,128)S(1)}, u32[]{:S(2)}, u32[]{:S(2)}) collective-permute-start(f32[1,192,512]{2,1,0:T(8,128)S(1)} %subtract_bitcast_fusion), channel_id=1, source_target_pairs={{1,0},{3,2},{5,4},{7,6},{9,8},{11,10},{13,12},{15,14},{17,16},{19,... | collective-permute-start | bytes 1179656 | tf_op jit(solution)/shard_map/ppermute | solution.py:44
  28.9 24.6 %collective-permute-start.11 = (f32[1,192,512]{2,1,0:T(8,128)S(1)}, f32[1,192,512]{2,1,0:T(8,128)S(1)}, u32[]{:S(2)}, u32[]{:S(2)}) collective-permute-start(f32[1,192,512]{2,1,0:T(8,128)S(1)} %get-tuple-element.61), channel_id=1, source_target_pairs={{0,1},{2,3},{4,5},{6,7},{8,9},{10,11},{12,13},{14,15},{16,17},{18,... | collective-permute-start | bytes 1179656 | tf_op jit(solution)/shard_map/ppermute | solution.py:41
  32.9 20.5 %collective-permute-start.8 = (f32[2,1,512]{2,1,0:T(1,128)S(1)}, f32[2,1,512]{2,1,0:T(1,128)S(1)}, u32[]{:S(2)}, u32[]{:S(2)}) collective-permute-start(f32[2,1,512]{2,1,0:T(1,128)S(1)} %get-tuple-element.71), channel_id=1, source_target_pairs={{2,0},{4,2},{6,4},{8,6},{10,8},{12,10},{14,12},{0,14},{3,1},{5,3},... | collective-permute-start | bytes 12296 | tf_op jit(solution)/shard_map/ppermute | solution.py:25
  38.2 15.3 %collective-permute-start.9 = (f32[2,1,512]{2,1,0:T(1,128)S(1)}, f32[2,1,512]{2,1,0:T(1,128)S(1)}, u32[]{:S(2)}, u32[]{:S(2)}) collective-permute-start(f32[2,1,512]{2,1,0:T(1,128)S(1)} %get-tuple-element.72), channel_id=1, source_target_pairs={{0,2},{2,4},{4,6},{6,8},{8,10},{10,12},{12,14},{14,0},{1,3},{3,5},... | collective-permute-start | bytes 12296 | tf_op jit(solution)/shard_map/ppermute | solution.py:24
  38.3 9.3 %collective-permute-start.7 = (f32[2,192,1]{2,1,0:T(8,128)S(1)}, f32[2,192,1]{2,1,0:T(8,128)S(1)}, u32[]{:S(2)}, u32[]{:S(2)}) collective-permute-start(f32[2,192,1]{2,1,0:T(8,128)S(1)} %get-tuple-element.73), channel_id=1, source_target_pairs={{0,16},{16,32},{32,48},{48,64},{64,80},{80,96},{96,112},{112,128},... | collective-permute-start | bytes 4616 | tf_op jit(solution)/shard_map/ppermute | solution.py:24
  47.6 5.8 %collective-permute-start.6 = (f32[2,192,1]{2,1,0:T(8,128)S(1)}, f32[2,192,1]{2,1,0:T(8,128)S(1)}, u32[]{:S(2)}, u32[]{:S(2)}) collective-permute-start(f32[2,192,1]{2,1,0:T(8,128)S(1)} %get-tuple-element.74), channel_id=1, source_target_pairs={{16,0},{32,16},{48,32},{64,48},{80,64},{96,80},{112,96},{128,112},... | collective-permute-start | bytes 4616 | tf_op jit(solution)/shard_map/ppermute | solution.py:25
  100.7 21.4 %collective-permute-start.16 = (f32[1,192,512]{2,1,0:T(8,128)S(1)}, f32[1,192,512]{2,1,0:T(8,128)S(1)}, u32[]{:S(2)}, u32[]{:S(2)}) collective-permute-start(f32[1,192,512]{2,1,0:T(8,128)S(1)} %get-tuple-element.58), channel_id=1, source_target_pairs={{1,0},{3,2},{5,4},{7,6},{9,8},{11,10},{13,12},{15,14},{17,16},{19,... | collective-permute-start | bytes 1179656 | tf_op jit(solution)/shard_map/ppermute | solution.py:44
  102.1 20.0 %collective-permute-start.17 = (f32[1,192,512]{2,1,0:T(8,128)S(1)}, f32[1,192,512]{2,1,0:T(8,128)S(1)}, u32[]{:S(2)}, u32[]{:S(2)}) collective-permute-start(f32[1,192,512]{2,1,0:T(8,128)S(1)} %get-tuple-element.59), channel_id=1, source_target_pairs={{0,1},{2,3},{4,5},{6,7},{8,9},{10,11},{12,13},{14,15},{16,17},{18,... | collective-permute-start | bytes 1179656 | tf_op jit(solution)/shard_map/ppermute | solution.py:41
  106.2 15.9 %collective-permute-start.14 = (f32[2,1,512]{2,1,0:T(1,128)S(1)}, f32[2,1,512]{2,1,0:T(1,128)S(1)}, u32[]{:S(2)}, u32[]{:S(2)}) collective-permute-start(f32[2,1,512]{2,1,0:T(1,128)S(1)} %get-tuple-element.67), channel_id=1, source_target_pairs={{2,0},{4,2},{6,4},{8,6},{10,8},{12,10},{14,12},{0,14},{3,1},{5,3},... | collective-permute-start | bytes 12296 | tf_op jit(solution)/shard_map/ppermute | solution.py:25
  107.5 14.6 %collective-permute-start.15 = (f32[2,1,512]{2,1,0:T(1,128)S(1)}, f32[2,1,512]{2,1,0:T(1,128)S(1)}, u32[]{:S(2)}, u32[]{:S(2)}) collective-permute-start(f32[2,1,512]{2,1,0:T(1,128)S(1)} %get-tuple-element.68), channel_id=1, source_target_pairs={{0,2},{2,4},{4,6},{6,8},{8,10},{10,12},{12,14},{14,0},{1,3},{3,5},... | collective-permute-start | bytes 12296 | tf_op jit(solution)/shard_map/ppermute | solution.py:24
  107.9 8.4 %collective-permute-start.13 = (f32[2,192,1]{2,1,0:T(8,128)S(1)}, f32[2,192,1]{2,1,0:T(8,128)S(1)}, u32[]{:S(2)}, u32[]{:S(2)}) collective-permute-start(f32[2,192,1]{2,1,0:T(8,128)S(1)} %get-tuple-element.69), channel_id=1, source_target_pairs={{0,16},{16,32},{32,48},{48,64},{64,80},{80,96},{96,112},{112,128},... | collective-permute-start | bytes 4616 | tf_op jit(solution)/shard_map/ppermute | solution.py:24
  116.3 5.8 %collective-permute-start.12 = (f32[2,192,1]{2,1,0:T(8,128)S(1)}, f32[2,192,1]{2,1,0:T(8,128)S(1)}, u32[]{:S(2)}, u32[]{:S(2)}) collective-permute-start(f32[2,192,1]{2,1,0:T(8,128)S(1)} %get-tuple-element.70), channel_id=1, source_target_pairs={{16,0},{32,16},{48,32},{64,48},{80,64},{96,80},{112,96},{128,112},... | collective-permute-start | bytes 4616 | tf_op jit(solution)/shard_map/ppermute | solution.py:25
  171.1 22.6 %collective-permute-start.22 = (f32[1,192,512]{2,1,0:T(8,128)S(1)}, f32[1,192,512]{2,1,0:T(8,128)S(1)}, u32[]{:S(2)}, u32[]{:S(2)}) collective-permute-start(f32[1,192,512]{2,1,0:T(8,128)S(1)} %get-tuple-element.55), channel_id=1, source_target_pairs={{1,0},{3,2},{5,4},{7,6},{9,8},{11,10},{13,12},{15,14},{17,16},{19,... | collective-permute-start | bytes 1179656 | tf_op jit(solution)/shard_map/ppermute | solution.py:44
  172.6 21.2 %collective-permute-start.23 = (f32[1,192,512]{2,1,0:T(8,128)S(1)}, f32[1,192,512]{2,1,0:T(8,128)S(1)}, u32[]{:S(2)}, u32[]{:S(2)}) collective-permute-start(f32[1,192,512]{2,1,0:T(8,128)S(1)} %get-tuple-element.56), channel_id=1, source_target_pairs={{0,1},{2,3},{4,5},{6,7},{8,9},{10,11},{12,13},{14,15},{16,17},{18,... | collective-permute-start | bytes 1179656 | tf_op jit(solution)/shard_map/ppermute | solution.py:41
  176.6 17.2 %collective-permute-start.20 = (f32[2,1,512]{2,1,0:T(1,128)S(1)}, f32[2,1,512]{2,1,0:T(1,128)S(1)}, u32[]{:S(2)}, u32[]{:S(2)}) collective-permute-start(f32[2,1,512]{2,1,0:T(1,128)S(1)} %get-tuple-element.63), channel_id=1, source_target_pairs={{2,0},{4,2},{6,4},{8,6},{10,8},{12,10},{14,12},{0,14},{3,1},{5,3},... | collective-permute-start | bytes 12296 | tf_op jit(solution)/shard_map/ppermute | solution.py:25
  177.9 15.9 %collective-permute-start.21 = (f32[2,1,512]{2,1,0:T(1,128)S(1)}, f32[2,1,512]{2,1,0:T(1,128)S(1)}, u32[]{:S(2)}, u32[]{:S(2)}) collective-permute-start(f32[2,1,512]{2,1,0:T(1,128)S(1)} %get-tuple-element.64), channel_id=1, source_target_pairs={{0,2},{2,4},{4,6},{6,8},{8,10},{10,12},{12,14},{14,0},{1,3},{3,5},... | collective-permute-start | bytes 12296 | tf_op jit(solution)/shard_map/ppermute | solution.py:24
  178.3 9.7 %collective-permute-start.19 = (f32[2,192,1]{2,1,0:T(8,128)S(1)}, f32[2,192,1]{2,1,0:T(8,128)S(1)}, u32[]{:S(2)}, u32[]{:S(2)}) collective-permute-start(f32[2,192,1]{2,1,0:T(8,128)S(1)} %get-tuple-element.65), channel_id=1, source_target_pairs={{0,16},{16,32},{32,48},{48,64},{64,80},{80,96},{96,112},{112,128},... | collective-permute-start | bytes 4616 | tf_op jit(solution)/shard_map/ppermute | solution.py:24
  187.9 5.8 %collective-permute-start.18 = (f32[2,192,1]{2,1,0:T(8,128)S(1)}, f32[2,192,1]{2,1,0:T(8,128)S(1)}, u32[]{:S(2)}, u32[]{:S(2)}) collective-permute-start(f32[2,192,1]{2,1,0:T(8,128)S(1)} %get-tuple-element.66), channel_id=1, source_target_pairs={{16,0},{32,16},{48,32},{64,48},{80,64},{96,80},{112,96},{128,112},... | collective-permute-start | bytes 4616 | tf_op jit(solution)/shard_map/ppermute | solution.py:25
  (24 other events, 322.0 us)
where the time goes:
time: 247 us; the launch traced here: 243 us
  blocking collectives  118 us (48%)
  starting transfers between devices  67.4 us (27%)
  other arithmetic  23.9 us (10%)
  waiting for transfers between devices  17.5 us (7%)
  between operations  10.7 us (4%)
  local copies, waits for them, and re-layouts  5.05 us (2%)
    psum x15, blocking collectives, by_axis(): array = lax.psum(array, axis)  118 us
    ppermute x8, starting transfers between devices, padded(): lax.ppermute(last, axis, up)  24.7 us
    ppermute x8, starting transfers between devices, padded(): lax.ppermute(leading, axis, [(b, a) for a, b in up])  21.2 us
    ppermute x4, starting transfers between devices, padded_2(): lax.ppermute(lax.slice_in_dim(block, block.shape[dim] - width, None, axis...  16 us
    reduce_sum x3, other arithmetic, merged_sums(): jnp.sum(image_field * precond)  9.43 us
    ppermute x8, waiting for transfers between devices, padded(): lax.ppermute(leading, axis, [(b, a) for a, b in up])  8.73 us
    ppermute x8, waiting for transfers between devices, padded(): lax.ppermute(last, axis, up)  7.86 us
    sub x3, other arithmetic, shards(): residual = residual - step_size * image_dir  7.35 us
  transfers between devices with their start and end apart: 24, of which 8 were waited for; matrix products, arithmetic and copies ran while one was open for 2% of the time, Pallas kernels for 0%

commit v1 on v0

--- a/solution.py
+++ b/solution.py
@@ -1,6 +1,8 @@
 import jax
 import jax.numpy as jnp
 from jax import lax
+from jax.experimental import pallas as pl
+from jax.experimental.pallas import tpu as pltpu
 from jax.sharding import Mesh
 from jax.sharding import PartitionSpec as P
 
@@ -106,7 +108,7 @@
     )
 
 
-def shards(load_current, sink_mask, pad_mask, plane_class, via_class, plane_table, via_table):
+def recurrence(load_current, sink_mask, pad_mask, plane_class, via_class, plane_table, via_table):
     n_layers, n_rows, n_cols = plane_class.shape
     g_plane = lookup(plane_class, plane_table)
     g_via = lookup(via_class, via_table)
@@ -178,6 +180,389 @@
     return (voltage, residual)
 
 
+STEP = 8
+LANES = 128
+GUARD = 0.02
+VMEM = pl.BlockSpec(memory_space=pltpu.VMEM)
+SMEM = pl.BlockSpec(memory_space=pltpu.SMEM)
+
+
+def select_class(classes, entry):
+    low = (classes & 1) != 0
+    mid = (classes & 2) != 0
+    high = (classes & 4) != 0
+    pairs = [jnp.where(low, entry(2 * k + 1), entry(2 * k)) for k in range(4)]
+    return jnp.where(high, jnp.where(mid, pairs[3], pairs[2]), jnp.where(mid, pairs[1], pairs[0]))
+
+
+def via_kernel(gz, table, classes, via_i, inner):
+    group = gz[0]
+    for r in range(0, via_i.shape[0], STEP):
+        rows = pl.ds(r, STEP)
+        one = select_class(classes[1 - group, rows, :], lambda k: table[1 - group, k])
+        two = select_class(classes[group, rows, :], lambda k: table[group, k])
+        via_i[rows, :] = one
+        inner[rows, :] = harmonic(one, two)
+
+
+def stage_columns(stage, r, field_i, field_o):
+    lane = lax.broadcasted_iota(jnp.int32, (STEP, LANES), 1)
+    last = field_i.shape[1] - LANES
+    first_o = pltpu.roll(field_o[:, :LANES], 1, 1)
+    last_i = pltpu.roll(field_i[:, last:], 3, 1)
+    last_o = pltpu.roll(field_o[:, last:], 4, 1)
+    picked = jnp.where(lane == 2, last_i, last_o)
+    picked = jnp.where(lane == 1, first_o, picked)
+    stage[pl.ds(r, STEP), :] = jnp.where(lane == 0, field_i[:, :LANES], picked)
+
+
+def send_edges(stage, field_i, field_o, edges):
+    first_row, last_row, first_col, last_col = edges
+    n_rows = field_i.shape[0]
+    first_row[0:1, :] = field_i[0:1, :]
+    first_row[1:2, :] = field_o[0:1, :]
+    last_row[0:1, :] = field_i[n_rows - 1 : n_rows, :]
+    last_row[1:2, :] = field_o[n_rows - 1 : n_rows, :]
+    turned = stage[...].T
+    first_col[...] = turned[0:2, :]
+    last_col[...] = turned[2:4, :]
+
+
+def take_columns(flat, west, east, columns):
+    flat[...] = jnp.zeros(flat.shape, jnp.float32)
+    flat[0:2, :] = west[...]
+    flat[2:4, :] = east[...]
+    columns[...] = flat[...].T
+
+
+def plane_kernel(gz, table, classes, plane_i, plane_o, *rest):
+    edges, stage = rest[:4], rest[4]
+    group = gz[0]
+    stage[...] = jnp.zeros(stage.shape, jnp.float32)
+    for r in range(0, plane_i.shape[0], STEP):
+        rows = pl.ds(r, STEP)
+        one = select_class(classes[1 - group, rows, :], lambda k: table[1 - group, k])
+        two = select_class(classes[group, rows, :], lambda k: table[group, k])
+        plane_i[rows, :] = one
+        plane_o[rows, :] = two
+        stage_columns(stage, r, one, two)
+    send_edges(stage, plane_i, plane_o, edges)
+
+
+def around(field, layer, r, south, north, columns):
+    n_rows, n_cols = field.shape
+    own = field[pl.ds(r, STEP), :]
+    sub = lax.broadcasted_iota(jnp.int32, own.shape, 0)
+    lane = lax.broadcasted_iota(jnp.int32, own.shape, 1)
+    if r:
+        below = field[r - 1 : r - 1 + STEP, :]
+    else:
+        below = jnp.where(sub == 0, south[layer : layer + 1, :], pltpu.roll(own, 1, 0))
+    if r + STEP < n_rows:
+        above = field[r + 1 : r + 1 + STEP, :]
+    else:
+        above = jnp.where(
+            sub == STEP - 1, north[layer : layer + 1, :], pltpu.roll(own, STEP - 1, 0)
+        )
+    west_col = columns[pl.ds(r, STEP), layer : layer + 1]
+    east_col = columns[pl.ds(r, STEP), layer + 2 : layer + 3]
+    west = jnp.where(lane == 0, west_col, pltpu.roll(own, 1, 1))
+    east = jnp.where(lane == n_cols - 1, east_col, pltpu.roll(own, n_cols - 1, 1))
+    return own, east, west, above, below
+
+
+def fold(total):
+    width = total.shape[1]
+    while width > LANES:
+        width //= 2
+        total = total[:, :width] + total[:, width:]
+    return jnp.sum(total, axis=0, keepdims=True)
+
+
+def edge_kernel(
+    gz, plane_i, plane_o, south, north, west, east, via_i, via_far, inner, load, sink, pad, *rest
+):
+    edges_i, edges_o = rest[0:4], rest[4:8]
+    cross, inv_ii, inv_oo, inv_io, v_i, v_o, source, payload = rest[8:16]
+    sends, part = rest[16:20], rest[20]
+    stage, flat, columns = rest[21:]
+    group = gz[0]
+    take_columns(flat, west, east, columns)
+    stage[...] = jnp.zeros(stage.shape, jnp.float32)
+    total = jnp.zeros((STEP, plane_i.shape[1]), jnp.float32)
+    for r in range(0, plane_i.shape[0], STEP):
+        rows = pl.ds(r, STEP)
+        sums = []
+        for layer, field, edges in ((0, plane_i, edges_i), (1, plane_o, edges_o)):
+            own, *others = around(field, layer, r, south, north, columns)
+            values = [harmonic(own, other) for other in others]
+            for edge, value in zip(edges, values):
+                edge[rows, :] = value
+            sums.append(values[0] + values[1] + values[2] + values[3])
+        up = inner[rows, :]
+        far = harmonic(via_i[rows, :], via_far[rows, :])
+        cross[rows, :] = far
+        pads = PAD_CONDUCTANCE * pad[rows, :].astype(jnp.float32)
+        diag_i = sums[0] + up + far
+        diag_o = sums[1] + up + jnp.where(group == 1, pads, 0.0)
+        inverse = 1.0 / (diag_i * diag_o - up * up)
+        ii, oo, io = diag_o * inverse, diag_i * inverse, up * inverse
+        drawn = sink[rows, :].astype(jnp.float32) * load[rows, :]
+        drawn = jnp.where(group == 0, drawn, 0.0)
+        one, two = io * drawn, oo * drawn
+        inv_ii[rows, :], inv_oo[rows, :], inv_io[rows, :] = ii, oo, io
+        source[rows, :] = drawn
+        v_i[rows, :], v_o[rows, :] = one, two
+        payload[rows, :] = jnp.where(group == 0, one, ii)
+        stage_columns(stage, r, one, two)
+        total = total + two * drawn
+    send_edges(stage, v_i, v_o, sends)
+    part[...] = jnp.zeros(part.shape, jnp.float32)
+    part[0:1, :] = fold(total)
+
+
+def stencil(field, layer, r, halos, columns, edges):
+    own, *others = around(field, layer, r, halos[0], halos[1], columns)
+    rows = pl.ds(r, STEP)
+    east, west, above, below = [edge[rows, :] * value for edge, value in zip(edges, others)]
+    return own, (east + west) + (above + below)
+
+
+def first_kernel(gz, v_i, v_o, south, north, west, east, *rest):
+    edges_i, edges_o = rest[0:4], rest[4:8]
+    cross, inv_ii, inv_oo, inv_io, given, before = rest[8:14]
+    n_i, n_o, w_i, w_o, far = rest[14:19]
+    sends, part = rest[19:23], rest[23]
+    stage, flat, columns = rest[24:]
+    group = gz[0]
+    take_columns(flat, west, east, columns)
+    stage[...] = jnp.zeros(stage.shape, jnp.float32)
+    sums = [jnp.zeros((STEP, v_i.shape[1]), jnp.float32)] * 2
+    for r in range(0, v_i.shape[0], STEP):
+        rows = pl.ds(r, STEP)
+        own_i, out_i = stencil(v_i, 0, r, (south, north), columns, edges_i)
+        own_o, out_o = stencil(v_o, 1, r, (south, north), columns, edges_o)
+        link, got = cross[rows, :], given[rows, :]
+        out_i = out_i + jnp.where(group == 1, link * got, 0.0)
+        far[rows, :] = link * own_i * got
+        ii, oo, io = inv_ii[rows, :], inv_oo[rows, :], inv_io[rows, :]
+        one, two = ii * out_i + io * out_o, io * out_i + oo * out_o
+        n_i[rows, :], n_o[rows, :] = out_i, out_o
+        w_i[rows, :], w_o[rows, :] = one, two
+        stage_columns(stage, r, one, two)
+        sums[0] = sums[0] + (own_i * out_i + own_o * out_o)
+        sums[1] = sums[1] + (one * out_i + two * out_o)
+    send_edges(stage, w_i, w_o, sends)
+    part[...] = before[...]
+    part[1:2, :] = fold(sums[0])
+    part[2:3, :] = fold(sums[1])
+
+
+def second_kernel(gz, v_i, v_o, south, north, west, east, *rest):
+    edges_i, edges_o = rest[0:4], rest[4:8]
+    cross, inv_ii, inv_oo, inv_io, made, given, before = rest[8:15]
+    n_i, n_o, w_i, w_o = rest[15:19]
+    sends, part = rest[19:23], rest[23]
+    stage, flat, columns = rest[24:]
+    group = gz[0]
+    take_columns(flat, west, east, columns)
+    stage[...] = jnp.zeros(stage.shape, jnp.float32)
+    sums = [jnp.zeros((STEP, v_i.shape[1]), jnp.float32)] * 2
+    for r in range(0, v_i.shape[0], STEP):
+        rows = pl.ds(r, STEP)
+        own_i, out_i = stencil(v_i, 0, r, (south, north), columns, edges_i)
+        own_o, out_o = stencil(v_o, 1, r, (south, north), columns, edges_o)
+        out_i = out_i + cross[rows, :] * jnp.where(group == 0, made[rows, :], given[rows, :])
+        ii, oo, io = inv_ii[rows, :], inv_oo[rows, :], inv_io[rows, :]
+        one, two = ii * out_i + io * out_o, io * out_i + oo * out_o
+        n_i[rows, :], n_o[rows, :] = out_i, out_o
+        w_i[rows, :], w_o[rows, :] = one, two
+        stage_columns(stage, r, one, two)
+        sums[0] = sums[0] + (own_i * out_i + own_o * out_o)
+        sums[1] = sums[1] + (one * out_i + two * out_o)
+    send_edges(stage, w_i, w_o, sends)
+    part[...] = before[...]
+    part[3:4, :] = fold(sums[0])
+    part[4:5, :] = fold(sums[1])
+
+
+def third_kernel(v_i, v_o, south, north, west, east, *rest):
+    edges_i, edges_o = rest[0:4], rest[4:8]
+    cross, given, before = rest[8:11]
+    n_i, n_o, spread = rest[11:14]
+    flat, columns = rest[14:]
+    take_columns(flat, west, east, columns)
+    total = jnp.zeros((STEP, v_i.shape[1]), jnp.float32)
+    for r in range(0, v_i.shape[0], STEP):
+        rows = pl.ds(r, STEP)
+        own_i, out_i = stencil(v_i, 0, r, (south, north), columns, edges_i)
+        own_o, out_o = stencil(v_o, 1, r, (south, north), columns, edges_o)
+        out_i = out_i + cross[rows, :] * given[rows, :]
+        n_i[rows, :], n_o[rows, :] = out_i, out_o
+        total = total + (own_i * out_i + own_o * out_o)
+    row = lax.broadcasted_iota(jnp.int32, before.shape, 0)
+    part = jnp.where(row == 5, fold(total), before[...])
+    for k in range(spread.shape[0]):
+        spread[k] = part
+
+
+def tree(parts):
+    values = [parts[k] for k in range(parts.shape[0])]
+    while len(values) > 1:
+        values = [a + b for a, b in zip(values[::2], values[1::2])]
+    return values[0]
+
+
+def relay_kernel(parts, spread):
+    total = tree(parts)
+    for k in range(spread.shape[0]):
+        spread[k] = total
+
+
+def solve_kernel(parts, coefs, flag):
+    sums = jnp.sum(tree(parts), axis=1, keepdims=True)
+    g = [jnp.broadcast_to(sums[k : k + 1, :], (1, LANES)) for k in range(6)]
+    step = [g[k] - g[k + 1] for k in range(5)]
+    scale = [lax.rsqrt(g[0]), lax.rsqrt(g[2]), lax.rsqrt(g[4])]
+
+    def entry(i, j):
+        return step[i + j] * scale[i] * scale[j]
+
+    d0 = entry(0, 0)
+    l10, l20 = entry(1, 0) / d0, entry(2, 0) / d0
+    d1 = entry(1, 1) - l10 * entry(1, 0)
+    e21 = entry(2, 1) - l20 * entry(1, 0)
+    l21 = e21 / d1
+    d2 = entry(2, 2) - l20 * entry(2, 0) - l21 * e21
+    y0 = g[0] * scale[0]
+    y1 = g[1] * scale[1] - l10 * y0
+    y2 = g[2] * scale[2] - l20 * y0 - l21 * y1
+    x2 = y2 / d2
+    x1 = y1 / d1 - l21 * x2
+    x0 = y0 / d0 - l10 * x1 - l20 * x2
+    c0, c1, c2 = x0 * scale[0], x1 * scale[1], x2 * scale[2]
+    for k, value in enumerate((c0, c1, c2, 1.0 - c0, c0 - c1, c1 - c2)):
+        coefs[k : k + 1, :] = value
+    coefs[6:8, :] = jnp.zeros((2, LANES), jnp.float32)
+    good = (d0 > GUARD) & (d1 > GUARD) & (d2 > GUARD)
+    flag[...] = jnp.where(good, 1, 0)
+
+
+def combine_kernel(gz, coefs, source, *rest):
+    fields, volts, left = rest[:12], rest[12], rest[13]
+    group = gz[0]
+    width = source.shape[1]
+    c = [jnp.broadcast_to(coefs[k : k + 1, 0:1], (STEP, width)) for k in range(6)]
+    for r in range(0, source.shape[0], STEP):
+        rows = pl.ds(r, STEP)
+        v0i, v0o, v1i, v1o, v2i, v2o, n0i, n0o, n1i, n1o, n2i, n2o = [f[rows, :] for f in fields]
+        volts[1 - group, rows, :] = c[0] * v0i + c[1] * v1i + c[2] * v2i
+        volts[group, rows, :] = c[0] * v0o + c[1] * v1o + c[2] * v2o
+        left[1 - group, rows, :] = c[4] * n0i + c[5] * n1i + c[2] * n2i
+        left[group, rows, :] = (
+            c[3] * source[rows, :] + c[4] * n0o + c[5] * n1o + c[2] * n2o
+        )
+
+
+def call(kernel, name, outs, scratch, n_smem, *args):
+    return pl.pallas_call(
+        kernel,
+        name=name,
+        in_specs=[SMEM] * n_smem + [VMEM] * (len(args) - n_smem),
+        out_specs=[VMEM] * len(outs),
+        out_shape=outs,
+        scratch_shapes=scratch,
+    )(*args)
+
+
+def halos(first_row, last_row, first_col, last_col):
+    def ring(axis):
+        size = lax.axis_size(axis)
+        return [(i, (i + 1) % size) for i in range(size)]
+
+    up_y, up_x = ring(GY), ring(GX)
+    back_y, back_x = [(b, a) for a, b in up_y], [(b, a) for a, b in up_x]
+    return (
+        lax.ppermute(last_row, GY, up_y),
+        lax.ppermute(first_row, GY, back_y),
+        lax.ppermute(last_col, GX, up_x),
+        lax.ppermute(first_col, GX, back_x),
+    )
+
+
+def shards(load_current, sink_mask, pad_mask, plane_class, via_class, plane_table, via_table):
+    _, n_rows, n_cols = plane_class.shape
+    tall = -(-n_rows // LANES) * LANES
+    f32 = jnp.float32
+    plane = jax.ShapeDtypeStruct((n_rows, n_cols), f32)
+    both = jax.ShapeDtypeStruct((2, n_rows, n_cols), f32)
+    row = jax.ShapeDtypeStruct((2, n_cols), f32)
+    col = jax.ShapeDtypeStruct((2, tall), f32)
+    sheet = jax.ShapeDtypeStruct((STEP, LANES), f32)
+    edge_outs = [row, row, col, col]
+    stage = pltpu.VMEM((tall, LANES), f32)
+    turn = [pltpu.VMEM((LANES, tall), f32), pltpu.VMEM((tall, LANES), f32)]
+    gz = lax.axis_index("gz").reshape(1).astype(jnp.int32)
+    swap = [(0, 1), (1, 0)]
+    n_gx, n_rest = lax.axis_size(GX), lax.axis_size(("gy_0", "gy_1", "gz"))
+
+    via_i, inner = call(via_kernel, "via", [plane] * 2, [], 2, gz, via_table, via_class)
+    via_far = lax.ppermute(via_i, "gz", swap)
+    plane_i, plane_o, *sends = call(
+        plane_kernel, "plane", [plane] * 2 + edge_outs, [stage], 2, gz, plane_table, plane_class
+    )
+    near = halos(*sends)
+    outs = call(
+        edge_kernel, "edge", [plane] * 16 + edge_outs + [sheet], [stage] + turn, 1,
+        gz, plane_i, plane_o, *near, via_i, via_far, inner, load_current, sink_mask, pad_mask,
+    )
+    edges, (cross, inv_ii, inv_oo, inv_io) = outs[0:8], outs[8:12]
+    v0i, v0o, source, payload = outs[12:16]
+    sends, part = outs[16:20], outs[20]
+    given = lax.ppermute(payload, "gz", swap)
+    near = halos(*sends)
+    n0i, n0o, v1i, v1o, made, *sends, part = call(
+        first_kernel, "first", [plane] * 5 + edge_outs + [sheet], [stage] + turn, 1,
+        gz, v0i, v0o, *near, *edges, cross, inv_ii, inv_oo, inv_io, given, part,
+    )
+    given = lax.ppermute(v1i, "gz", [(0, 1)])
+    near = halos(*sends)
+    n1i, n1o, v2i, v2o, *sends, part = call(
+        second_kernel, "second", [plane] * 4 + edge_outs + [sheet], [stage] + turn, 1,
+        gz, v1i, v1o, *near, *edges, cross, inv_ii, inv_oo, inv_io, made, given, part,
+    )
+    given = lax.ppermute(v2i, "gz", swap)
+    near = halos(*sends)
+    n2i, n2o, spread = call(
+        third_kernel, "third",
+        [plane] * 2 + [jax.ShapeDtypeStruct((n_gx, STEP, LANES), f32)], turn, 0,
+        v2i, v2o, *near, *edges, cross, given, part,
+    )
+    parts = lax.all_to_all(spread, GX, 0, 0, tiled=True)
+    (spread,) = call(
+        relay_kernel, "relay", [jax.ShapeDtypeStruct((n_rest, STEP, LANES), f32)], [], 0, parts
+    )
+    parts = lax.all_to_all(spread, ("gy_0", "gy_1", "gz"), 0, 0, tiled=True)
+    coefs, flag = call(
+        solve_kernel, "solve", [sheet, jax.ShapeDtypeStruct((1, LANES), jnp.int32)], [], 0, parts
+    )
+
+    def fast():
+        return tuple(
+            call(
+                combine_kernel, "combine", [both] * 2, [], 1, gz, coefs, source,
+                v0i, v0o, v1i, v1o, v2i, v2o, n0i, n0o, n1i, n1o, n2i, n2o,
+            )
+        )
+
+    def careful():
+        return recurrence(
+            load_current, sink_mask, pad_mask, plane_class, via_class, plane_table, via_table
+        )
+
+    return lax.cond(flag[0, 0] == 1, fast, careful)
+
+
 def solution(mesh):
     split = Mesh(
         mesh.devices.reshape(8, 2, 2, 4, mesh.shape["gz"]), ("gx_0", "gx_1", "gy_0", "gy_1", "gz")

time: 247 us -> 119 us (0.48); the launches traced: 243 us -> 119 us
  blocking collectives: 118 us -> 17.7 us
  Pallas kernels: 0 us -> 32.4 us
  starting transfers between devices: 67.4 us -> 43.1 us
  other arithmetic: 23.9 us -> 0 us
  between operations: 10.7 us -> 1.57 us
  waiting for transfers between devices: 17.5 us -> 20.6 us
    psum x15 -> x0, blocking collectives: 118 us -> none  [by_axis(): array = lax.psum(array, axis)]
    pallas_call x0 -> x9, Pallas kernels: none -> 32.4 us  [call(): pl.pallas_call(kernel, name=name, in_specs=[SMEM] * n_smem + [VMEM] * (le...]
    ppermute x24 -> x20, starting transfers between devices: 67.4 us -> 37.7 us  [the longest x4 19 us: halos(): lax.ppermute(first_row, GY, back_y)]
    all_to_all x0 -> x1, blocking collectives: none -> 17.7 us  [shards(): parts = lax.all_to_all(spread, GX, 0, 0, tiled=True)]
    reduce_sum x3 -> x0, other arithmetic: 9.43 us -> none  [merged_sums(): jnp.sum(image_field * precond)]
    sub x5 -> x0, other arithmetic: 7.83 us -> none  [the longest x3 7.35 us: shards(): residual = residual - step_size * image_dir]
    all_to_all x0 -> x1, waiting for transfers between devices: none -> 6.52 us  [shards(): parts = lax.all_to_all(spread, ('gy_0', 'gy_1', 'gz'), 0, 0, tiled=True)]
    all_to_all x0 -> x1, starting transfers between devices: none -> 5.45 us  [shards(): parts = lax.all_to_all(spread, ('gy_0', 'gy_1', 'gz'), 0, 0, tiled=True)]
  transfers between devices with their start and end apart: 24 -> 21, of which waited for: 8 -> 10; matrix products, arithmetic and copies ran while one was open for 2% -> 0% of each run, Pallas kernels for 0% -> 2%
where the time goes in v1:
time: 119 us
  starting transfers between devices  43.1 us (36%)
  Pallas kernels  32.4 us (27%)
  waiting for transfers between devices  20.6 us (17%)
  blocking collectives  17.7 us (15%)
  local copies, waits for them, and re-layouts  3.64 us (3%)
  between operations  1.57 us (1%)
    pallas_call x9, Pallas kernels, call(): pl.pallas_call(kernel, name=name, in_specs=[SMEM] * n_smem + [VMEM] * (le...  32.4 us
    ppermute x4, starting transfers between devices, halos(): lax.ppermute(first_row, GY, back_y)  19 us
    all_to_all x1, blocking collectives, shards(): parts = lax.all_to_all(spread, GX, 0, 0, tiled=True)  17.7 us
    ppermute x4, starting transfers between devices, halos(): lax.ppermute(last_col, GX, up_x)  10.4 us
    ppermute x4, waiting for transfers between devices, halos(): lax.ppermute(first_col, GX, back_x)  9.97 us
    all_to_all x1, waiting for transfers between devices, shards(): parts = lax.all_to_all(spread, ('gy_0', 'gy_1', 'gz'), 0, 0, tiled=True)  6.52 us
    all_to_all x1, starting transfers between devices, shards(): parts = lax.all_to_all(spread, ('gy_0', 'gy_1', 'gz'), 0, 0, tiled=True)  5.45 us
    ppermute x4, waiting for transfers between devices, halos(): lax.ppermute(last_col, GX, up_x)  3.77 us
  transfers between devices with their start and end apart: 21, of which 10 were waited for; matrix products, arithmetic and copies ran while one was open for 0% of the time, Pallas kernels for 2%

profile of v1, /device:TPU:1, one launch (start us, length us, event | category | flops | bytes accessed | tf_op | source)
XLA Modules:
  0.0 119.0 jit_solution(4257993019336061863)
XLA Ops:
  0.7 2.6 %via.1 = (f32[192,512]{1,0:T(8,128)}, f32[192,512]{1,0:T(8,128)}) custom-call(s32[1]{0:T(128)} %bitcast.23.gz, f32[2,8]{1,0:T(2,128)} %table.3, s32[2,192,512]{2,1,0:T(8,128)} %classes.3), custom_call_target="tpu_custom_call" | custom-call | tf_op jit(solution)/shard_map/via/pallas_call | solution.py:468
  3.2 2.0 %collective-permute-start.28 = (f32[192,512]{1,0:T(8,128)}, f32[192,512]{1,0:T(8,128)S(1)}, u32[]{:S(2)}, u32[]{:S(2)}) collective-permute-start(f32[192,512]{1,0:T(8,128)} %get-tuple-element.127.via_i), channel_id=1, source_target_pairs={{0,1},{1,0},{2,3},{3,2},{4,5},{5,4},{6,7},{7,6},{8,9},{9,8},{10,11... | collective-permute-start | bytes 1179656 | tf_op jit(solution)/shard_map/ppermute | solution.py:510
  5.3 1.9 %plane.1 = (f32[192,512]{1,0:T(8,128)}, f32[192,512]{1,0:T(8,128)}, f32[2,512]{1,0:T(2,128)}, f32[2,512]{1,0:T(2,128)}, f32[2,256]{1,0:T(2,128)}, /*index=5*/f32[2,256]{1,0:T(2,128)}) custom-call(s32[1]{0:T(128)} %bitcast.23.gz, f32[2,8]{1,0:T(2,128)} %table.2, s32[2,192,512]{2,1,0:T(8,128)S(1)} %copy-done.18), custom_call_target="tpu_custom_call" | custom-call | tf_op jit(solution)/shard_map/plane/pallas_call | solution.py:468
  8.5 3.8 %collective-permute-start.25 = (f32[2,512]{1,0:T(2,128)}, f32[2,512]{1,0:T(2,128)S(1)}, u32[]{:S(2)}, u32[]{:S(2)}) collective-permute-start(f32[2,512]{1,0:T(2,128)} %get-tuple-element.124), channel_id=1, source_target_pairs={{2,0},{4,2},{6,4},{8,6},{10,8},{12,10},{14,12},{0,14},{3,1},{5,3},... | collective-permute-start | bytes 12296 | tf_op jit(solution)/shard_map/ppermute | solution.py:487
  12.3 3.0 %collective-permute-start.26 = (f32[2,256]{1,0:T(2,128)}, f32[2,256]{1,0:T(2,128)S(1)}, u32[]{:S(2)}, u32[]{:S(2)}) collective-permute-start(f32[2,256]{1,0:T(2,128)} %get-tuple-element.125), channel_id=1, source_target_pairs={{0,16},{16,32},{32,48},{48,64},{64,80},{80,96},{96,112},{112,128},... | collective-permute-start | bytes 6152 | tf_op jit(solution)/shard_map/ppermute | solution.py:488
  16.2 2.6 %collective-permute-done.27.east = f32[2,256]{1,0:T(2,128)S(1)} collective-permute-done((f32[2,256]{1,0:T(2,128)}, f32[2,256]{1,0:T(2,128)S(1)}, u32[]{:S(2)}, u32[]{:S(2)}) %collective-permute-start.27) | collective-permute-done | bytes 2080 | tf_op jit(solution)/shard_map/ppermute | solution.py:489
  19.6 6.5 %edge.1 = (f32[192,512]{1,0:T(8,128)}, f32[192,512]{1,0:T(8,128)}, f32[192,512]{1,0:T(8,128)}, f32[192,512]{1,0:T(8,128)}, f32[192,512]{1,0:T(8,128)}, /*index=5...) custom-call(s32[1]{0:T(128)} %bitcast.23.gz, ...), custom_call_target="tpu_custom_call" | custom-call | tf_op jit(solution)/shard_map/edge/pallas_call | solution.py:468
  26.5 5.1 %collective-permute-start.30 = (f32[2,512]{1,0:T(2,128)}, f32[2,512]{1,0:T(2,128)S(1)}, u32[]{:S(2)}, u32[]{:S(2)}) collective-permute-start(f32[2,512]{1,0:T(2,128)} %get-tuple-element.132), channel_id=1, source_target_pairs={{2,0},{4,2},{6,4},{8,6},{10,8},{12,10},{14,12},{0,14},{3,1},{5,3},... | collective-permute-start | bytes 12296 | tf_op jit(solution)/shard_map/ppermute | solution.py:487
  31.5 3.7 %collective-permute-start.31 = (f32[2,256]{1,0:T(2,128)}, f32[2,256]{1,0:T(2,128)S(1)}, u32[]{:S(2)}, u32[]{:S(2)}) collective-permute-start(f32[2,256]{1,0:T(2,128)} %get-tuple-element.133), channel_id=1, source_target_pairs={{0,16},{16,32},{32,48},{48,64},{64,80},{80,96},{96,112},{112,128},... | collective-permute-start | bytes 6152 | tf_op jit(solution)/shard_map/ppermute | solution.py:488
  36.2 2.3 %collective-permute-done.32.east = f32[2,256]{1,0:T(2,128)S(1)} collective-permute-done((f32[2,256]{1,0:T(2,128)}, f32[2,256]{1,0:T(2,128)S(1)}, u32[]{:S(2)}, u32[]{:S(2)}) %collective-permute-start.32) | collective-permute-done | bytes 2080 | tf_op jit(solution)/shard_map/ppermute | solution.py:489
  39.3 5.6 %first.1 = (f32[192,512]{1,0:T(8,128)}, f32[192,512]{1,0:T(8,128)}, f32[192,512]{1,0:T(8,128)S(1)}, f32[192,512]{1,0:T(8,128)S(1)}, f32[192,512]{1,0:T(8,128)}, ...) custom-call(s32[1]{0:T(128)} %bitcast.23.gz, ...), custom_call_target="tpu_custom_call" | custom-call | tf_op jit(solution)/shard_map/first/pallas_call | solution.py:468
  45.0 3.5 %collective-permute-start.38 = (f32[192,512]{1,0:T(8,128)S(1)}, f32[192,512]{1,0:T(8,128)S(1)}, u32[]{:S(2)}, u32[]{:S(2)}) collective-permute-start(f32[192,512]{1,0:T(8,128)S(1)} %get-tuple-element.149.v_i), channel_id=1, source_target_pairs={{0,1},{2,3},{4,5},{6,7},{8,9},{10,11},{12,13},{14,15},{16,17},{18,... | collective-permute-start | bytes 1179656 | tf_op jit(solution)/shard_map/ppermute | solution.py:528
  48.5 5.1 %collective-permute-start.35 = (f32[2,512]{1,0:T(2,128)}, f32[2,512]{1,0:T(2,128)S(1)}, u32[]{:S(2)}, u32[]{:S(2)}) collective-permute-start(f32[2,512]{1,0:T(2,128)} %get-tuple-element.152), channel_id=1, source_target_pairs={{2,0},{4,2},{6,4},{8,6},{10,8},{12,10},{14,12},{0,14},{3,1},{5,3},... | collective-permute-start | bytes 12296 | tf_op jit(solution)/shard_map/ppermute | solution.py:487
  55.5 2.6 %collective-permute-done.37.east = f32[2,256]{1,0:T(2,128)S(1)} collective-permute-done((f32[2,256]{1,0:T(2,128)}, f32[2,256]{1,0:T(2,128)S(1)}, u32[]{:S(2)}, u32[]{:S(2)}) %collective-permute-start.37) | collective-permute-done | bytes 2080 | tf_op jit(solution)/shard_map/ppermute | solution.py:489
  58.9 5.6 %second.1 = (f32[192,512]{1,0:T(8,128)}, f32[192,512]{1,0:T(8,128)}, f32[192,512]{1,0:T(8,128)S(1)}, f32[192,512]{1,0:T(8,128)S(1)}, f32[2,512]{1,0:T(2,128)}, /...) custom-call(s32[1]{0:T(128)} %bitcast.23.gz, ...), custom_call_target="tpu_custom_call" | custom-call | tf_op jit(solution)/shard_map/second/pallas_call | solution.py:468
  65.6 5.1 %collective-permute-start.40 = (f32[2,512]{1,0:T(2,128)}, f32[2,512]{1,0:T(2,128)S(1)}, u32[]{:S(2)}, u32[]{:S(2)}) collective-permute-start(f32[2,512]{1,0:T(2,128)} %get-tuple-element.160), channel_id=1, source_target_pairs={{2,0},{4,2},{6,4},{8,6},{10,8},{12,10},{14,12},{0,14},{3,1},{5,3},... | collective-permute-start | bytes 12296 | tf_op jit(solution)/shard_map/ppermute | solution.py:487
  70.7 2.6 %collective-permute-start.41 = (f32[2,256]{1,0:T(2,128)}, f32[2,256]{1,0:T(2,128)S(1)}, u32[]{:S(2)}, u32[]{:S(2)}) collective-permute-start(f32[2,256]{1,0:T(2,128)} %get-tuple-element.161), channel_id=1, source_target_pairs={{0,16},{16,32},{32,48},{48,64},{64,80},{80,96},{96,112},{112,128},... | collective-permute-start | bytes 6152 | tf_op jit(solution)/shard_map/ppermute | solution.py:488
  74.2 2.6 %collective-permute-done.42.east = f32[2,256]{1,0:T(2,128)S(1)} collective-permute-done((f32[2,256]{1,0:T(2,128)}, f32[2,256]{1,0:T(2,128)S(1)}, u32[]{:S(2)}, u32[]{:S(2)}) %collective-permute-start.42) | collective-permute-done | bytes 2080 | tf_op jit(solution)/shard_map/ppermute | solution.py:489
  77.8 3.8 %third.1 = (f32[192,512]{1,0:T(8,128)}, f32[192,512]{1,0:T(8,128)}, f32[16,8,128]{2,1,0:T(8,128)}) custom-call(f32[192,512]{1,0:T(8,128)S(1)} %get-tuple-element.157.v_i, f32[192,512]{1,0:T(8,128)S(1)} %get-tuple-element.158.v_o, f32[2,512]{1,0:T(2,128)} %copy-done.36, f32[2,512]{1,0:T(2,128)} %copy-done.39, f32[2,256]{1,0:T(2,128)} %copy-done.45, ...), custom_call_target="tpu_custom_call" | custom-call | tf_op jit(solution)/shard_map/third/pallas_call | solution.py:468
  81.6 17.7 %all_to_all.10.parts = f32[16,8,128]{2,1,0:T(8,128)} all-to-all(f32[16,8,128]{2,1,0:T(8,128)} %get-tuple-element.164), channel_id=1, replica_groups=mesh['gx_0'=8,'gx_1'=2,'gy_0'=2,'gy_1'=4,'gz'=2] {'gx_0','gx_1'}, dimensions={0} | all-to-all | bytes 131072 | tf_op jit(solution)/shard_map/all_to_all | solution.py:541
  100.8 5.5 %all-to-all-start.1 = ((f32[16,8,128]{2,1,0:T(8,128)}), f32[16,8,128]{2,1,0:T(8,128)S(1)}, u32[]{:S(2)}, u32[]{:S(2)}) async-start(f32[16,8,128]{2,1,0:T(8,128)} %relay.1), calls=%async_computation.1 | async-start | bytes 131072 | tf_op jit(solution)/shard_map/all_to_all | solution.py:545
  106.3 6.5 %all-to-all-done.1.parts = f32[16,8,128]{2,1,0:T(8,128)S(1)} async-done(((f32[16,8,128]{2,1,0:T(8,128)}), f32[16,8,128]{2,1,0:T(8,128)S(1)}, u32[]{:S(2)}, u32[]{:S(2)}) %all-to-all-start.1) | async-done | bytes 65568 | tf_op jit(solution)/shard_map/all_to_all | solution.py:545
  115.6 3.4 %conditional.1 = ((f32[2,192,512]{2,1,0:T(8,128)}, f32[2,192,512]{2,1,0:T(8,128)})) conditional(s32[]{:T(128)} %bitcast.24, (s32[192,512]{1,0:T(8,128)}, f32[192,512]{1,0:T(8,128)}, s32[2,192,512]{2,1,0:T(8,128)S(1)}, f32[2,8]{1,0:T(2,128)S(1)}, s32[2,192,512]{2,1,0:T(8,128)S(1)}, /*index=5*/f32[2,8]{1,0:T(2,128)S(1)}, ...), branch_computations={%region_0.37_spmd, %region_37.38_spmd} | conditional | flops 52322824 | bytes 125735176 | solution.py:563
  115.6 3.4 %combine.1 = (f32[2,192,512]{2,1,0:T(8,128)}, f32[2,192,512]{2,1,0:T(8,128)}) custom-call(s32[1]{0:T(128)} %get-tuple-element.51.gz, f32[8,128]{1,0:T(8,128)S(1)} %get-tuple-element.52.coefs, f32[192,512]{1,0:T(8,128)} %get-tuple-element.53.source, f32[192,512]{1,0:T(8,128)} %get-tuple-element.54.rest_0_, f32[192,512]{1,0:T(8,128)} %get-tuple-element.55.rest_1_, ...), custom_call_target="tpu_custom_call" | custom-call | tf_op jit(solution)/shard_map/cond/branch_1_fun/combine/pallas_call | solution.py:468
  (87 shorter events, 14.5 us)
Async XLA Ops:
  3.2 15.6 %collective-permute-start.28 = (f32[192,512]{1,0:T(8,128)}, f32[192,512]{1,0:T(8,128)S(1)}, u32[]{:S(2)}, u32[]{:S(2)}) collective-permute-start(f32[192,512]{1,0:T(8,128)} %get-tuple-element.127.via_i), channel_id=1, source_target_pairs={{0,1},{1,0},{2,3},{3,2},{4,5},{5,4},{6,7},{7,6},{8,9},{9,8},{10,11... | collective-permute-start | bytes 1179656 | tf_op jit(solution)/shard_map/ppermute | solution.py:510
  7.2 11.6 %collective-permute-start.24 = (f32[2,512]{1,0:T(2,128)}, f32[2,512]{1,0:T(2,128)S(1)}, u32[]{:S(2)}, u32[]{:S(2)}) collective-permute-start(f32[2,512]{1,0:T(2,128)} %get-tuple-element.123), channel_id=1, source_target_pairs={{0,2},{2,4},{4,6},{6,8},{8,10},{10,12},{12,14},{14,0},{1,3},{3,5},... | collective-permute-start | bytes 12296 | tf_op jit(solution)/shard_map/ppermute | solution.py:486
  8.5 10.3 %collective-permute-start.25 = (f32[2,512]{1,0:T(2,128)}, f32[2,512]{1,0:T(2,128)S(1)}, u32[]{:S(2)}, u32[]{:S(2)}) collective-permute-start(f32[2,512]{1,0:T(2,128)} %get-tuple-element.124), channel_id=1, source_target_pairs={{2,0},{4,2},{6,4},{8,6},{10,8},{12,10},{14,12},{0,14},{3,1},{5,3},... | collective-permute-start | bytes 12296 | tf_op jit(solution)/shard_map/ppermute | solution.py:487
  12.3 4.0 %collective-permute-start.26 = (f32[2,256]{1,0:T(2,128)}, f32[2,256]{1,0:T(2,128)S(1)}, u32[]{:S(2)}, u32[]{:S(2)}) collective-permute-start(f32[2,256]{1,0:T(2,128)} %get-tuple-element.125), channel_id=1, source_target_pairs={{0,16},{16,32},{32,48},{48,64},{64,80},{80,96},{96,112},{112,128},... | collective-permute-start | bytes 6152 | tf_op jit(solution)/shard_map/ppermute | solution.py:488
  15.3 3.5 %collective-permute-start.27 = (f32[2,256]{1,0:T(2,128)}, f32[2,256]{1,0:T(2,128)S(1)}, u32[]{:S(2)}, u32[]{:S(2)}) collective-permute-start(f32[2,256]{1,0:T(2,128)} %get-tuple-element.126), channel_id=1, source_target_pairs={{16,0},{32,16},{48,32},{64,48},{80,64},{96,80},{112,96},{128,112},... | collective-permute-start | bytes 6152 | tf_op jit(solution)/shard_map/ppermute | solution.py:489
  26.1 12.4 %collective-permute-start.33 = (f32[192,512]{1,0:T(8,128)}, f32[192,512]{1,0:T(8,128)S(1)}, u32[]{:S(2)}, u32[]{:S(2)}) collective-permute-start(f32[192,512]{1,0:T(8,128)} %get-tuple-element.147), channel_id=1, source_target_pairs={{0,1},{1,0},{2,3},{3,2},{4,5},{5,4},{6,7},{7,6},{8,9},{9,8},{10,11... | collective-permute-start | bytes 1179656 | tf_op jit(solution)/shard_map/ppermute | solution.py:522
  26.5 12.1 %collective-permute-start.29 = (f32[2,512]{1,0:T(2,128)}, f32[2,512]{1,0:T(2,128)S(1)}, u32[]{:S(2)}, u32[]{:S(2)}) collective-permute-start(f32[2,512]{1,0:T(2,128)} %get-tuple-element.131), channel_id=1, source_target_pairs={{0,2},{2,4},{4,6},{6,8},{8,10},{10,12},{12,14},{14,0},{1,3},{3,5},... | collective-permute-start | bytes 12296 | tf_op jit(solution)/shard_map/ppermute | solution.py:486
  26.5 12.1 %collective-permute-start.30 = (f32[2,512]{1,0:T(2,128)}, f32[2,512]{1,0:T(2,128)S(1)}, u32[]{:S(2)}, u32[]{:S(2)}) collective-permute-start(f32[2,512]{1,0:T(2,128)} %get-tuple-element.132), channel_id=1, source_target_pairs={{2,0},{4,2},{6,4},{8,6},{10,8},{12,10},{14,12},{0,14},{3,1},{5,3},... | collective-permute-start | bytes 12296 | tf_op jit(solution)/shard_map/ppermute | solution.py:487
  31.5 4.7 %collective-permute-start.31 = (f32[2,256]{1,0:T(2,128)}, f32[2,256]{1,0:T(2,128)S(1)}, u32[]{:S(2)}, u32[]{:S(2)}) collective-permute-start(f32[2,256]{1,0:T(2,128)} %get-tuple-element.133), channel_id=1, source_target_pairs={{0,16},{16,32},{32,48},{48,64},{64,80},{80,96},{96,112},{112,128},... | collective-permute-start | bytes 6152 | tf_op jit(solution)/shard_map/ppermute | solution.py:488
  35.3 3.2 %collective-permute-start.32 = (f32[2,256]{1,0:T(2,128)}, f32[2,256]{1,0:T(2,128)S(1)}, u32[]{:S(2)}, u32[]{:S(2)}) collective-permute-start(f32[2,256]{1,0:T(2,128)} %get-tuple-element.134), channel_id=1, source_target_pairs={{16,0},{32,16},{48,32},{64,48},{80,64},{96,80},{112,96},{128,112},... | collective-permute-start | bytes 6152 | tf_op jit(solution)/shard_map/ppermute | solution.py:489
  45.0 13.2 %collective-permute-start.38 = (f32[192,512]{1,0:T(8,128)S(1)}, f32[192,512]{1,0:T(8,128)S(1)}, u32[]{:S(2)}, u32[]{:S(2)}) collective-permute-start(f32[192,512]{1,0:T(8,128)S(1)} %get-tuple-element.149.v_i), channel_id=1, source_target_pairs={{0,1},{2,3},{4,5},{6,7},{8,9},{10,11},{12,13},{14,15},{16,17},{18,... | collective-permute-start | bytes 1179656 | tf_op jit(solution)/shard_map/ppermute | solution.py:528
  48.4 9.7 %collective-permute-start.34 = (f32[2,512]{1,0:T(2,128)}, f32[2,512]{1,0:T(2,128)S(1)}, u32[]{:S(2)}, u32[]{:S(2)}) collective-permute-start(f32[2,512]{1,0:T(2,128)} %get-tuple-element.151), channel_id=1, source_target_pairs={{0,2},{2,4},{4,6},{6,8},{8,10},{10,12},{12,14},{14,0},{1,3},{3,5},... | collective-permute-start | bytes 12296 | tf_op jit(solution)/shard_map/ppermute | solution.py:486
  48.5 9.6 %collective-permute-start.35 = (f32[2,512]{1,0:T(2,128)}, f32[2,512]{1,0:T(2,128)S(1)}, u32[]{:S(2)}, u32[]{:S(2)}) collective-permute-start(f32[2,512]{1,0:T(2,128)} %get-tuple-element.152), channel_id=1, source_target_pairs={{2,0},{4,2},{6,4},{8,6},{10,8},{12,10},{14,12},{0,14},{3,1},{5,3},... | collective-permute-start | bytes 12296 | tf_op jit(solution)/shard_map/ppermute | solution.py:487
  53.6 2.0 %collective-permute-start.36 = (f32[2,256]{1,0:T(2,128)}, f32[2,256]{1,0:T(2,128)S(1)}, u32[]{:S(2)}, u32[]{:S(2)}) collective-permute-start(f32[2,256]{1,0:T(2,128)} %get-tuple-element.153), channel_id=1, source_target_pairs={{0,16},{16,32},{32,48},{48,64},{64,80},{80,96},{96,112},{112,128},... | collective-permute-start | bytes 6152 | tf_op jit(solution)/shard_map/ppermute | solution.py:488
  54.6 3.5 %collective-permute-start.37 = (f32[2,256]{1,0:T(2,128)}, f32[2,256]{1,0:T(2,128)S(1)}, u32[]{:S(2)}, u32[]{:S(2)}) collective-permute-start(f32[2,256]{1,0:T(2,128)} %get-tuple-element.154), channel_id=1, source_target_pairs={{16,0},{32,16},{48,32},{64,48},{80,64},{96,80},{112,96},{128,112},... | collective-permute-start | bytes 6152 | tf_op jit(solution)/shard_map/ppermute | solution.py:489
  64.5 12.5 %collective-permute-start.43 = (f32[192,512]{1,0:T(8,128)S(1)}, f32[192,512]{1,0:T(8,128)S(1)}, u32[]{:S(2)}, u32[]{:S(2)}) collective-permute-start(f32[192,512]{1,0:T(8,128)S(1)} %get-tuple-element.157.v_i), channel_id=1, source_target_pairs={{0,1},{1,0},{2,3},{3,2},{4,5},{5,4},{6,7},{7,6},{8,9},{9,8},{10,11... | collective-permute-start | bytes 1179656 | tf_op jit(solution)/shard_map/ppermute | solution.py:534
  65.6 11.5 %collective-permute-start.39 = (f32[2,512]{1,0:T(2,128)}, f32[2,512]{1,0:T(2,128)S(1)}, u32[]{:S(2)}, u32[]{:S(2)}) collective-permute-start(f32[2,512]{1,0:T(2,128)} %get-tuple-element.159), channel_id=1, source_target_pairs={{0,2},{2,4},{4,6},{6,8},{8,10},{10,12},{12,14},{14,0},{1,3},{3,5},... | collective-permute-start | bytes 12296 | tf_op jit(solution)/shard_map/ppermute | solution.py:486
  65.6 11.5 %collective-permute-start.40 = (f32[2,512]{1,0:T(2,128)}, f32[2,512]{1,0:T(2,128)S(1)}, u32[]{:S(2)}, u32[]{:S(2)}) collective-permute-start(f32[2,512]{1,0:T(2,128)} %get-tuple-element.160), channel_id=1, source_target_pairs={{2,0},{4,2},{6,4},{8,6},{10,8},{12,10},{14,12},{0,14},{3,1},{5,3},... | collective-permute-start | bytes 12296 | tf_op jit(solution)/shard_map/ppermute | solution.py:487
  70.7 3.5 %collective-permute-start.41 = (f32[2,256]{1,0:T(2,128)}, f32[2,256]{1,0:T(2,128)S(1)}, u32[]{:S(2)}, u32[]{:S(2)}) collective-permute-start(f32[2,256]{1,0:T(2,128)} %get-tuple-element.161), channel_id=1, source_target_pairs={{0,16},{16,32},{32,48},{48,64},{64,80},{80,96},{96,112},{112,128},... | collective-permute-start | bytes 6152 | tf_op jit(solution)/shard_map/ppermute | solution.py:488
  73.3 3.5 %collective-permute-start.42 = (f32[2,256]{1,0:T(2,128)}, f32[2,256]{1,0:T(2,128)S(1)}, u32[]{:S(2)}, u32[]{:S(2)}) collective-permute-start(f32[2,256]{1,0:T(2,128)} %get-tuple-element.162), channel_id=1, source_target_pairs={{16,0},{32,16},{48,32},{64,48},{80,64},{96,80},{112,96},{128,112},... | collective-permute-start | bytes 6152 | tf_op jit(solution)/shard_map/ppermute | solution.py:489
  77.8 37.7 %copy-start.19 = (s32[2,192,512]{2,1,0:T(8,128)S(1)}, s32[2,192,512]{2,1,0:T(8,128)}, u32[]{:S(2)}) copy-start(s32[2,192,512]{2,1,0:T(8,128)} %classes.3) | copy-start | bytes 2359300
  77.8 37.7 %copy-start.41 = (f32[2,8]{1,0:T(2,128)S(1)}, f32[2,8]{1,0:T(2,128)}, u32[]{:S(2)}) copy-start(f32[2,8]{1,0:T(2,128)} %table.2) | copy-start | bytes 196
  77.8 37.7 %copy-start.42 = (f32[2,8]{1,0:T(2,128)S(1)}, f32[2,8]{1,0:T(2,128)}, u32[]{:S(2)}) copy-start(f32[2,8]{1,0:T(2,128)} %table.3) | copy-start | bytes 196
  100.8 12.0 %all-to-all-start.1 = ((f32[16,8,128]{2,1,0:T(8,128)}), f32[16,8,128]{2,1,0:T(8,128)S(1)}, u32[]{:S(2)}, u32[]{:S(2)}) async-start(f32[16,8,128]{2,1,0:T(8,128)} %relay.1), calls=%async_computation.1 | async-start | bytes 131072 | tf_op jit(solution)/shard_map/all_to_all | solution.py:545
  (26 other events, 101.4 us)

commit v2 on v1

--- a/solution.py
+++ b/solution.py
@@ -183,6 +183,7 @@
 STEP = 8
 LANES = 128
 GUARD = 0.02
+GRANT = 16 * 1024 * 1024
 VMEM = pl.BlockSpec(memory_space=pltpu.VMEM)
 SMEM = pl.BlockSpec(memory_space=pltpu.SMEM)
 
@@ -472,6 +473,7 @@
         out_specs=[VMEM] * len(outs),
         out_shape=outs,
         scratch_shapes=scratch,
+        compiler_params=pltpu.CompilerParams(vmem_limit_bytes=GRANT),
     )(*args)
 
 
@@ -547,20 +549,17 @@
         solve_kernel, "solve", [sheet, jax.ShapeDtypeStruct((1, LANES), jnp.int32)], [], 0, parts
     )
 
-    def fast():
-        return tuple(
-            call(
-                combine_kernel, "combine", [both] * 2, [], 1, gz, coefs, source,
-                v0i, v0o, v1i, v1o, v2i, v2o, n0i, n0o, n1i, n1o, n2i, n2o,
-            )
-        )
+    quick = call(
+        combine_kernel, "combine", [both] * 2, [], 1, gz, coefs, source,
+        v0i, v0o, v1i, v1o, v2i, v2o, n0i, n0o, n1i, n1o, n2i, n2o,
+    )
 
     def careful():
         return recurrence(
             load_current, sink_mask, pad_mask, plane_class, via_class, plane_table, via_table
         )
 
-    return lax.cond(flag[0, 0] == 1, fast, careful)
+    return lax.cond(flag[0, 0] == 1, lambda: tuple(quick), careful)
 
 
 def solution(mesh):

time: 119 us -> 102 us (0.86)
  Pallas kernels: 32.4 us -> 14.3 us
  local copies, waits for them, and re-layouts: 3.64 us -> 6.12 us
    pallas_call x9, Pallas kernels: 32.4 us -> 14.3 us  [call(): pl.pallas_call(kernel, name=name, in_specs=[SMEM] * n_smem + [VMEM] * (le...]
    unnamed x58 -> x28, local copies, waits for them, and re-layouts: 3.64 us -> 6.12 us
  transfers between devices with their start and end apart: 21 -> 21, of which waited for: 10 -> 11; matrix products, arithmetic and copies ran while one was open for 0% -> 0% of each run, Pallas kernels for 2% -> 1%
where the time goes in v2:
time: 102 us
  starting transfers between devices  42.5 us (42%)
  waiting for transfers between devices  20.7 us (20%)
  blocking collectives  17.4 us (17%)
  Pallas kernels  14.3 us (14%)
  local copies, waits for them, and re-layouts  6.12 us (6%)
    ppermute x4, starting transfers between devices, halos(): lax.ppermute(first_row, GY, back_y)  19 us
    all_to_all x1, blocking collectives, shards(): parts = lax.all_to_all(spread, GX, 0, 0, tiled=True)  17.4 us
    pallas_call x9, Pallas kernels, call(): pl.pallas_call(kernel, name=name, in_specs=[SMEM] * n_smem + [VMEM] * (le...  14.3 us
    ppermute x4, starting transfers between devices, halos(): lax.ppermute(last_col, GX, up_x)  10.4 us
    ppermute x4, waiting for transfers between devices, halos(): lax.ppermute(first_col, GX, back_x)  9.85 us
    all_to_all x1, waiting for transfers between devices, shards(): parts = lax.all_to_all(spread, ('gy_0', 'gy_1', 'gz'), 0, 0, tiled=True)  6.57 us
    unnamed x28, local copies, waits for them, and re-layouts  6.12 us
    all_to_all x1, starting transfers between devices, shards(): parts = lax.all_to_all(spread, ('gy_0', 'gy_1', 'gz'), 0, 0, tiled=True)  4.62 us
  transfers between devices with their start and end apart: 21, of which 11 were waited for; matrix products, arithmetic and copies ran while one was open for 0% of the time, Pallas kernels for 1%

profile of v2, /device:TPU:1, one launch (start us, length us, event | category | flops | bytes accessed | tf_op | source)
XLA Modules:
  0.0 101.8 jit_solution(5835251674435572678)
XLA Ops:
  0.7 1.7 %via.1 = (f32[192,512]{1,0:T(8,128)S(1)}, f32[192,512]{1,0:T(8,128)S(1)}) custom-call(s32[1]{0:T(128)} %bitcast.23.gz, f32[2,8]{1,0:T(2,128)} %table.3, s32[2,192,512]{2,1,0:T(8,128)} %classes.3), custom_call_target="tpu_custom_call" | custom-call | tf_op jit(solution)/shard_map/via/pallas_call | solution.py:469
  2.4 2.1 %collective-permute-start.28 = (f32[192,512]{1,0:T(8,128)S(1)}, f32[192,512]{1,0:T(8,128)S(1)}, u32[]{:S(2)}, u32[]{:S(2)}) collective-permute-start(f32[192,512]{1,0:T(8,128)S(1)} %get-tuple-element.86.via_i), channel_id=1, source_target_pairs={{0,1},{1,0},{2,3},{3,2},{4,5},{5,4},{6,7},{7,6},{8,9},{9,8},{10,11... | collective-permute-start | bytes 1179656 | tf_op jit(solution)/shard_map/ppermute | solution.py:512
  4.5 1.1 %plane.1 = (f32[192,512]{1,0:T(8,128)S(1)}, f32[192,512]{1,0:T(8,128)S(1)}, f32[2,512]{1,0:T(2,128)S(1)}, f32[2,512]{1,0:T(2,128)S(1)}, f32[2,256]{1,0:T(2,128)S(1)}, /*index=5*/f32[2,256]{1,0:T(2,128)S(1)}) custom-call(s32[1]{0:T(128)} %bitcast.23.gz, f32[2,8]{1,0:T(2,128)} %table.2, s32[2,192,512]{2,1,0:T(8,128)S(1)} %copy-done.27), custom_call_target="tpu_custom_call" | custom-call | tf_op jit(solution)/shard_map/plane/pallas_call | solution.py:469
  5.6 1.3 %collective-permute-start.24 = (f32[2,512]{1,0:T(2,128)S(1)}, f32[2,512]{1,0:T(2,128)S(1)}, u32[]{:S(2)}, u32[]{:S(2)}) collective-permute-start(f32[2,512]{1,0:T(2,128)S(1)} %get-tuple-element.82), channel_id=1, source_target_pairs={{0,2},{2,4},{4,6},{6,8},{8,10},{10,12},{12,14},{14,0},{1,3},{3,5},... | collective-permute-start | bytes 12296 | tf_op jit(solution)/shard_map/ppermute | solution.py:488
  7.0 3.8 %collective-permute-start.25 = (f32[2,512]{1,0:T(2,128)S(1)}, f32[2,512]{1,0:T(2,128)S(1)}, u32[]{:S(2)}, u32[]{:S(2)}) collective-permute-start(f32[2,512]{1,0:T(2,128)S(1)} %get-tuple-element.83), channel_id=1, source_target_pairs={{2,0},{4,2},{6,4},{8,6},{10,8},{12,10},{14,12},{0,14},{3,1},{5,3},... | collective-permute-start | bytes 12296 | tf_op jit(solution)/shard_map/ppermute | solution.py:489
  10.8 3.0 %collective-permute-start.26 = (f32[2,256]{1,0:T(2,128)S(1)}, f32[2,256]{1,0:T(2,128)S(1)}, u32[]{:S(2)}, u32[]{:S(2)}) collective-permute-start(f32[2,256]{1,0:T(2,128)S(1)} %get-tuple-element.84), channel_id=1, source_target_pairs={{0,16},{16,32},{32,48},{48,64},{64,80},{80,96},{96,112},{112,128},... | collective-permute-start | bytes 6152 | tf_op jit(solution)/shard_map/ppermute | solution.py:490
  14.5 2.6 %collective-permute-done.27.east = f32[2,256]{1,0:T(2,128)S(1)} collective-permute-done((f32[2,256]{1,0:T(2,128)S(1)}, f32[2,256]{1,0:T(2,128)S(1)}, u32[]{:S(2)}, u32[]{:S(2)}) %collective-permute-start.27) | collective-permute-done | bytes 2080 | tf_op jit(solution)/shard_map/ppermute | solution.py:491
  17.8 3.7 %edge.1 = (f32[192,512]{1,0:T(8,128)S(1)}, f32[192,512]{1,0:T(8,128)S(1)}, f32[192,512]{1,0:T(8,128)S(1)}, f32[192,512]{1,0:T(8,128)S(1)}, f32[192,512]{1,0:T(8,...) custom-call(s32[1]{0:T(128)} %bitcast.23.gz, ...), custom_call_target="tpu_custom_call" | custom-call | tf_op jit(solution)/shard_map/edge/pallas_call | solution.py:469
  21.5 5.1 %collective-permute-start.30 = (f32[2,512]{1,0:T(2,128)S(1)}, f32[2,512]{1,0:T(2,128)S(1)}, u32[]{:S(2)}, u32[]{:S(2)}) collective-permute-start(f32[2,512]{1,0:T(2,128)S(1)} %get-tuple-element.91), channel_id=1, source_target_pairs={{2,0},{4,2},{6,4},{8,6},{10,8},{12,10},{14,12},{0,14},{3,1},{5,3},... | collective-permute-start | bytes 12296 | tf_op jit(solution)/shard_map/ppermute | solution.py:489
  26.6 4.0 %collective-permute-start.31 = (f32[2,256]{1,0:T(2,128)S(1)}, f32[2,256]{1,0:T(2,128)S(1)}, u32[]{:S(2)}, u32[]{:S(2)}) collective-permute-start(f32[2,256]{1,0:T(2,128)S(1)} %get-tuple-element.92), channel_id=1, source_target_pairs={{0,16},{16,32},{32,48},{48,64},{64,80},{80,96},{96,112},{112,128},... | collective-permute-start | bytes 6152 | tf_op jit(solution)/shard_map/ppermute | solution.py:490
  31.4 2.3 %collective-permute-done.32.east = f32[2,256]{1,0:T(2,128)S(1)} collective-permute-done((f32[2,256]{1,0:T(2,128)S(1)}, f32[2,256]{1,0:T(2,128)S(1)}, u32[]{:S(2)}, u32[]{:S(2)}) %collective-permute-start.32) | collective-permute-done | bytes 2080 | tf_op jit(solution)/shard_map/ppermute | solution.py:491
  33.7 2.2 %first.1 = (f32[192,512]{1,0:T(8,128)S(1)}, f32[192,512]{1,0:T(8,128)S(1)}, f32[192,512]{1,0:T(8,128)S(1)}, f32[192,512]{1,0:T(8,128)S(1)}, f32[192,512]{1,0:T(8...) custom-call(s32[1]{0:T(128)} %bitcast.23.gz, ...), custom_call_target="tpu_custom_call" | custom-call | tf_op jit(solution)/shard_map/first/pallas_call | solution.py:469
  35.9 3.4 %collective-permute-start.38 = (f32[192,512]{1,0:T(8,128)S(1)}, f32[192,512]{1,0:T(8,128)S(1)}, u32[]{:S(2)}, u32[]{:S(2)}) collective-permute-start(f32[192,512]{1,0:T(8,128)S(1)} %get-tuple-element.108.v_i.rest_2_), channel_id=1, source_target_pairs={{0,1},{2,3},{4,5},{6,7},{8,9},{10,11},{12,13},{14,15},{16,17},{18,... | collective-permute-start | bytes 1179656 | tf_op jit(solution)/shard_map/ppermute | solution.py:530
  39.5 5.1 %collective-permute-start.35 = (f32[2,512]{1,0:T(2,128)S(1)}, f32[2,512]{1,0:T(2,128)S(1)}, u32[]{:S(2)}, u32[]{:S(2)}) collective-permute-start(f32[2,512]{1,0:T(2,128)S(1)} %get-tuple-element.111), channel_id=1, source_target_pairs={{2,0},{4,2},{6,4},{8,6},{10,8},{12,10},{14,12},{0,14},{3,1},{5,3},... | collective-permute-start | bytes 12296 | tf_op jit(solution)/shard_map/ppermute | solution.py:489
  46.2 2.6 %collective-permute-done.37.east = f32[2,256]{1,0:T(2,128)S(1)} collective-permute-done((f32[2,256]{1,0:T(2,128)S(1)}, f32[2,256]{1,0:T(2,128)S(1)}, u32[]{:S(2)}, u32[]{:S(2)}) %collective-permute-start.37) | collective-permute-done | bytes 2080 | tf_op jit(solution)/shard_map/ppermute | solution.py:491
  48.7 2.3 %second.1 = (f32[192,512]{1,0:T(8,128)S(1)}, f32[192,512]{1,0:T(8,128)S(1)}, f32[192,512]{1,0:T(8,128)S(1)}, f32[192,512]{1,0:T(8,128)S(1)}, f32[2,512]{1,0:T(2,...) custom-call(s32[1]{0:T(128)} %bitcast.23.gz, ...), custom_call_target="tpu_custom_call" | custom-call | tf_op jit(solution)/shard_map/second/pallas_call | solution.py:469
  51.0 1.3 %collective-permute-start.43 = (f32[192,512]{1,0:T(8,128)S(1)}, f32[192,512]{1,0:T(8,128)S(1)}, u32[]{:S(2)}, u32[]{:S(2)}) collective-permute-start(f32[192,512]{1,0:T(8,128)S(1)} %get-tuple-element.116.v_i.rest_4_), channel_id=1, source_target_pairs={{0,1},{1,0},{2,3},{3,2},{4,5},{5,4},{6,7},{7,6},{8,9},{9,8},{10,11... | collective-permute-start | bytes 1179656 | tf_op jit(solution)/shard_map/ppermute | solution.py:536
  52.3 5.1 %collective-permute-start.40 = (f32[2,512]{1,0:T(2,128)S(1)}, f32[2,512]{1,0:T(2,128)S(1)}, u32[]{:S(2)}, u32[]{:S(2)}) collective-permute-start(f32[2,512]{1,0:T(2,128)S(1)} %get-tuple-element.119), channel_id=1, source_target_pairs={{2,0},{4,2},{6,4},{8,6},{10,8},{12,10},{14,12},{0,14},{3,1},{5,3},... | collective-permute-start | bytes 12296 | tf_op jit(solution)/shard_map/ppermute | solution.py:489
  57.3 2.5 %collective-permute-start.41 = (f32[2,256]{1,0:T(2,128)S(1)}, f32[2,256]{1,0:T(2,128)S(1)}, u32[]{:S(2)}, u32[]{:S(2)}) collective-permute-start(f32[2,256]{1,0:T(2,128)S(1)} %get-tuple-element.120), channel_id=1, source_target_pairs={{0,16},{16,32},{32,48},{48,64},{64,80},{80,96},{96,112},{112,128},... | collective-permute-start | bytes 6152 | tf_op jit(solution)/shard_map/ppermute | solution.py:490
  60.6 2.4 %collective-permute-done.42.east = f32[2,256]{1,0:T(2,128)S(1)} collective-permute-done((f32[2,256]{1,0:T(2,128)S(1)}, f32[2,256]{1,0:T(2,128)S(1)}, u32[]{:S(2)}, u32[]{:S(2)}) %collective-permute-start.42) | collective-permute-done | bytes 2080 | tf_op jit(solution)/shard_map/ppermute | solution.py:491
  66.1 17.4 %all_to_all.10.parts = f32[16,8,128]{2,1,0:T(8,128)S(1)} all-to-all(f32[16,8,128]{2,1,0:T(8,128)S(1)} %get-tuple-element.123), channel_id=1, replica_groups=mesh['gx_0'=8,'gx_1'=2,'gy_0'=2,'gy_1'=4,'gz'=2] {'gx_0','gx_1'}, dimensions={0} | all-to-all | bytes 131072 | tf_op jit(solution)/shard_map/all_to_all | solution.py:543
  84.1 4.6 %all-to-all-start.1 = ((f32[16,8,128]{2,1,0:T(8,128)}), f32[16,8,128]{2,1,0:T(8,128)}, u32[]{:S(2)}, u32[]{:S(2)}) async-start(f32[16,8,128]{2,1,0:T(8,128)} %copy-done.8), calls=%async_computation.1 | async-start | bytes 131072 | tf_op jit(solution)/shard_map/all_to_all | solution.py:547
  88.7 6.6 %all-to-all-done.1.parts = f32[16,8,128]{2,1,0:T(8,128)} async-done(((f32[16,8,128]{2,1,0:T(8,128)}), f32[16,8,128]{2,1,0:T(8,128)}, u32[]{:S(2)}, u32[]{:S(2)}) %all-to-all-start.1) | async-done | bytes 65568 | tf_op jit(solution)/shard_map/all_to_all | solution.py:547
  100.3 1.5 %combine.1 = (f32[2,192,512]{2,1,0:T(8,128)}, f32[2,192,512]{2,1,0:T(8,128)}) custom-call(s32[1]{0:T(128)} %bitcast.23.gz, f32[8,128]{1,0:T(8,128)S(1)} %get-tuple-element.125.coefs, f32[192,512]{1,0:T(8,128)S(1)} %get-tuple-element.126.source, f32[192,512]{1,0:T(8,128)S(1)} %get-tuple-element.88.v_i.rest_0_, f32[192,512]{1,0:T(8,128)S(1)} %get-tuple-element.89.v_o.rest_1_, ...), custom_call_target="tpu_custom_call" | custom-call | tf_op jit(solution)/shard_map/combine/pallas_call | solution.py:469
  (57 shorter events, 13.3 us)
Async XLA Ops:
  0.6 17.1 %copy-start.29 = (s32[192,512]{1,0:T(8,128)S(1)}, s32[192,512]{1,0:T(8,128)}, u32[]{:S(2)}) copy-start(s32[192,512]{1,0:T(8,128)} %pad.624) | copy-start | bytes 1179652
  0.7 17.1 %copy-start.31 = (f32[192,512]{1,0:T(8,128)S(1)}, f32[192,512]{1,0:T(8,128)}, u32[]{:S(2)}) copy-start(f32[192,512]{1,0:T(8,128)} %load.1) | copy-start | bytes 1179652
  2.4 15.3 %collective-permute-start.28 = (f32[192,512]{1,0:T(8,128)S(1)}, f32[192,512]{1,0:T(8,128)S(1)}, u32[]{:S(2)}, u32[]{:S(2)}) collective-permute-start(f32[192,512]{1,0:T(8,128)S(1)} %get-tuple-element.86.via_i), channel_id=1, source_target_pairs={{0,1},{1,0},{2,3},{3,2},{4,5},{5,4},{6,7},{7,6},{8,9},{9,8},{10,11... | collective-permute-start | bytes 1179656 | tf_op jit(solution)/shard_map/ppermute | solution.py:512
  5.6 12.1 %collective-permute-start.24 = (f32[2,512]{1,0:T(2,128)S(1)}, f32[2,512]{1,0:T(2,128)S(1)}, u32[]{:S(2)}, u32[]{:S(2)}) collective-permute-start(f32[2,512]{1,0:T(2,128)S(1)} %get-tuple-element.82), channel_id=1, source_target_pairs={{0,2},{2,4},{4,6},{6,8},{8,10},{10,12},{12,14},{14,0},{1,3},{3,5},... | collective-permute-start | bytes 12296 | tf_op jit(solution)/shard_map/ppermute | solution.py:488
  7.0 10.8 %collective-permute-start.25 = (f32[2,512]{1,0:T(2,128)S(1)}, f32[2,512]{1,0:T(2,128)S(1)}, u32[]{:S(2)}, u32[]{:S(2)}) collective-permute-start(f32[2,512]{1,0:T(2,128)S(1)} %get-tuple-element.83), channel_id=1, source_target_pairs={{2,0},{4,2},{6,4},{8,6},{10,8},{12,10},{14,12},{0,14},{3,1},{5,3},... | collective-permute-start | bytes 12296 | tf_op jit(solution)/shard_map/ppermute | solution.py:489
  10.8 3.8 %collective-permute-start.26 = (f32[2,256]{1,0:T(2,128)S(1)}, f32[2,256]{1,0:T(2,128)S(1)}, u32[]{:S(2)}, u32[]{:S(2)}) collective-permute-start(f32[2,256]{1,0:T(2,128)S(1)} %get-tuple-element.84), channel_id=1, source_target_pairs={{0,16},{16,32},{32,48},{48,64},{64,80},{80,96},{96,112},{112,128},... | collective-permute-start | bytes 6152 | tf_op jit(solution)/shard_map/ppermute | solution.py:490
  13.8 3.3 %collective-permute-start.27 = (f32[2,256]{1,0:T(2,128)S(1)}, f32[2,256]{1,0:T(2,128)S(1)}, u32[]{:S(2)}, u32[]{:S(2)}) collective-permute-start(f32[2,256]{1,0:T(2,128)S(1)} %get-tuple-element.85), channel_id=1, source_target_pairs={{16,0},{32,16},{48,32},{64,48},{80,64},{96,80},{112,96},{128,112},... | collective-permute-start | bytes 6152 | tf_op jit(solution)/shard_map/ppermute | solution.py:491
  21.4 12.3 %collective-permute-start.33 = (f32[192,512]{1,0:T(8,128)S(1)}, f32[192,512]{1,0:T(8,128)S(1)}, u32[]{:S(2)}, u32[]{:S(2)}) collective-permute-start(f32[192,512]{1,0:T(8,128)S(1)} %get-tuple-element.106), channel_id=1, source_target_pairs={{0,1},{1,0},{2,3},{3,2},{4,5},{5,4},{6,7},{7,6},{8,9},{9,8},{10,11... | collective-permute-start | bytes 1179656 | tf_op jit(solution)/shard_map/ppermute | solution.py:524
  21.5 12.2 %collective-permute-start.29 = (f32[2,512]{1,0:T(2,128)S(1)}, f32[2,512]{1,0:T(2,128)S(1)}, u32[]{:S(2)}, u32[]{:S(2)}) collective-permute-start(f32[2,512]{1,0:T(2,128)S(1)} %get-tuple-element.90), channel_id=1, source_target_pairs={{0,2},{2,4},{4,6},{6,8},{8,10},{10,12},{12,14},{14,0},{1,3},{3,5},... | collective-permute-start | bytes 12296 | tf_op jit(solution)/shard_map/ppermute | solution.py:488
  21.5 12.1 %collective-permute-start.30 = (f32[2,512]{1,0:T(2,128)S(1)}, f32[2,512]{1,0:T(2,128)S(1)}, u32[]{:S(2)}, u32[]{:S(2)}) collective-permute-start(f32[2,512]{1,0:T(2,128)S(1)} %get-tuple-element.91), channel_id=1, source_target_pairs={{2,0},{4,2},{6,4},{8,6},{10,8},{12,10},{14,12},{0,14},{3,1},{5,3},... | collective-permute-start | bytes 12296 | tf_op jit(solution)/shard_map/ppermute | solution.py:489
  26.6 4.8 %collective-permute-start.31 = (f32[2,256]{1,0:T(2,128)S(1)}, f32[2,256]{1,0:T(2,128)S(1)}, u32[]{:S(2)}, u32[]{:S(2)}) collective-permute-start(f32[2,256]{1,0:T(2,128)S(1)} %get-tuple-element.92), channel_id=1, source_target_pairs={{0,16},{16,32},{32,48},{48,64},{64,80},{80,96},{96,112},{112,128},... | collective-permute-start | bytes 6152 | tf_op jit(solution)/shard_map/ppermute | solution.py:490
  30.7 3.0 %collective-permute-start.32 = (f32[2,256]{1,0:T(2,128)S(1)}, f32[2,256]{1,0:T(2,128)S(1)}, u32[]{:S(2)}, u32[]{:S(2)}) collective-permute-start(f32[2,256]{1,0:T(2,128)S(1)} %get-tuple-element.93), channel_id=1, source_target_pairs={{16,0},{32,16},{48,32},{64,48},{80,64},{96,80},{112,96},{128,112},... | collective-permute-start | bytes 6152 | tf_op jit(solution)/shard_map/ppermute | solution.py:491
  35.9 12.8 %collective-permute-start.38 = (f32[192,512]{1,0:T(8,128)S(1)}, f32[192,512]{1,0:T(8,128)S(1)}, u32[]{:S(2)}, u32[]{:S(2)}) collective-permute-start(f32[192,512]{1,0:T(8,128)S(1)} %get-tuple-element.108.v_i.rest_2_), channel_id=1, source_target_pairs={{0,1},{2,3},{4,5},{6,7},{8,9},{10,11},{12,13},{14,15},{16,17},{18,... | collective-permute-start | bytes 1179656 | tf_op jit(solution)/shard_map/ppermute | solution.py:530
  39.4 9.4 %collective-permute-start.34 = (f32[2,512]{1,0:T(2,128)S(1)}, f32[2,512]{1,0:T(2,128)S(1)}, u32[]{:S(2)}, u32[]{:S(2)}) collective-permute-start(f32[2,512]{1,0:T(2,128)S(1)} %get-tuple-element.110), channel_id=1, source_target_pairs={{0,2},{2,4},{4,6},{6,8},{8,10},{10,12},{12,14},{14,0},{1,3},{3,5},... | collective-permute-start | bytes 12296 | tf_op jit(solution)/shard_map/ppermute | solution.py:488
  39.5 9.3 %collective-permute-start.35 = (f32[2,512]{1,0:T(2,128)S(1)}, f32[2,512]{1,0:T(2,128)S(1)}, u32[]{:S(2)}, u32[]{:S(2)}) collective-permute-start(f32[2,512]{1,0:T(2,128)S(1)} %get-tuple-element.111), channel_id=1, source_target_pairs={{2,0},{4,2},{6,4},{8,6},{10,8},{12,10},{14,12},{0,14},{3,1},{5,3},... | collective-permute-start | bytes 12296 | tf_op jit(solution)/shard_map/ppermute | solution.py:489
  44.5 1.6 %collective-permute-start.36 = (f32[2,256]{1,0:T(2,128)S(1)}, f32[2,256]{1,0:T(2,128)S(1)}, u32[]{:S(2)}, u32[]{:S(2)}) collective-permute-start(f32[2,256]{1,0:T(2,128)S(1)} %get-tuple-element.112), channel_id=1, source_target_pairs={{0,16},{16,32},{32,48},{48,64},{64,80},{80,96},{96,112},{112,128},... | collective-permute-start | bytes 6152 | tf_op jit(solution)/shard_map/ppermute | solution.py:490
  45.4 3.3 %collective-permute-start.37 = (f32[2,256]{1,0:T(2,128)S(1)}, f32[2,256]{1,0:T(2,128)S(1)}, u32[]{:S(2)}, u32[]{:S(2)}) collective-permute-start(f32[2,256]{1,0:T(2,128)S(1)} %get-tuple-element.113), channel_id=1, source_target_pairs={{16,0},{32,16},{48,32},{64,48},{80,64},{96,80},{112,96},{128,112},... | collective-permute-start | bytes 6152 | tf_op jit(solution)/shard_map/ppermute | solution.py:491
  51.0 13.5 %copy-start.2 = (f32[192,512]{1,0:T(8,128)}, f32[192,512]{1,0:T(8,128)S(1)}, u32[]{:S(2)}) copy-start(f32[192,512]{1,0:T(8,128)S(1)} %get-tuple-element.130.rest_9_) | copy-start | bytes 1179652
  51.0 12.7 %collective-permute-start.43 = (f32[192,512]{1,0:T(8,128)S(1)}, f32[192,512]{1,0:T(8,128)S(1)}, u32[]{:S(2)}, u32[]{:S(2)}) collective-permute-start(f32[192,512]{1,0:T(8,128)S(1)} %get-tuple-element.116.v_i.rest_4_), channel_id=1, source_target_pairs={{0,1},{1,0},{2,3},{3,2},{4,5},{5,4},{6,7},{7,6},{8,9},{9,8},{10,11... | collective-permute-start | bytes 1179656 | tf_op jit(solution)/shard_map/ppermute | solution.py:536
  52.3 11.5 %collective-permute-start.39 = (f32[2,512]{1,0:T(2,128)S(1)}, f32[2,512]{1,0:T(2,128)S(1)}, u32[]{:S(2)}, u32[]{:S(2)}) collective-permute-start(f32[2,512]{1,0:T(2,128)S(1)} %get-tuple-element.118), channel_id=1, source_target_pairs={{0,2},{2,4},{4,6},{6,8},{8,10},{10,12},{12,14},{14,0},{1,3},{3,5},... | collective-permute-start | bytes 12296 | tf_op jit(solution)/shard_map/ppermute | solution.py:488
  52.3 11.5 %collective-permute-start.40 = (f32[2,512]{1,0:T(2,128)S(1)}, f32[2,512]{1,0:T(2,128)S(1)}, u32[]{:S(2)}, u32[]{:S(2)}) collective-permute-start(f32[2,512]{1,0:T(2,128)S(1)} %get-tuple-element.119), channel_id=1, source_target_pairs={{2,0},{4,2},{6,4},{8,6},{10,8},{12,10},{14,12},{0,14},{3,1},{5,3},... | collective-permute-start | bytes 12296 | tf_op jit(solution)/shard_map/ppermute | solution.py:489
  57.3 3.2 %collective-permute-start.41 = (f32[2,256]{1,0:T(2,128)S(1)}, f32[2,256]{1,0:T(2,128)S(1)}, u32[]{:S(2)}, u32[]{:S(2)}) collective-permute-start(f32[2,256]{1,0:T(2,128)S(1)} %get-tuple-element.120), channel_id=1, source_target_pairs={{0,16},{16,32},{32,48},{48,64},{64,80},{80,96},{96,112},{112,128},... | collective-permute-start | bytes 6152 | tf_op jit(solution)/shard_map/ppermute | solution.py:490
  59.8 3.2 %collective-permute-start.42 = (f32[2,256]{1,0:T(2,128)S(1)}, f32[2,256]{1,0:T(2,128)S(1)}, u32[]{:S(2)}, u32[]{:S(2)}) collective-permute-start(f32[2,256]{1,0:T(2,128)S(1)} %get-tuple-element.121), channel_id=1, source_target_pairs={{16,0},{32,16},{48,32},{64,48},{80,64},{96,80},{112,96},{128,112},... | collective-permute-start | bytes 6152 | tf_op jit(solution)/shard_map/ppermute | solution.py:491
  84.1 11.2 %all-to-all-start.1 = ((f32[16,8,128]{2,1,0:T(8,128)}), f32[16,8,128]{2,1,0:T(8,128)}, u32[]{:S(2)}, u32[]{:S(2)}) async-start(f32[16,8,128]{2,1,0:T(8,128)} %copy-done.8), calls=%async_computation.1 | async-start | bytes 131072 | tf_op jit(solution)/shard_map/all_to_all | solution.py:547
  (11 other events, 26.5 us)

commit v3 on v0

--- a/solution.py
+++ b/solution.py
@@ -1,6 +1,8 @@
 import jax
 import jax.numpy as jnp
 from jax import lax
+from jax.experimental import pallas as pl
+from jax.experimental.pallas import tpu as pltpu
 from jax.sharding import Mesh
 from jax.sharding import PartitionSpec as P
 
@@ -106,7 +108,7 @@
     )
 
 
-def shards(load_current, sink_mask, pad_mask, plane_class, via_class, plane_table, via_table):
+def recurrence(load_current, sink_mask, pad_mask, plane_class, via_class, plane_table, via_table):
     n_layers, n_rows, n_cols = plane_class.shape
     g_plane = lookup(plane_class, plane_table)
     g_via = lookup(via_class, via_table)
@@ -178,6 +180,579 @@
     return (voltage, residual)
 
 
+STEP = 8
+LANES = 128
+DEEP = 4
+GUARD = 0.02
+GRANT = 16 * 1024 * 1024
+N_OWN = 6
+N_FAR = 4
+VMEM = pl.BlockSpec(memory_space=pltpu.VMEM)
+SMEM = pl.BlockSpec(memory_space=pltpu.SMEM)
+
+
+def block(k):
+    return pl.ds(pl.multiple_of(k * STEP, STEP), STEP)
+
+
+def select_class(classes, entry):
+    low = (classes & 1) != 0
+    mid = (classes & 2) != 0
+    high = (classes & 4) != 0
+    pairs = [jnp.where(low, entry(2 * k + 1), entry(2 * k)) for k in range(4)]
+    return jnp.where(high, jnp.where(mid, pairs[3], pairs[2]), jnp.where(mid, pairs[1], pairs[0]))
+
+
+def via_kernel(gz, table, classes, via, pair, lone):
+    group = gz[0]
+    n_rows = via.shape[1]
+    half = n_rows // 2 // STEP
+
+    def fill(k, carry):
+        rows = block(k)
+        one = select_class(classes[1 - group, rows, :], lambda e: table[1 - group, e])
+        two = select_class(classes[group, rows, :], lambda e: table[group, e])
+        via[0, rows, :] = one
+        via[1, rows, :] = harmonic(one, two)
+        return carry
+
+    lax.fori_loop(0, n_rows // STEP, fill, 0, unroll=2)
+
+    def copy(k, carry):
+        for f in range(2):
+            pair[f, block(k), :] = via[f, block(k + (1 - group) * half), :]
+        lone[block(k), :] = via[0, block(k + group * half), :]
+        return carry
+
+    lax.fori_loop(0, half, copy, 0, unroll=2)
+
+
+def plane_kernel(gz, table, classes, load, sink, pad, via, plane, drawn, pair, top, bottom):
+    group = gz[0]
+    n_rows = plane.shape[1]
+    half = n_rows // 2 // STEP
+
+    def fill(k, carry):
+        rows = block(k)
+        plane[0, rows, :] = select_class(
+            classes[1 - group, rows, :], lambda e: table[1 - group, e]
+        )
+        plane[1, rows, :] = select_class(classes[group, rows, :], lambda e: table[group, e])
+        plane[2, rows, :] = PAD_CONDUCTANCE * pad[rows, :].astype(jnp.float32)
+        drawn[rows, :] = sink[rows, :].astype(jnp.float32) * load[rows, :]
+        return carry
+
+    lax.fori_loop(0, n_rows // STEP, fill, 0, unroll=2)
+
+    def copy(k, carry):
+        for f in range(2):
+            pair[f, block(k), :] = plane[f, block(k + (1 - group) * half), :]
+        return carry
+
+    lax.fori_loop(0, half, copy, 0, unroll=2)
+    for f in range(N_OWN):
+        at = pl.ds(DEEP * f, DEEP)
+        top[at, :] = field_rows(plane, via, drawn, f, pl.ds(0, DEEP))
+        bottom[at, :] = field_rows(plane, via, drawn, f, pl.ds(n_rows - DEEP, DEEP))
+
+
+def field_rows(plane, via, drawn, f, rows):
+    if f == 4:
+        return drawn[rows, :]
+    if f in (2, 3):
+        return via[f - 2, rows, :]
+    return plane[2 if f == 5 else f, rows, :]
+
+
+def tile_of(stack, f, upper):
+    rows = stack[f // 2 * STEP : f // 2 * STEP + STEP, :]
+    return rows if (f % 2 == 1) == upper else pltpu.roll(rows, DEEP, 0)
+
+
+def columns_kernel(plane, via, drawn, south, north, first, last, stage):
+    n_rows, n_cols = drawn.shape
+    lane = lax.broadcasted_iota(jnp.int32, (STEP, LANES), 1)
+    place = lane // DEEP
+
+    def put(rows, pick):
+        out = jnp.zeros((STEP, LANES), jnp.float32)
+        for f in range(N_OWN):
+            value = pick(f)
+            head, tail = value[:, :LANES], value[:, n_cols - LANES :]
+            if f:
+                head = pltpu.roll(head, DEEP * f, 1)
+            tail = pltpu.roll(tail, DEEP * (N_OWN + f + 1), 1)
+            out = jnp.where(place == f, head, jnp.where(place == N_OWN + f, tail, out))
+        stage[rows, :] = out
+
+    def inner(k, carry):
+        put(block(k + 1), lambda f: field_rows(plane, via, drawn, f, block(k)))
+        return carry
+
+    put(pl.ds(0, STEP), lambda f: tile_of(south, f, True))
+    lax.fori_loop(0, n_rows // STEP, inner, 0, unroll=2)
+    put(pl.ds(n_rows + STEP, STEP), lambda f: tile_of(north, f, False))
+    rest = n_rows + 2 * STEP
+    stage[rest:, :] = jnp.zeros((stage.shape[0] - rest, LANES), jnp.float32)
+    turned = stage[...].T
+    size = DEEP * N_OWN
+    first[...] = turned[:size, :]
+    last[...] = turned[size : 2 * size, :]
+
+
+def side(strip, slot, blank):
+    lane = lax.broadcasted_iota(jnp.int32, strip.shape, 1)
+    turned = pltpu.roll(strip, (LANES - DEEP - 2 * DEEP * slot) % LANES, 1)
+    return jnp.where((lane < DEEP) | (lane >= LANES - DEEP), turned, blank)
+
+
+def corner_kernel(gz, plane, via, south, north, west, east, small):
+    group = gz[0]
+    half, tall_rows = plane.shape[1] // 2, west.shape[1]
+    for f in range(N_FAR):
+        at, mine = 2 * DEEP * f, pl.ds(DEEP * f, DEEP)
+        inner = field_rows(plane, via, None, f, pl.ds(half - DEEP, DEEP))
+        small[at : at + DEEP, :] = jnp.where(group == 0, inner, south[mine, :])
+        inner = field_rows(plane, via, None, f, pl.ds(half, DEEP))
+        small[at + DEEP : at + 2 * DEEP, :] = jnp.where(group == 0, north[mine, :], inner)
+    at, size = 2 * DEEP * N_FAR, DEEP * N_FAR
+    small[at : at + size, :tall_rows] = west[:size, :]
+    small[at : at + size, tall_rows:] = east[:size, :]
+
+
+def own_kernel(gz, plane, via, drawn, south, north, west, east, near, edge_e, edge_n, near_sum, far_sum, wide, flat, tall):
+    group = gz[0]
+    n_rows, n_cols = drawn.shape
+    half = n_rows // 2
+    flat[...] = jnp.zeros(flat.shape, jnp.float32)
+    for f in range(N_OWN):
+        at = 2 * DEEP * f
+        flat[at : at + DEEP, :] = west[DEEP * f : DEEP * f + DEEP, :]
+        flat[at + DEEP : at + 2 * DEEP, :] = east[DEEP * f : DEEP * f + DEEP, :]
+    tall[...] = flat[...].T
+
+    def put(rows, pick):
+        strip = tall[rows, :]
+        for f in range(N_OWN):
+            wide[f, rows, :n_cols] = pick(f)
+            wide[f, rows, n_cols:] = side(strip, f, 1.0 if f < N_FAR else 0.0)
+
+    def inner(k, carry):
+        put(block(k + 1), lambda f: field_rows(plane, via, drawn, f, block(k)))
+        return carry
+
+    put(pl.ds(0, STEP), lambda f: tile_of(south, f, True))
+    lax.fori_loop(0, n_rows // STEP, inner, 0, unroll=2)
+    put(pl.ds(n_rows + STEP, STEP), lambda f: tile_of(north, f, False))
+    last = n_rows // STEP + 1
+
+    def around(layer, k):
+        value = wide[layer, block(k), :]
+        over = wide[layer, block(jnp.minimum(k + 1, last)), :]
+        under = wide[layer, block(jnp.maximum(k - 1, 0)), :]
+        sub = lax.broadcasted_iota(jnp.int32, value.shape, 0)
+        above = jnp.where(
+            sub == STEP - 1, pltpu.roll(over, STEP - 1, 0), pltpu.roll(value, STEP - 1, 0)
+        )
+        below = jnp.where(sub == 0, pltpu.roll(under, 1, 0), pltpu.roll(value, 1, 0))
+        to_east, to_north = harmonic(value, eastward(value)), harmonic(value, above)
+        return to_east, to_north, (to_east + westward(to_east)) + (to_north + harmonic(value, below))
+
+    def frame(k, carry):
+        at = k + group * (half // STEP)
+        for layer in range(2):
+            to_east, to_north, total = around(layer, at)
+            edge_e[layer, block(k), :] = to_east
+            edge_n[layer, block(k), :] = to_north
+            near_sum[layer, block(k), :] = total
+            near[2 + layer, block(k), :] = wide[N_FAR + layer, block(at), :]
+            near[layer, block(k), :] = wide[2 + layer, block(at), :]
+        return carry
+
+    lax.fori_loop(0, half // STEP + 2, frame, 0, unroll=2)
+
+    def other(k, carry):
+        for layer in range(2):
+            total = around(layer, k + 1 + (1 - group) * (half // STEP))[2]
+            far_sum[layer, block(k), :] = total[:, :n_cols]
+        return carry
+
+    lax.fori_loop(0, half // STEP, other, 0, unroll=2)
+
+
+def above_of(field, j, r):
+    n_rows = field.shape[1]
+    if r + STEP < n_rows:
+        return field[j, r + 1 : r + 1 + STEP, :]
+    return pltpu.roll(field[j, r : r + STEP, :], STEP - 1, 0)
+
+
+def below_of(field, j, r):
+    if r:
+        return field[j, r - 1 : r - 1 + STEP, :]
+    return pltpu.roll(field[j, r : r + STEP, :], 1, 0)
+
+
+def eastward(value):
+    return pltpu.roll(value, value.shape[1] - 1, 1)
+
+
+def westward(value):
+    return pltpu.roll(value, 1, 1)
+
+
+def fold(total):
+    width = total.shape[1]
+    while width > LANES:
+        width //= 2
+        total = total[:, :width] + total[:, width:]
+    return jnp.sum(total, axis=0, keepdims=True)
+
+
+def images(field, r, near, far, cross):
+    owns, outs = [], []
+    for j in range(4):
+        east, north = near if j < 2 else far
+        e = j % 2
+        rows = pl.ds(r, STEP)
+        own, edge = field[j, rows, :], east[e, rows, :]
+        across = edge * eastward(own) + westward(edge * own)
+        along = north[e, rows, :] * above_of(field, j, r)
+        owns.append(own)
+        outs.append(across + (along + below_of(north, e, r) * below_of(field, j, r)))
+    link = cross[pl.ds(r, STEP), :]
+    outs[0] = outs[0] + link * owns[2]
+    outs[2] = outs[2] + link * owns[0]
+    return owns, outs
+
+
+def solved(inverse, r, outs):
+    news = []
+    for q in range(2):
+        ii, oo, io = [inverse[3 * q + e, pl.ds(r, STEP), :] for e in range(3)]
+        one, two = outs[2 * q], outs[2 * q + 1]
+        news += [ii * one + io * two, io * one + oo * two]
+    return news
+
+
+def dot(left, right, n_cols):
+    pairs = [a * b for a, b in zip(left, right)]
+    return ((pairs[0] + pairs[1]) + (pairs[2] + pairs[3]))[:, :n_cols]
+
+
+def edge_kernel(gz, near, near_e, near_n, near_sum, big_plane, big_via, small, far_e, far_n, cross, inverse, step_1, n_own, inv_own, send, part, *scratch):
+    fields, step_0, flat, tall = scratch
+    group = gz[0]
+    half, n_cols = big_via.shape[1:]
+    n_rows = half + 2 * STEP
+    n_blocks = n_rows // STEP
+    tall_rows = tall.shape[0]
+    flat[...] = jnp.zeros(flat.shape, jnp.float32)
+    for f in range(N_FAR):
+        at, row = 2 * DEEP * f, 2 * DEEP * N_FAR + DEEP * f
+        flat[at : at + DEEP, :] = small[row : row + DEEP, :tall_rows]
+        flat[at + DEEP : at + 2 * DEEP, :] = small[row : row + DEEP, tall_rows:]
+    tall[...] = flat[...].T
+    for k in range(n_blocks):
+        rows = pl.ds(k * STEP, STEP)
+        strip = tall[block(k + group * (half // STEP)), :]
+        for f in range(N_FAR):
+            if 0 < k < n_blocks - 1:
+                core = (big_plane if f < 2 else big_via)[f % 2, (k - 1) * STEP : k * STEP, :]
+            else:
+                core = pltpu.roll(small[2 * DEEP * f : 2 * DEEP * f + STEP, :], DEEP, 0)
+            fields[f, rows, :n_cols] = core
+            fields[f, rows, n_cols:] = side(strip, f, 1.0)
+    total = jnp.zeros((STEP, n_cols), jnp.float32)
+    for k in range(n_blocks):
+        r = k * STEP
+        rows = pl.ds(r, STEP)
+        sums = [near_sum[0, rows, :], near_sum[1, rows, :]]
+        for layer in range(2):
+            value = fields[layer, rows, :]
+            to_east = harmonic(value, eastward(value))
+            to_north = harmonic(value, above_of(fields, layer, r))
+            far_e[layer, rows, :] = to_east
+            far_n[layer, rows, :] = to_north
+            carried = pltpu.roll(to_north, 1, 0)
+            if k:
+                sub = lax.broadcasted_iota(jnp.int32, value.shape, 0)
+                under = pltpu.roll(far_n[layer, r - STEP : r, :], 1, 0)
+                carried = jnp.where(sub == 0, under, carried)
+            sums.append((to_east + westward(to_east)) + (to_north + carried))
+        link = harmonic(near[0, rows, :], fields[2, rows, :])
+        cross[rows, :] = link
+        drawn, pads = near[2, rows, :], near[3, rows, :]
+        inner = pl.ds(r - STEP, STEP)
+        for q, up in ((0, near[1, rows, :]), (1, fields[3, rows, :])):
+            diag_i = sums[2 * q] + up + link
+            diag_o = sums[2 * q + 1] + up + jnp.where(group == 1 - q, pads, 0.0)
+            scale = 1.0 / (diag_i * diag_o - up * up)
+            found = (diag_o * scale, diag_i * scale, up * scale)
+            for e in range(3):
+                inverse[3 * q + e, rows, :] = found[e]
+                if q == 0 and 0 < k < n_blocks - 1:
+                    inv_own[e, inner, :] = found[e][:, :n_cols]
+            here = jnp.where(group == q, drawn, 0.0)
+            one, two = found[2] * here, found[1] * here
+            step_0[2 * q, rows, :], step_0[2 * q + 1, rows, :] = one, two
+            if 0 < k < n_blocks - 1:
+                total = total + (two * here)[:, :n_cols]
+    part[...] = jnp.zeros(part.shape, jnp.float32)
+    part[0:1, :] = fold(total)
+    sums = [jnp.zeros((STEP, n_cols), jnp.float32)] * 2
+    for k in range(n_blocks):
+        r = k * STEP
+        owns, outs = images(step_0, r, (near_e, near_n), (far_e, far_n), cross)
+        news = solved(inverse, r, outs)
+        for j in range(4):
+            step_1[j, pl.ds(r, STEP), :] = news[j]
+        if 0 < k < n_blocks - 1:
+            inner = pl.ds(r - STEP, STEP)
+            for layer in range(2):
+                n_own[layer, inner, :] = outs[layer][:, :n_cols]
+                send[layer, inner, :] = outs[2 + layer][:, :n_cols]
+            sums[0] = sums[0] + dot(owns, outs, n_cols)
+            sums[1] = sums[1] + dot(news, outs, n_cols)
+    part[1:2, :] = fold(sums[0])
+    part[2:3, :] = fold(sums[1])
+
+
+def steps_kernel(step_1, near_e, near_n, far_e, far_n, cross, inverse, before, n_own, send, spread, step_2):
+    n_rows = step_1.shape[1]
+    n_cols = n_own.shape[2]
+    n_blocks = n_rows // STEP
+    near, far = (near_e, near_n), (far_e, far_n)
+    sums = [jnp.zeros((STEP, n_cols), jnp.float32)] * 3
+
+    def keep(first, r, outs):
+        inner = pl.ds(r - STEP, STEP)
+        for layer in range(2):
+            n_own[first + layer, inner, :] = outs[layer][:, :n_cols]
+            send[first + layer, inner, :] = outs[2 + layer][:, :n_cols]
+
+    for k in range(n_blocks):
+        r = k * STEP
+        owns, outs = images(step_1, r, near, far, cross)
+        news = solved(inverse, r, outs)
+        for j in range(4):
+            step_2[j, pl.ds(r, STEP), :] = news[j]
+        if 0 < k < n_blocks - 1:
+            keep(0, r, outs)
+            sums[0] = sums[0] + dot(owns, outs, n_cols)
+            sums[1] = sums[1] + dot(news, outs, n_cols)
+    for k in range(1, n_blocks - 1):
+        r = k * STEP
+        owns, outs = images(step_2, r, near, far, cross)
+        keep(2, r, outs)
+        sums[2] = sums[2] + dot(owns, outs, n_cols)
+    row = lax.broadcasted_iota(jnp.int32, before.shape, 0)
+    part = before[...]
+    for j in range(3):
+        part = jnp.where(row == 3 + j, fold(sums[j]), part)
+    for k in range(spread.shape[0]):
+        spread[k] = part
+
+
+def inverse_kernel(gz, plane, via, sums, given, inverse):
+    group = gz[0]
+    half = inverse.shape[1]
+
+    def fill(k, carry):
+        rows, at = block(k), block(k + (1 - group) * (half // STEP))
+        up = via[1, at, :]
+        diag_i = sums[0, rows, :] + up + harmonic(via[0, at, :], given[rows, :])
+        diag_o = sums[1, rows, :] + up + jnp.where(group == 1, plane[2, at, :], 0.0)
+        scale = 1.0 / (diag_i * diag_o - up * up)
+        inverse[0, rows, :] = diag_o * scale
+        inverse[1, rows, :] = diag_i * scale
+        inverse[2, rows, :] = up * scale
+        return carry
+
+    lax.fori_loop(0, half // STEP, fill, 0, unroll=2)
+
+
+def tree(parts):
+    values = [parts[k] for k in range(parts.shape[0])]
+    while len(values) > 1:
+        values = [a + b for a, b in zip(values[::2], values[1::2])]
+    return values[0]
+
+
+def relay_kernel(parts, spread):
+    total = tree(parts)
+    for k in range(spread.shape[0]):
+        spread[k] = total
+
+
+def solve_kernel(parts, coefs, flag):
+    sums = jnp.sum(tree(parts), axis=1, keepdims=True)
+    g = [jnp.broadcast_to(sums[k : k + 1, :], (1, LANES)) for k in range(6)]
+    step = [g[k] - g[k + 1] for k in range(5)]
+    scale = [lax.rsqrt(g[0]), lax.rsqrt(g[2]), lax.rsqrt(g[4])]
+
+    def entry(i, j):
+        return step[i + j] * scale[i] * scale[j]
+
+    d0 = entry(0, 0)
+    l10, l20 = entry(1, 0) / d0, entry(2, 0) / d0
+    d1 = entry(1, 1) - l10 * entry(1, 0)
+    e21 = entry(2, 1) - l20 * entry(1, 0)
+    l21 = e21 / d1
+    d2 = entry(2, 2) - l20 * entry(2, 0) - l21 * e21
+    y0 = g[0] * scale[0]
+    y1 = g[1] * scale[1] - l10 * y0
+    y2 = g[2] * scale[2] - l20 * y0 - l21 * y1
+    x2 = y2 / d2
+    x1 = y1 / d1 - l21 * x2
+    x0 = y0 / d0 - l10 * x1 - l20 * x2
+    c0, c1, c2 = x0 * scale[0], x1 * scale[1], x2 * scale[2]
+    for k, value in enumerate((c0, c1, c2, 1.0 - c0, c0 - c1, c1 - c2)):
+        coefs[k : k + 1, :] = value
+    coefs[6:8, :] = jnp.zeros((2, LANES), jnp.float32)
+    good = (d0 > GUARD) & (d1 > GUARD) & (d2 > GUARD)
+    flag[...] = jnp.where(good, 1, 0)
+
+
+def combine_kernel(gz, coefs, current, inv_near, inv_far, n_0, n_0_far, n_12, n_12_far, volts, left):
+    group = gz[0]
+    half, n_cols = n_0.shape[1:]
+    c = [jnp.broadcast_to(coefs[k : k + 1, 0:1], (STEP, n_cols)) for k in range(6)]
+
+    def fill(near, inv, first, second):
+        start = (group if near else 1 - group) * (half // STEP)
+
+        def body(k, carry):
+            rows, at = block(k), block(k + start)
+            drawn = jnp.where(group == 0, current[at, :], 0.0)
+            n0i, n0o = first[0, rows, :], first[1, rows, :]
+            n1i, n1o, n2i, n2o = [second[j, rows, :] for j in range(4)]
+            ii, oo, io = [inv[e, rows, :] for e in range(3)]
+            one = c[1] * n0i + c[2] * n1i
+            two = c[0] * drawn + (c[1] * n0o + c[2] * n1o)
+            volts[1 - group, at, :] = ii * one + io * two
+            volts[group, at, :] = io * one + oo * two
+            left[1 - group, at, :] = c[4] * n0i + c[5] * n1i + c[2] * n2i
+            left[group, at, :] = c[3] * drawn + c[4] * n0o + c[5] * n1o + c[2] * n2o
+            return carry
+
+        lax.fori_loop(0, half // STEP, body, 0, unroll=2)
+
+    fill(True, inv_near, n_0, n_12)
+    fill(False, inv_far, n_0_far, n_12_far)
+
+
+def call(kernel, outs, scratch, n_smem, *args):
+    return pallas(kernel, outs, scratch, n_smem, args)
+
+
+def pallas(kernel, outs, scratch, n_smem, args):
+    return pl.pallas_call(
+        kernel,
+        in_specs=[SMEM] * n_smem + [VMEM] * (len(args) - n_smem),
+        out_specs=[VMEM] * len(outs),
+        out_shape=outs,
+        scratch_shapes=scratch,
+        compiler_params=pltpu.CompilerParams(vmem_limit_bytes=GRANT),
+    )(*args)
+
+
+def shards(load_current, sink_mask, pad_mask, plane_class, via_class, plane_table, via_table):
+    _, n_rows, n_cols = plane_class.shape
+    half, frame = n_rows // 2, n_rows // 2 + 2 * STEP
+    tall = -(-(n_rows + 2 * STEP) // LANES) * LANES
+    broad = n_cols + LANES
+
+    def array(*shape):
+        return jax.ShapeDtypeStruct(shape, jnp.float32)
+
+    def ring(axis):
+        size = lax.axis_size(axis)
+        return [(i, (i + 1) % size) for i in range(size)]
+
+    def back(pairs):
+        return [(b, a) for a, b in pairs]
+
+    turn = [pltpu.VMEM((LANES, tall), jnp.float32), pltpu.VMEM((tall, LANES), jnp.float32)]
+    gz = lax.axis_index("gz").reshape(1).astype(jnp.int32)
+    swap = [(0, 1), (1, 0)]
+    rest = ("gy_0", "gy_1", "gz")
+    n_gx, n_rest = lax.axis_size(GX), lax.axis_size(rest)
+
+    via, pair, via_send = call(
+        via_kernel,
+        [array(2, n_rows, n_cols), array(2, half, n_cols), array(half, n_cols)],
+        [], 2, gz, via_table, via_class,
+    )
+    big_via = lax.ppermute(pair, "gz", swap)
+    plane, drawn, pair, top, bottom = call(
+        plane_kernel,
+        [array(3, n_rows, n_cols), array(n_rows, n_cols), array(2, half, n_cols)]
+        + [array(DEEP * N_OWN, n_cols)] * 2,
+        [], 2, gz, plane_table, plane_class, load_current, sink_mask, pad_mask, via,
+    )
+    south = lax.ppermute(bottom, GY, ring(GY))
+    north = lax.ppermute(top, GY, back(ring(GY)))
+    big_plane = lax.ppermute(pair, "gz", swap)
+    first, last = call(
+        columns_kernel, [array(DEEP * N_OWN, tall)] * 2, turn[1:], 0,
+        plane, via, drawn, south, north,
+    )
+    west = lax.ppermute(last, GX, ring(GX))
+    east = lax.ppermute(first, GX, back(ring(GX)))
+    (small_send,) = call(
+        corner_kernel, [array(N_FAR * 3 * DEEP, n_cols)], [], 1,
+        gz, plane, via, south, north, west, east,
+    )
+    small = lax.ppermute(small_send, "gz", swap)
+    via_far = lax.ppermute(via_send, "gz", swap)
+    near, near_e, near_n, near_sum, far_sum = call(
+        own_kernel,
+        [array(4, frame, broad)] + [array(2, frame, broad)] * 3 + [array(2, half, n_cols)],
+        [pltpu.VMEM((N_OWN, n_rows + 2 * STEP, broad), jnp.float32)] + turn,
+        1, gz, plane, via, drawn, south, north, west, east,
+    )
+    far_e, far_n, cross, inverse, step_1, n_0, inv_near, send, part = call(
+        edge_kernel,
+        [array(2, frame, broad)] * 2
+        + [array(frame, broad), array(6, frame, broad), array(4, frame, broad),
+           array(2, half, n_cols), array(3, half, n_cols), array(2, half, n_cols), array(STEP, LANES)],
+        [pltpu.VMEM((N_FAR, frame, broad), jnp.float32), pltpu.VMEM((4, frame, broad), jnp.float32)]
+        + turn,
+        1, gz, near, near_e, near_n, near_sum, big_plane, big_via, small,
+    )
+    n_0_far = lax.ppermute(send, "gz", swap)
+    (inv_far,) = call(
+        inverse_kernel, [array(3, half, n_cols)], [], 1,
+        gz, plane, via, far_sum, via_far,
+    )
+    n_12, send, spread = call(
+        steps_kernel,
+        [array(4, half, n_cols), array(4, half, n_cols), array(n_gx, STEP, LANES)],
+        [pltpu.VMEM((4, frame, broad), jnp.float32)],
+        0, step_1, near_e, near_n, far_e, far_n, cross, inverse, part,
+    )
+    n_12_far = lax.ppermute(send, "gz", swap)
+    parts = lax.all_to_all(spread, GX, 0, 0, tiled=True)
+    (spread,) = call(relay_kernel, [array(n_rest, STEP, LANES)], [], 0, parts)
+    parts = lax.all_to_all(spread, rest, 0, 0, tiled=True)
+    coefs, flag = call(
+        solve_kernel,
+        [array(STEP, LANES), jax.ShapeDtypeStruct((1, LANES), jnp.int32)], [], 0, parts,
+    )
+    quick = call(
+        combine_kernel, [array(2, n_rows, n_cols)] * 2, [], 1,
+        gz, coefs, drawn, inv_near, inv_far, n_0, n_0_far, n_12, n_12_far,
+    )
+
+    def careful():
+        return recurrence(
+            load_current, sink_mask, pad_mask, plane_class, via_class, plane_table, via_table
+        )
+
+    return lax.cond(flag[0, 0] == 1, lambda: tuple(quick), careful)
+
+
 def solution(mesh):
     split = Mesh(
         mesh.devices.reshape(8, 2, 2, 4, mesh.shape["gz"]), ("gx_0", "gx_1", "gy_0", "gy_1", "gz")

time: 247 us -> 89.2 us (0.36); the launches traced: 243 us -> 87.9 us
  blocking collectives: 118 us -> 16.6 us
  starting transfers between devices: 67.4 us -> 18.1 us
  other arithmetic: 23.9 us -> 0 us
  Pallas kernels: 0 us -> 20.3 us
  between operations: 10.7 us -> 1 us
  waiting for transfers between devices: 17.5 us -> 25.5 us
    psum x15 -> x0, blocking collectives: 118 us -> none  [by_axis(): array = lax.psum(array, axis)]
    ppermute x24 -> x10, starting transfers between devices: 67.4 us -> 13.9 us  [the longest x1 3.9 us: shards(): north = lax.ppermute(top, GY, back(ring(GY)))]
    pallas_call x0 -> x11, Pallas kernels: none -> 20.3 us  [pallas(): pl.pallas_call(kernel, in_specs=[SMEM] * n_smem + [VMEM] * (len(args) - n...]
    all_to_all x0 -> x1, blocking collectives: none -> 16.6 us  [shards(): parts = lax.all_to_all(spread, GX, 0, 0, tiled=True)]
    reduce_sum x3 -> x0, other arithmetic: 9.43 us -> none  [merged_sums(): jnp.sum(image_field * precond)]
    ppermute x24 -> x10, waiting for transfers between devices: 17.5 us -> 25.5 us  [the longest x1 15.2 us: shards(): south = lax.ppermute(bottom, GY, ring(GY))]
    sub x5 -> x0, other arithmetic: 7.83 us -> none  [the longest x3 7.35 us: shards(): residual = residual - step_size * image_dir]
    unnamed x48 -> x22, local copies, waits for them, and re-layouts: 1.78 us -> 6.37 us
  transfers between devices with their start and end apart: 24 -> 11, of which waited for: 8 -> 4; matrix products, arithmetic and copies ran while one was open for 2% -> 0% of each run, Pallas kernels for 0% -> 10%
where the time goes in v3:
time: 89.2 us; the launch traced here: 87.9 us
  waiting for transfers between devices  25.5 us (29%)
  Pallas kernels  20.3 us (23%)
  starting transfers between devices  18.1 us (20%)
  blocking collectives  16.6 us (19%)
  local copies, waits for them, and re-layouts  6.37 us (7%)
  between operations  1 us (1%)
    pallas_call x11, Pallas kernels, pallas(): pl.pallas_call(kernel, in_specs=[SMEM] * n_smem + [VMEM] * (len(args) - n...  20.3 us
    all_to_all x1, blocking collectives, shards(): parts = lax.all_to_all(spread, GX, 0, 0, tiled=True)  16.6 us
    ppermute x1, waiting for transfers between devices, shards(): south = lax.ppermute(bottom, GY, ring(GY))  15.2 us
    ppermute x1, waiting for transfers between devices, shards(): via_far = lax.ppermute(via_send, 'gz', swap)  6.76 us
    unnamed x22, local copies, waits for them, and re-layouts  6.37 us
    all_to_all x1, starting transfers between devices, shards(): parts = lax.all_to_all(spread, rest, 0, 0, tiled=True)  4.15 us
    ppermute x1, starting transfers between devices, shards(): north = lax.ppermute(top, GY, back(ring(GY)))  3.9 us
    ppermute x1, starting transfers between devices, shards(): west = lax.ppermute(last, GX, ring(GX))  3.36 us
  transfers between devices with their start and end apart: 11, of which 4 were waited for; matrix products, arithmetic and copies ran while one was open for 0% of the time, Pallas kernels for 10%

profile of v3, /device:TPU:1, one launch (start us, length us, event | category | flops | bytes accessed | tf_op | source)
XLA Modules:
  0.0 87.9 jit_solution(7752286927447855342)
XLA Ops:
  0.6 2.6 %shard_map.90 = (f32[2,192,512]{2,1,0:T(8,128)S(1)}, f32[2,96,512]{2,1,0:T(8,128)S(1)}, f32[96,512]{1,0:T(8,128)}) custom-call(s32[1]{0:T(128)} %bitcast.23.gz, f32[2,8]{1,0:T(2,128)} %table.2, s32[2,192,512]{2,1,0:T(8,128)} %classes.2), custom_call_target="tpu_custom_call" | custom-call | tf_op jit(solution)/shard_map/pallas_call | solution.py:650
  3.2 2.0 %collective-permute-start.29 = (f32[2,96,512]{2,1,0:T(8,128)S(1)}, f32[2,96,512]{2,1,0:T(8,128)S(1)}, u32[]{:S(2)}, u32[]{:S(2)}) collective-permute-start(f32[2,96,512]{2,1,0:T(8,128)S(1)} %get-tuple-element.68), channel_id=1, source_target_pairs={{0,1},{1,0},{2,3},{3,2},{4,5},{5,4},{6,7},{7,6},{8,9},{9,8},{10,11... | collective-permute-start | bytes 1179656 | tf_op jit(solution)/shard_map/ppermute | solution.py:687
  5.3 1.9 %shard_map.91 = (f32[3,192,512]{2,1,0:T(8,128)S(1)}, f32[192,512]{1,0:T(8,128)S(1)}, f32[2,96,512]{2,1,0:T(8,128)S(1)}, f32[24,512]{1,0:T(8,128)S(1)}, f32[24,512]{1,0:T(8,128)S(1)}) custom-call(s32[1]{0:T(128)} %bitcast.23.gz, f32[2,8]{1,0:T(2,128)} %table.3, s32[2,192,512]{2,1,0:T(8,128)S(1)} %copy-done.27, f32[192,512]{1,0:T(8,128)} %load.1, ...), custom_call_target="tpu_custom_call" | custom-call | tf_op jit(solution)/shard_map/pallas_call | solution.py:650
  7.3 1.5 %collective-permute-start.24 = (f32[24,512]{1,0:T(8,128)S(1)}, f32[24,512]{1,0:T(8,128)S(1)}, u32[]{:S(2)}, u32[]{:S(2)}) collective-permute-start(f32[24,512]{1,0:T(8,128)S(1)} %get-tuple-element.59), channel_id=1, source_target_pairs={{0,2},{2,4},{4,6},{6,8},{8,10},{10,12},{12,14},{14,0},{1,3},{3,5},... | collective-permute-start | bytes 147464 | tf_op jit(solution)/shard_map/ppermute | solution.py:694
  8.8 3.9 %collective-permute-start.25 = (f32[24,512]{1,0:T(8,128)S(1)}, f32[24,512]{1,0:T(8,128)S(1)}, u32[]{:S(2)}, u32[]{:S(2)}) collective-permute-start(f32[24,512]{1,0:T(8,128)S(1)} %get-tuple-element.60), channel_id=1, source_target_pairs={{2,0},{4,2},{6,4},{8,6},{10,8},{12,10},{14,12},{0,14},{3,1},{5,3},... | collective-permute-start | bytes 147464 | tf_op jit(solution)/shard_map/ppermute | solution.py:695
  12.7 15.2 %collective-permute-done.24.south = f32[24,512]{1,0:T(8,128)S(1)} collective-permute-done((f32[24,512]{1,0:T(8,128)S(1)}, f32[24,512]{1,0:T(8,128)S(1)}, u32[]{:S(2)}, u32[]{:S(2)}) %collective-permute-start.24) | collective-permute-done | bytes 49184 | tf_op jit(solution)/shard_map/ppermute | solution.py:694
  27.9 1.2 %shard_map.92 = (f32[24,256]{1,0:T(8,128)S(1)}, f32[24,256]{1,0:T(8,128)S(1)}) custom-call(f32[3,192,512]{2,1,0:T(8,128)S(1)} %get-tuple-element.57.plane, f32[2,192,512]{2,1,0:T(8,128)S(1)} %get-tuple-element.56.via, f32[192,512]{1,0:T(8,128)S(1)} %get-tuple-element.58.drawn.current, f32[24,512]{1,0:T(8,128)S(1)} %collective-permute-done.24.south, ...), custom_call_target="tpu_custom_call" | custom-call | tf_op jit(solution)/shard_map/pallas_call | solution.py:650
  29.1 3.4 %collective-permute-start.26 = (f32[24,256]{1,0:T(8,128)S(1)}, f32[24,256]{1,0:T(8,128)S(1)}, u32[]{:S(2)}, u32[]{:S(2)}) collective-permute-start(f32[24,256]{1,0:T(8,128)S(1)} %get-tuple-element.61), channel_id=1, source_target_pairs={{0,16},{16,32},{32,48},{48,64},{64,80},{80,96},{96,112},{112,128},... | collective-permute-start | bytes 73736 | tf_op jit(solution)/shard_map/ppermute | solution.py:701
  32.5 0.9 %collective-permute-done.26.west = f32[24,256]{1,0:T(8,128)S(1)} collective-permute-done((f32[24,256]{1,0:T(8,128)S(1)}, f32[24,256]{1,0:T(8,128)S(1)}, u32[]{:S(2)}, u32[]{:S(2)}) %collective-permute-start.26) | collective-permute-done | bytes 24608 | tf_op jit(solution)/shard_map/ppermute | solution.py:701
  33.4 2.6 %collective-permute-done.27.east = f32[24,256]{1,0:T(8,128)S(1)} collective-permute-done((f32[24,256]{1,0:T(8,128)S(1)}, f32[24,256]{1,0:T(8,128)S(1)}, u32[]{:S(2)}, u32[]{:S(2)}) %collective-permute-start.27) | collective-permute-done | bytes 24608 | tf_op jit(solution)/shard_map/ppermute | solution.py:702
  36.2 3.4 %shard_map.93 = (f32[4,112,640]{2,1,0:T(8,128)S(1)}, f32[2,112,640]{2,1,0:T(8,128)S(1)}, f32[2,112,640]{2,1,0:T(8,128)S(1)}, f32[2,112,640]{2,1,0:T(8,128)S(1)}, f32[2,96,512]{2,1,0:T(8,128)S(1)}) custom-call(s32[1]{0:T(128)} %bitcast.23.gz, f32[3,192,512]{2,1,0:T(8,128)S(1)} %get-tuple-element.57.plane, f32[2,192,512]{2,1,0:T(8,128)S(1)} %get-tuple-element.56.via, ...), custom_call_target="tpu_custom_call" | custom-call | tf_op jit(solution)/shard_map/pallas_call | solution.py:650
  40.4 4.1 %shard_map.95 = (f32[2,112,640]{2,1,0:T(8,128)S(1)}, f32[2,112,640]{2,1,0:T(8,128)S(1)}, f32[112,640]{1,0:T(8,128)S(1)}, f32[6,112,640]{2,1,0:T(8,128)S(1)}, f32...) custom-call(s32[1]{0:T(128)} %bitcast.23.gz, ...), custom_call_target="tpu_custom_call" | custom-call | tf_op jit(solution)/shard_map/pallas_call | solution.py:650
  44.5 2.3 %shard_map.96 = (f32[4,96,512]{2,1,0:T(8,128)S(1)}, f32[4,96,512]{2,1,0:T(8,128)}, f32[16,8,128]{2,1,0:T(8,128)S(1)}) custom-call(f32[4,112,640]{2,1,0:T(8,128)S(1)} %get-tuple-element.69.step_1, f32[2,112,640]{2,1,0:T(8,128)S(1)} %get-tuple-element.64.near_e, f32[2,112,640]{2,1,0:T(8,128)S(1)} %get-tuple-element.65.near_n, ...), custom_call_target="tpu_custom_call" | custom-call | tf_op jit(solution)/shard_map/pallas_call | solution.py:650
  47.7 1.4 %collective-permute-start.33 = (f32[4,96,512]{2,1,0:T(8,128)}, f32[4,96,512]{2,1,0:T(8,128)}, u32[]{:S(2)}, u32[]{:S(2)}) collective-permute-start(f32[4,96,512]{2,1,0:T(8,128)} %get-tuple-element.84), channel_id=1, source_target_pairs={{0,1},{1,0},{2,3},{3,2},{4,5},{5,4},{6,7},{7,6},{8,9},{9,8},{10,11... | collective-permute-start | bytes 2359304 | tf_op jit(solution)/shard_map/ppermute | solution.py:735
  49.1 1.4 %collective-permute-start.31 = (f32[96,512]{1,0:T(8,128)}, f32[96,512]{1,0:T(8,128)S(1)}, u32[]{:S(2)}, u32[]{:S(2)}) collective-permute-start(f32[96,512]{1,0:T(8,128)} %get-tuple-element.80), channel_id=1, source_target_pairs={{0,1},{1,0},{2,3},{3,2},{4,5},{5,4},{6,7},{7,6},{8,9},{9,8},{10,11... | collective-permute-start | bytes 589832 | tf_op jit(solution)/shard_map/ppermute | solution.py:708
  50.6 16.6 %all_to_all.10.parts = f32[16,8,128]{2,1,0:T(8,128)S(1)} all-to-all(f32[16,8,128]{2,1,0:T(8,128)S(1)} %get-tuple-element.75), channel_id=1, replica_groups=mesh['gx_0'=8,'gx_1'=2,'gy_0'=2,'gy_1'=4,'gz'=2] {'gx_0','gx_1'}, dimensions={0} | all-to-all | bytes 131072 | tf_op jit(solution)/shard_map/all_to_all | solution.py:736
  67.8 4.1 %all-to-all-start.1 = ((f32[16,8,128]{2,1,0:T(8,128)}), f32[16,8,128]{2,1,0:T(8,128)}, u32[]{:S(2)}, u32[]{:S(2)}) async-start(f32[16,8,128]{2,1,0:T(8,128)} %shard_map.97), calls=%async_computation.1 | async-start | bytes 131072 | tf_op jit(solution)/shard_map/all_to_all | solution.py:738
  71.9 6.8 %collective-permute-done.31.given = f32[96,512]{1,0:T(8,128)S(1)} collective-permute-done((f32[96,512]{1,0:T(8,128)}, f32[96,512]{1,0:T(8,128)S(1)}, u32[]{:S(2)}, u32[]{:S(2)}) %collective-permute-start.31) | collective-permute-done | bytes 196640 | tf_op jit(solution)/shard_map/ppermute | solution.py:708
  79.4 1.0 %copy-done.5 = f32[2,96,512]{2,1,0:T(8,128)S(1)} copy-done((f32[2,96,512]{2,1,0:T(8,128)S(1)}, f32[2,96,512]{2,1,0:T(8,128)}, u32[]{:S(2)}) %copy-start.5) | copy-done | bytes 393240
  80.4 0.9 %copy-done.7 = f32[96,512]{1,0:T(8,128)S(1)} copy-done((f32[96,512]{1,0:T(8,128)S(1)}, f32[96,512]{1,0:T(8,128)}, u32[]{:S(2)}) %copy-start.7) | copy-done | bytes 196632
  81.5 1.0 %shard_map.98 = (f32[8,128]{1,0:T(8,128)S(1)}, s32[1,128]{1,0:T(1,128)S(1)}) custom-call(f32[16,8,128]{2,1,0:T(8,128)} %all-to-all-done.1.parts), custom_call_target="tpu_custom_call" | custom-call | tf_op jit(solution)/shard_map/pallas_call | solution.py:650
  82.5 1.1 %copy-done.1 = f32[4,96,512]{2,1,0:T(8,128)S(1)} copy-done((f32[4,96,512]{2,1,0:T(8,128)S(1)}, f32[4,96,512]{2,1,0:T(8,128)}, u32[]{:S(2)}) %copy-start.1) | copy-done | bytes 786456
  83.7 1.0 %copy-done.3 = f32[2,96,512]{2,1,0:T(8,128)S(1)} copy-done((f32[2,96,512]{2,1,0:T(8,128)S(1)}, f32[2,96,512]{2,1,0:T(8,128)}, u32[]{:S(2)}) %copy-start.3) | copy-done | bytes 393240
  84.7 2.9 %shard_map.100 = (f32[2,192,512]{2,1,0:T(8,128)}, f32[2,192,512]{2,1,0:T(8,128)}) custom-call(s32[1]{0:T(128)} %bitcast.23.gz, f32[8,128]{1,0:T(8,128)S(1)} %get-tuple-element.77.coefs, f32[192,512]{1,0:T(8,128)S(1)} %get-tuple-element.58.drawn.current, f32[3,96,512]{2,1,0:T(8,128)S(1)} %get-tuple-element.78.inv_near, f32[3,96,512]{2,1,0:T(8,128)S(1)} %shard_map.99.inv_far, ...), custom_call_target="tpu_custom_call" | custom-call | tf_op jit(solution)/shard_map/pallas_call | solution.py:650
  (33 shorter events, 3.5 us)
Async XLA Ops:
  0.6 4.6 %copy-start.27 = (s32[2,192,512]{2,1,0:T(8,128)S(1)}, s32[2,192,512]{2,1,0:T(8,128)}, u32[]{:S(2)}) copy-start(s32[2,192,512]{2,1,0:T(8,128)} %classes.3) | copy-start | bytes 2359300
  3.2 37.1 %collective-permute-start.29 = (f32[2,96,512]{2,1,0:T(8,128)S(1)}, f32[2,96,512]{2,1,0:T(8,128)S(1)}, u32[]{:S(2)}, u32[]{:S(2)}) collective-permute-start(f32[2,96,512]{2,1,0:T(8,128)S(1)} %get-tuple-element.68), channel_id=1, source_target_pairs={{0,1},{1,0},{2,3},{3,2},{4,5},{5,4},{6,7},{7,6},{8,9},{9,8},{10,11... | collective-permute-start | bytes 1179656 | tf_op jit(solution)/shard_map/ppermute | solution.py:687
  7.2 33.2 %collective-permute-start.28 = (f32[2,96,512]{2,1,0:T(8,128)S(1)}, f32[2,96,512]{2,1,0:T(8,128)S(1)}, u32[]{:S(2)}, u32[]{:S(2)}) collective-permute-start(f32[2,96,512]{2,1,0:T(8,128)S(1)} %get-tuple-element.67), channel_id=1, source_target_pairs={{0,1},{1,0},{2,3},{3,2},{4,5},{5,4},{6,7},{7,6},{8,9},{9,8},{10,11... | collective-permute-start | bytes 1179656 | tf_op jit(solution)/shard_map/ppermute | solution.py:696
  7.3 20.6 %collective-permute-start.24 = (f32[24,512]{1,0:T(8,128)S(1)}, f32[24,512]{1,0:T(8,128)S(1)}, u32[]{:S(2)}, u32[]{:S(2)}) collective-permute-start(f32[24,512]{1,0:T(8,128)S(1)} %get-tuple-element.59), channel_id=1, source_target_pairs={{0,2},{2,4},{4,6},{6,8},{8,10},{10,12},{12,14},{14,0},{1,3},{3,5},... | collective-permute-start | bytes 147464 | tf_op jit(solution)/shard_map/ppermute | solution.py:694
  8.8 19.1 %collective-permute-start.25 = (f32[24,512]{1,0:T(8,128)S(1)}, f32[24,512]{1,0:T(8,128)S(1)}, u32[]{:S(2)}, u32[]{:S(2)}) collective-permute-start(f32[24,512]{1,0:T(8,128)S(1)} %get-tuple-element.60), channel_id=1, source_target_pairs={{2,0},{4,2},{6,4},{8,6},{10,8},{12,10},{14,12},{0,14},{3,1},{5,3},... | collective-permute-start | bytes 147464 | tf_op jit(solution)/shard_map/ppermute | solution.py:695
  29.1 4.3 %collective-permute-start.26 = (f32[24,256]{1,0:T(8,128)S(1)}, f32[24,256]{1,0:T(8,128)S(1)}, u32[]{:S(2)}, u32[]{:S(2)}) collective-permute-start(f32[24,256]{1,0:T(8,128)S(1)} %get-tuple-element.61), channel_id=1, source_target_pairs={{0,16},{16,32},{32,48},{48,64},{64,80},{80,96},{96,112},{112,128},... | collective-permute-start | bytes 73736 | tf_op jit(solution)/shard_map/ppermute | solution.py:701
  32.5 3.5 %collective-permute-start.27 = (f32[24,256]{1,0:T(8,128)S(1)}, f32[24,256]{1,0:T(8,128)S(1)}, u32[]{:S(2)}, u32[]{:S(2)}) collective-permute-start(f32[24,256]{1,0:T(8,128)S(1)} %get-tuple-element.62), channel_id=1, source_target_pairs={{16,0},{32,16},{48,32},{64,48},{80,64},{96,80},{112,96},{128,112},... | collective-permute-start | bytes 73736 | tf_op jit(solution)/shard_map/ppermute | solution.py:702
  36.1 4.3 %collective-permute-start.30 = (f32[48,512]{1,0:T(8,128)S(1)}, f32[48,512]{1,0:T(8,128)S(1)}, u32[]{:S(2)}, u32[]{:S(2)}) collective-permute-start(f32[48,512]{1,0:T(8,128)S(1)} %shard_map.94), channel_id=1, source_target_pairs={{0,1},{1,0},{2,3},{3,2},{4,5},{5,4},{6,7},{7,6},{8,9},{9,8},{10,11... | collective-permute-start | bytes 294920 | tf_op jit(solution)/shard_map/ppermute | solution.py:707
  39.6 0.8 copy-start.4
  44.5 2.3 %copy-start.2 = (f32[2,96,512]{2,1,0:T(8,128)}, f32[2,96,512]{2,1,0:T(8,128)S(1)}, u32[]{:S(2)}) copy-start(f32[2,96,512]{2,1,0:T(8,128)S(1)} %get-tuple-element.81.n_0) | copy-start | bytes 1179652
  46.8 0.9 %copy-start = (f32[4,96,512]{2,1,0:T(8,128)}, f32[4,96,512]{2,1,0:T(8,128)S(1)}, u32[]{:S(2)}) copy-start(f32[4,96,512]{2,1,0:T(8,128)S(1)} %get-tuple-element.83.n_12) | copy-start | bytes 2359300
  47.7 34.9 %collective-permute-start.33 = (f32[4,96,512]{2,1,0:T(8,128)}, f32[4,96,512]{2,1,0:T(8,128)}, u32[]{:S(2)}, u32[]{:S(2)}) collective-permute-start(f32[4,96,512]{2,1,0:T(8,128)} %get-tuple-element.84), channel_id=1, source_target_pairs={{0,1},{1,0},{2,3},{3,2},{4,5},{5,4},{6,7},{7,6},{8,9},{9,8},{10,11... | collective-permute-start | bytes 2359304 | tf_op jit(solution)/shard_map/ppermute | solution.py:735
  49.1 33.4 %collective-permute-start.32 = (f32[2,96,512]{2,1,0:T(8,128)}, f32[2,96,512]{2,1,0:T(8,128)}, u32[]{:S(2)}, u32[]{:S(2)}) collective-permute-start(f32[2,96,512]{2,1,0:T(8,128)} %get-tuple-element.82), channel_id=1, source_target_pairs={{0,1},{1,0},{2,3},{3,2},{4,5},{5,4},{6,7},{7,6},{8,9},{9,8},{10,11... | collective-permute-start | bytes 1179656 | tf_op jit(solution)/shard_map/ppermute | solution.py:724
  49.1 29.6 %collective-permute-start.31 = (f32[96,512]{1,0:T(8,128)}, f32[96,512]{1,0:T(8,128)S(1)}, u32[]{:S(2)}, u32[]{:S(2)}) collective-permute-start(f32[96,512]{1,0:T(8,128)} %get-tuple-element.80), channel_id=1, source_target_pairs={{0,1},{1,0},{2,3},{3,2},{4,5},{5,4},{6,7},{7,6},{8,9},{9,8},{10,11... | collective-permute-start | bytes 589832 | tf_op jit(solution)/shard_map/ppermute | solution.py:708
  67.8 13.7 %all-to-all-start.1 = ((f32[16,8,128]{2,1,0:T(8,128)}), f32[16,8,128]{2,1,0:T(8,128)}, u32[]{:S(2)}, u32[]{:S(2)}) async-start(f32[16,8,128]{2,1,0:T(8,128)} %shard_map.97), calls=%async_computation.1 | async-start | bytes 131072 | tf_op jit(solution)/shard_map/all_to_all | solution.py:738
  78.7 0.7 copy-start.6
  79.4 1.0 %copy-start.5 = (f32[2,96,512]{2,1,0:T(8,128)S(1)}, f32[2,96,512]{2,1,0:T(8,128)}, u32[]{:S(2)}) copy-start(f32[2,96,512]{2,1,0:T(8,128)} %copy-done.4) | copy-start | bytes 1179652
  80.4 0.9 %copy-start.7 = (f32[96,512]{1,0:T(8,128)S(1)}, f32[96,512]{1,0:T(8,128)}, u32[]{:S(2)}) copy-start(f32[96,512]{1,0:T(8,128)} %copy-done.6) | copy-start | bytes 589828
  82.5 1.1 %copy-start.1 = (f32[4,96,512]{2,1,0:T(8,128)S(1)}, f32[4,96,512]{2,1,0:T(8,128)}, u32[]{:S(2)}) copy-start(f32[4,96,512]{2,1,0:T(8,128)} %copy-done) | copy-start | bytes 2359300
  83.7 1.0 %copy-start.3 = (f32[2,96,512]{2,1,0:T(8,128)S(1)}, f32[2,96,512]{2,1,0:T(8,128)}, u32[]{:S(2)}) copy-start(f32[2,96,512]{2,1,0:T(8,128)} %copy-done.2) | copy-start | bytes 1179652
  84.7 2.9 %copy-start.33 = (f32[2,8]{1,0:T(2,128)S(1)}, f32[2,8]{1,0:T(2,128)}, u32[]{:S(2)}) copy-start(f32[2,8]{1,0:T(2,128)} %table.3) | copy-start | bytes 196
  84.7 2.9 %copy-start.34 = (f32[2,8]{1,0:T(2,128)S(1)}, f32[2,8]{1,0:T(2,128)}, u32[]{:S(2)}) copy-start(f32[2,8]{1,0:T(2,128)} %table.2) | copy-start | bytes 196

commit v4 on v3

--- a/solution.py
+++ b/solution.py
@@ -189,34 +189,46 @@
 N_FAR = 4
 VMEM = pl.BlockSpec(memory_space=pltpu.VMEM)
 SMEM = pl.BlockSpec(memory_space=pltpu.SMEM)
+OUTSIDE = pl.BlockSpec(memory_space=pl.ANY)
 
 
 def block(k):
     return pl.ds(pl.multiple_of(k * STEP, STEP), STEP)
 
 
-def select_class(classes, entry):
+def mean(first, second):
+    return 1.0 / (first + second)
+
+
+def half_reciprocals(table, layer, n_cols):
+    row = 0.5 / table[pl.ds(layer, 1), :]
+    return [jnp.broadcast_to(row[:, e : e + 1], (STEP, n_cols)) for e in range(row.shape[1])]
+
+
+def look_up(entries, classes):
     low = (classes & 1) != 0
     mid = (classes & 2) != 0
-    high = (classes & 4) != 0
-    pairs = [jnp.where(low, entry(2 * k + 1), entry(2 * k)) for k in range(4)]
-    return jnp.where(high, jnp.where(mid, pairs[3], pairs[2]), jnp.where(mid, pairs[1], pairs[0]))
+    pairs = [jnp.where(low, entries[2 * k + 1], entries[2 * k]) for k in range(4)]
+    return jnp.where(
+        classes > 3, jnp.where(mid, pairs[3], pairs[2]), jnp.where(mid, pairs[1], pairs[0])
+    )
 
 
 def via_kernel(gz, table, classes, via, pair, lone):
     group = gz[0]
-    n_rows = via.shape[1]
+    n_rows, n_cols = via.shape[1:]
     half = n_rows // 2 // STEP
+    of_i, of_o = [half_reciprocals(table, layer, n_cols) for layer in (1 - group, group)]
 
     def fill(k, carry):
         rows = block(k)
-        one = select_class(classes[1 - group, rows, :], lambda e: table[1 - group, e])
-        two = select_class(classes[group, rows, :], lambda e: table[group, e])
+        one = look_up(of_i, classes[1 - group, rows, :])
+        two = look_up(of_o, classes[group, rows, :])
         via[0, rows, :] = one
-        via[1, rows, :] = harmonic(one, two)
+        via[1, rows, :] = mean(one, two)
         return carry
 
-    lax.fori_loop(0, n_rows // STEP, fill, 0, unroll=2)
+    lax.fori_loop(0, n_rows // STEP, fill, 0, unroll=4)
 
     def copy(k, carry):
         for f in range(2):
@@ -224,32 +236,31 @@
         lone[block(k), :] = via[0, block(k + group * half), :]
         return carry
 
-    lax.fori_loop(0, half, copy, 0, unroll=2)
+    lax.fori_loop(0, half, copy, 0, unroll=4)
 
 
 def plane_kernel(gz, table, classes, load, sink, pad, via, plane, drawn, pair, top, bottom):
     group = gz[0]
-    n_rows = plane.shape[1]
+    n_rows, n_cols = plane.shape[1:]
     half = n_rows // 2 // STEP
+    of_i, of_o = [half_reciprocals(table, layer, n_cols) for layer in (1 - group, group)]
 
     def fill(k, carry):
         rows = block(k)
-        plane[0, rows, :] = select_class(
-            classes[1 - group, rows, :], lambda e: table[1 - group, e]
-        )
-        plane[1, rows, :] = select_class(classes[group, rows, :], lambda e: table[group, e])
+        plane[0, rows, :] = look_up(of_i, classes[1 - group, rows, :])
+        plane[1, rows, :] = look_up(of_o, classes[group, rows, :])
         plane[2, rows, :] = PAD_CONDUCTANCE * pad[rows, :].astype(jnp.float32)
         drawn[rows, :] = sink[rows, :].astype(jnp.float32) * load[rows, :]
         return carry
 
-    lax.fori_loop(0, n_rows // STEP, fill, 0, unroll=2)
+    lax.fori_loop(0, n_rows // STEP, fill, 0, unroll=4)
 
     def copy(k, carry):
         for f in range(2):
             pair[f, block(k), :] = plane[f, block(k + (1 - group) * half), :]
         return carry
 
-    lax.fori_loop(0, half, copy, 0, unroll=2)
+    lax.fori_loop(0, half, copy, 0, unroll=4)
     for f in range(N_OWN):
         at = pl.ds(DEEP * f, DEEP)
         top[at, :] = field_rows(plane, via, drawn, f, pl.ds(0, DEEP))
@@ -320,10 +331,31 @@
     small[at : at + size, tall_rows:] = east[:size, :]
 
 
+def eastward(value):
+    return pltpu.roll(value, value.shape[1] - 1, 1)
+
+
+def westward(value):
+    return pltpu.roll(value, 1, 1)
+
+
+def rows_up(value):
+    return pltpu.roll(value, STEP - 1, 0)
+
+
+def rows_down(value):
+    return pltpu.roll(value, 1, 0)
+
+
+def joined(edge, inner, outer):
+    sub = lax.broadcasted_iota(jnp.int32, inner.shape, 0)
+    return jnp.where(sub == edge, outer, inner)
+
+
 def own_kernel(gz, plane, via, drawn, south, north, west, east, near, edge_e, edge_n, near_sum, far_sum, wide, flat, tall):
     group = gz[0]
     n_rows, n_cols = drawn.shape
-    half = n_rows // 2
+    half, last = n_rows // 2 // STEP, n_rows // STEP + 1
     flat[...] = jnp.zeros(flat.shape, jnp.float32)
     for f in range(N_OWN):
         at = 2 * DEEP * f
@@ -333,72 +365,53 @@
 
     def put(rows, pick):
         strip = tall[rows, :]
-        for f in range(N_OWN):
+        for f in range(2):
             wide[f, rows, :n_cols] = pick(f)
-            wide[f, rows, n_cols:] = side(strip, f, 1.0 if f < N_FAR else 0.0)
+            wide[f, rows, n_cols:] = side(strip, f, 1.0)
 
     def inner(k, carry):
-        put(block(k + 1), lambda f: field_rows(plane, via, drawn, f, block(k)))
+        put(block(k + 1), lambda f: plane[f, block(k), :])
         return carry
 
     put(pl.ds(0, STEP), lambda f: tile_of(south, f, True))
-    lax.fori_loop(0, n_rows // STEP, inner, 0, unroll=2)
+    lax.fori_loop(0, n_rows // STEP, inner, 0, unroll=4)
     put(pl.ds(n_rows + STEP, STEP), lambda f: tile_of(north, f, False))
-    last = n_rows // STEP + 1
 
     def around(layer, k):
         value = wide[layer, block(k), :]
         over = wide[layer, block(jnp.minimum(k + 1, last)), :]
         under = wide[layer, block(jnp.maximum(k - 1, 0)), :]
-        sub = lax.broadcasted_iota(jnp.int32, value.shape, 0)
-        above = jnp.where(
-            sub == STEP - 1, pltpu.roll(over, STEP - 1, 0), pltpu.roll(value, STEP - 1, 0)
-        )
-        below = jnp.where(sub == 0, pltpu.roll(under, 1, 0), pltpu.roll(value, 1, 0))
-        to_east, to_north = harmonic(value, eastward(value)), harmonic(value, above)
-        return to_east, to_north, (to_east + westward(to_east)) + (to_north + harmonic(value, below))
+        above = joined(STEP - 1, rows_up(value), rows_up(over))
+        below = joined(0, rows_down(value), rows_down(under))
+        to_east, to_north = mean(value, eastward(value)), mean(value, above)
+        return to_east, to_north, (to_east + westward(to_east)) + (to_north + mean(value, below))
 
     def frame(k, carry):
-        at = k + group * (half // STEP)
+        at = k + group * half
         for layer in range(2):
             to_east, to_north, total = around(layer, at)
             edge_e[layer, block(k), :] = to_east
             edge_n[layer, block(k), :] = to_north
             near_sum[layer, block(k), :] = total
-            near[2 + layer, block(k), :] = wide[N_FAR + layer, block(at), :]
-            near[layer, block(k), :] = wide[2 + layer, block(at), :]
+        strip = tall[block(at), :]
+        inside = block(jnp.clip(at - 1, 0, last - 2))
+        for place, f in enumerate((2, 3, 4, 5)):
+            core = field_rows(plane, via, drawn, f, inside)
+            core = jnp.where(at == 0, tile_of(south, f, True), core)
+            core = jnp.where(at == last, tile_of(north, f, False), core)
+            near[place, block(k), :n_cols] = core
+            near[place, block(k), n_cols:] = side(strip, f, 1.0 if f < N_FAR else 0.0)
         return carry
 
-    lax.fori_loop(0, half // STEP + 2, frame, 0, unroll=2)
+    lax.fori_loop(0, half + 2, frame, 0, unroll=2)
 
     def other(k, carry):
         for layer in range(2):
-            total = around(layer, k + 1 + (1 - group) * (half // STEP))[2]
+            total = around(layer, k + 1 + (1 - group) * half)[2]
             far_sum[layer, block(k), :] = total[:, :n_cols]
         return carry
 
-    lax.fori_loop(0, half // STEP, other, 0, unroll=2)
-
-
-def above_of(field, j, r):
-    n_rows = field.shape[1]
-    if r + STEP < n_rows:
-        return field[j, r + 1 : r + 1 + STEP, :]
-    return pltpu.roll(field[j, r : r + STEP, :], STEP - 1, 0)
-
-
-def below_of(field, j, r):
-    if r:
-        return field[j, r - 1 : r - 1 + STEP, :]
-    return pltpu.roll(field[j, r : r + STEP, :], 1, 0)
-
-
-def eastward(value):
-    return pltpu.roll(value, value.shape[1] - 1, 1)
-
-
-def westward(value):
-    return pltpu.roll(value, 1, 1)
+    lax.fori_loop(0, half, other, 0, unroll=2)
 
 
 def fold(total):
@@ -409,43 +422,72 @@
     return jnp.sum(total, axis=0, keepdims=True)
 
 
-def images(field, r, near, far, cross):
-    owns, outs = [], []
-    for j in range(4):
-        east, north = near if j < 2 else far
-        e = j % 2
-        rows = pl.ds(r, STEP)
-        own, edge = field[j, rows, :], east[e, rows, :]
-        across = edge * eastward(own) + westward(edge * own)
-        along = north[e, rows, :] * above_of(field, j, r)
-        owns.append(own)
-        outs.append(across + (along + below_of(north, e, r) * below_of(field, j, r)))
-    link = cross[pl.ds(r, STEP), :]
-    outs[0] = outs[0] + link * owns[2]
-    outs[2] = outs[2] + link * owns[0]
-    return owns, outs
-
-
-def solved(inverse, r, outs):
-    news = []
+def image_pass(field, edges, cross, blocks, done):
+    last = field.shape[1] // STEP - 1
+
+    def at(k):
+        return pl.ds(k * STEP, STEP)
+
     for q in range(2):
-        ii, oo, io = [inverse[3 * q + e, pl.ds(r, STEP), :] for e in range(3)]
-        one, two = outs[2 * q], outs[2 * q + 1]
-        news += [ii * one + io * two, io * one + oo * two]
-    return news
+        east, north = edges[q]
+        ups, downs = {}, {}
+
+        def up(layer, k):
+            if (layer, k) not in ups:
+                ups[layer, k] = rows_up(field[2 * q + layer, at(k), :])
+            return ups[layer, k]
+
+        def down(layer, k):
+            if (layer, k) not in downs:
+                flux = north[layer, at(k), :] * field[2 * q + layer, at(k), :]
+                downs[layer, k] = rows_down(flux)
+            return downs[layer, k]
+
+        for k in blocks:
+            owns, outs = [], []
+            for layer in range(2):
+                own, edge = field[2 * q + layer, at(k), :], east[layer, at(k), :]
+                above = joined(STEP - 1, up(layer, k), up(layer, min(k + 1, last)))
+                below = joined(0, down(layer, k), down(layer, max(k - 1, 0)))
+                across = edge * eastward(own) + westward(edge * own)
+                owns.append(own)
+                outs.append(across + (north[layer, at(k), :] * above + below))
+            outs[0] = outs[0] + cross[at(k), :] * field[2 - 2 * q, at(k), :]
+            done(q, k, owns, outs)
+
+
+def solved(inverse, q, k, outs):
+    ii, oo, io = [inverse[3 * q + e, pl.ds(k * STEP, STEP), :] for e in range(3)]
+    return [ii * outs[0] + io * outs[1], io * outs[0] + oo * outs[1]]
 
 
 def dot(left, right, n_cols):
-    pairs = [a * b for a, b in zip(left, right)]
-    return ((pairs[0] + pairs[1]) + (pairs[2] + pairs[3]))[:, :n_cols]
+    return (left[0] * right[0] + left[1] * right[1])[:, :n_cols]
+
+
+def image_step(field, edges, cross, inverse, stepped, keep, n_cols):
+    n_blocks = field.shape[1] // STEP
+    sums = [jnp.zeros((STEP, n_cols), jnp.float32)] * 2
+
+    def done(q, k, owns, outs):
+        news = solved(inverse, q, k, outs)
+        for layer in range(2):
+            stepped[2 * q + layer, pl.ds(k * STEP, STEP), :] = news[layer]
+        if 0 < k < n_blocks - 1:
+            for layer in range(2):
+                keep[q][layer, pl.ds((k - 1) * STEP, STEP), :] = outs[layer][:, :n_cols]
+            sums[0] = sums[0] + dot(owns, outs, n_cols)
+            sums[1] = sums[1] + dot(news, outs, n_cols)
+
+    image_pass(field, edges, cross, range(n_blocks), done)
+    return sums
 
 
 def edge_kernel(gz, near, near_e, near_n, near_sum, big_plane, big_via, small, far_e, far_n, cross, inverse, step_1, n_own, inv_own, send, part, *scratch):
     fields, step_0, flat, tall = scratch
     group = gz[0]
     half, n_cols = big_via.shape[1:]
-    n_rows = half + 2 * STEP
-    n_blocks = n_rows // STEP
+    n_blocks = half // STEP + 2
     tall_rows = tall.shape[0]
     flat[...] = jnp.zeros(flat.shape, jnp.float32)
     for f in range(N_FAR):
@@ -464,31 +506,34 @@
             fields[f, rows, :n_cols] = core
             fields[f, rows, n_cols:] = side(strip, f, 1.0)
     total = jnp.zeros((STEP, n_cols), jnp.float32)
+    ups, downs = {}, {}
+
+    def up(layer, k):
+        if (layer, k) not in ups:
+            ups[layer, k] = rows_up(fields[layer, k * STEP : k * STEP + STEP, :])
+        return ups[layer, k]
+
     for k in range(n_blocks):
-        r = k * STEP
-        rows = pl.ds(r, STEP)
+        rows = pl.ds(k * STEP, STEP)
         sums = [near_sum[0, rows, :], near_sum[1, rows, :]]
         for layer in range(2):
             value = fields[layer, rows, :]
-            to_east = harmonic(value, eastward(value))
-            to_north = harmonic(value, above_of(fields, layer, r))
+            above = joined(STEP - 1, up(layer, k), up(layer, min(k + 1, n_blocks - 1)))
+            to_east, to_north = mean(value, eastward(value)), mean(value, above)
             far_e[layer, rows, :] = to_east
             far_n[layer, rows, :] = to_north
-            carried = pltpu.roll(to_north, 1, 0)
-            if k:
-                sub = lax.broadcasted_iota(jnp.int32, value.shape, 0)
-                under = pltpu.roll(far_n[layer, r - STEP : r, :], 1, 0)
-                carried = jnp.where(sub == 0, under, carried)
+            downs[layer, k] = rows_down(to_north)
+            carried = joined(0, downs[layer, k], downs[layer, max(k - 1, 0)])
             sums.append((to_east + westward(to_east)) + (to_north + carried))
-        link = harmonic(near[0, rows, :], fields[2, rows, :])
+        link = mean(near[0, rows, :], fields[2, rows, :])
         cross[rows, :] = link
         drawn, pads = near[2, rows, :], near[3, rows, :]
-        inner = pl.ds(r - STEP, STEP)
-        for q, up in ((0, near[1, rows, :]), (1, fields[3, rows, :])):
-            diag_i = sums[2 * q] + up + link
-            diag_o = sums[2 * q + 1] + up + jnp.where(group == 1 - q, pads, 0.0)
-            scale = 1.0 / (diag_i * diag_o - up * up)
-            found = (diag_o * scale, diag_i * scale, up * scale)
+        inner = pl.ds((k - 1) * STEP, STEP)
+        for q, up_edge in ((0, near[1, rows, :]), (1, fields[3, rows, :])):
+            diag_i = sums[2 * q] + up_edge + link
+            diag_o = sums[2 * q + 1] + up_edge + jnp.where(group == 1 - q, pads, 0.0)
+            scale = 1.0 / (diag_i * diag_o - up_edge * up_edge)
+            found = (diag_o * scale, diag_i * scale, up_edge * scale)
             for e in range(3):
                 inverse[3 * q + e, rows, :] = found[e]
                 if q == 0 and 0 < k < n_blocks - 1:
@@ -500,52 +545,29 @@
                 total = total + (two * here)[:, :n_cols]
     part[...] = jnp.zeros(part.shape, jnp.float32)
     part[0:1, :] = fold(total)
-    sums = [jnp.zeros((STEP, n_cols), jnp.float32)] * 2
-    for k in range(n_blocks):
-        r = k * STEP
-        owns, outs = images(step_0, r, (near_e, near_n), (far_e, far_n), cross)
-        news = solved(inverse, r, outs)
-        for j in range(4):
-            step_1[j, pl.ds(r, STEP), :] = news[j]
-        if 0 < k < n_blocks - 1:
-            inner = pl.ds(r - STEP, STEP)
-            for layer in range(2):
-                n_own[layer, inner, :] = outs[layer][:, :n_cols]
-                send[layer, inner, :] = outs[2 + layer][:, :n_cols]
-            sums[0] = sums[0] + dot(owns, outs, n_cols)
-            sums[1] = sums[1] + dot(news, outs, n_cols)
+    sums = image_step(
+        step_0, ((near_e, near_n), (far_e, far_n)), cross, inverse, step_1, (n_own, send), n_cols
+    )
     part[1:2, :] = fold(sums[0])
     part[2:3, :] = fold(sums[1])
 
 
 def steps_kernel(step_1, near_e, near_n, far_e, far_n, cross, inverse, before, n_own, send, spread, step_2):
-    n_rows = step_1.shape[1]
     n_cols = n_own.shape[2]
-    n_blocks = n_rows // STEP
-    near, far = (near_e, near_n), (far_e, far_n)
-    sums = [jnp.zeros((STEP, n_cols), jnp.float32)] * 3
-
-    def keep(first, r, outs):
-        inner = pl.ds(r - STEP, STEP)
+    edges = ((near_e, near_n), (far_e, far_n))
+    first, second = pl.ds(0, 2), pl.ds(2, 2)
+    sums = image_step(
+        step_1, edges, cross, inverse, step_2, (n_own.at[first], send.at[first]), n_cols
+    )
+    keep = (n_own.at[second], send.at[second])
+    sums.append(jnp.zeros((STEP, n_cols), jnp.float32))
+
+    def done(q, k, owns, outs):
         for layer in range(2):
-            n_own[first + layer, inner, :] = outs[layer][:, :n_cols]
-            send[first + layer, inner, :] = outs[2 + layer][:, :n_cols]
-
-    for k in range(n_blocks):
-        r = k * STEP
-        owns, outs = images(step_1, r, near, far, cross)
-        news = solved(inverse, r, outs)
-        for j in range(4):
-            step_2[j, pl.ds(r, STEP), :] = news[j]
-        if 0 < k < n_blocks - 1:
-            keep(0, r, outs)
-            sums[0] = sums[0] + dot(owns, outs, n_cols)
-            sums[1] = sums[1] + dot(news, outs, n_cols)
-    for k in range(1, n_blocks - 1):
-        r = k * STEP
-        owns, outs = images(step_2, r, near, far, cross)
-        keep(2, r, outs)
+            keep[q][layer, pl.ds((k - 1) * STEP, STEP), :] = outs[layer][:, :n_cols]
         sums[2] = sums[2] + dot(owns, outs, n_cols)
+
+    image_pass(step_2, edges, cross, range(1, step_1.shape[1] // STEP - 1), done)
     row = lax.broadcasted_iota(jnp.int32, before.shape, 0)
     part = before[...]
     for j in range(3):
@@ -561,7 +583,7 @@
     def fill(k, carry):
         rows, at = block(k), block(k + (1 - group) * (half // STEP))
         up = via[1, at, :]
-        diag_i = sums[0, rows, :] + up + harmonic(via[0, at, :], given[rows, :])
+        diag_i = sums[0, rows, :] + up + mean(via[0, at, :], given[rows, :])
         diag_o = sums[1, rows, :] + up + jnp.where(group == 1, plane[2, at, :], 0.0)
         scale = 1.0 / (diag_i * diag_o - up * up)
         inverse[0, rows, :] = diag_o * scale
@@ -585,7 +607,7 @@
         spread[k] = total
 
 
-def solve_kernel(parts, coefs, flag):
+def solve(parts):
     sums = jnp.sum(tree(parts), axis=1, keepdims=True)
     g = [jnp.broadcast_to(sums[k : k + 1, :], (1, LANES)) for k in range(6)]
     step = [g[k] - g[k + 1] for k in range(5)]
@@ -607,50 +629,61 @@
     x1 = y1 / d1 - l21 * x2
     x0 = y0 / d0 - l10 * x1 - l20 * x2
     c0, c1, c2 = x0 * scale[0], x1 * scale[1], x2 * scale[2]
-    for k, value in enumerate((c0, c1, c2, 1.0 - c0, c0 - c1, c1 - c2)):
-        coefs[k : k + 1, :] = value
-    coefs[6:8, :] = jnp.zeros((2, LANES), jnp.float32)
     good = (d0 > GUARD) & (d1 > GUARD) & (d2 > GUARD)
-    flag[...] = jnp.where(good, 1, 0)
-
-
-def combine_kernel(gz, coefs, current, inv_near, inv_far, n_0, n_0_far, n_12, n_12_far, volts, left):
+    return (c0, c1, c2, 1.0 - c0, c0 - c1, c1 - c2), good
+
+
+def combine_kernel(gz, parts, current, inv_near, inv_far, n_0, n_0_far, n_12, n_12_far, volts, left, flag, volts_here, left_here, sems):
     group = gz[0]
     half, n_cols = n_0.shape[1:]
-    c = [jnp.broadcast_to(coefs[k : k + 1, 0:1], (STEP, n_cols)) for k in range(6)]
-
-    def fill(near, inv, first, second):
-        start = (group if near else 1 - group) * (half // STEP)
-
+    values, good = solve(parts)
+    flag[...] = jnp.where(good, 1, 0)
+    c = [jnp.broadcast_to(value[:, 0:1], (STEP, n_cols)) for value in values]
+
+    def fill(part, inv, first, second):
         def body(k, carry):
-            rows, at = block(k), block(k + start)
+            rows, at = block(k), block(k + part * (half // STEP))
             drawn = jnp.where(group == 0, current[at, :], 0.0)
             n0i, n0o = first[0, rows, :], first[1, rows, :]
             n1i, n1o, n2i, n2o = [second[j, rows, :] for j in range(4)]
             ii, oo, io = [inv[e, rows, :] for e in range(3)]
             one = c[1] * n0i + c[2] * n1i
             two = c[0] * drawn + (c[1] * n0o + c[2] * n1o)
-            volts[1 - group, at, :] = ii * one + io * two
-            volts[group, at, :] = io * one + oo * two
-            left[1 - group, at, :] = c[4] * n0i + c[5] * n1i + c[2] * n2i
-            left[group, at, :] = c[3] * drawn + c[4] * n0o + c[5] * n1o + c[2] * n2o
+            volts_here[1 - group, at, :] = ii * one + io * two
+            volts_here[group, at, :] = io * one + oo * two
+            left_here[1 - group, at, :] = c[4] * n0i + c[5] * n1i + c[2] * n2i
+            left_here[group, at, :] = c[3] * drawn + c[4] * n0o + c[5] * n1o + c[2] * n2o
             return carry
 
         lax.fori_loop(0, half // STEP, body, 0, unroll=2)
 
-    fill(True, inv_near, n_0, n_12)
-    fill(False, inv_far, n_0_far, n_12_far)
-
-
-def call(kernel, outs, scratch, n_smem, *args):
-    return pallas(kernel, outs, scratch, n_smem, args)
-
-
-def pallas(kernel, outs, scratch, n_smem, args):
+    copies = []
+    for part in range(2):
+
+        @pl.when(group == part)
+        def _(part=part):
+            fill(part, inv_near, n_0, n_12)
+
+        @pl.when(group != part)
+        def _(part=part):
+            fill(part, inv_far, n_0_far, n_12_far)
+
+        for j, (source, target) in enumerate(((volts_here, volts), (left_here, left))):
+            rows = pl.ds(part * half, half)
+            copy = pltpu.make_async_copy(
+                source.at[:, rows, :], target.at[:, rows, :], sems.at[2 * part + j]
+            )
+            copy.start()
+            copies.append(copy)
+    for copy in copies:
+        copy.wait()
+
+
+def call(kernel, outs, scratch, n_smem, *args, outside=0):
     return pl.pallas_call(
         kernel,
         in_specs=[SMEM] * n_smem + [VMEM] * (len(args) - n_smem),
-        out_specs=[VMEM] * len(outs),
+        out_specs=[OUTSIDE] * outside + [VMEM] * (len(outs) - outside),
         out_shape=outs,
         scratch_shapes=scratch,
         compiler_params=pltpu.CompilerParams(vmem_limit_bytes=GRANT),
@@ -682,14 +715,14 @@
     via, pair, via_send = call(
         via_kernel,
         [array(2, n_rows, n_cols), array(2, half, n_cols), array(half, n_cols)],
-        [], 2, gz, via_table, via_class,
+        [], 1, gz, via_table, via_class,
     )
     big_via = lax.ppermute(pair, "gz", swap)
     plane, drawn, pair, top, bottom = call(
         plane_kernel,
         [array(3, n_rows, n_cols), array(n_rows, n_cols), array(2, half, n_cols)]
         + [array(DEEP * N_OWN, n_cols)] * 2,
-        [], 2, gz, plane_table, plane_class, load_current, sink_mask, pad_mask, via,
+        [], 1, gz, plane_table, plane_class, load_current, sink_mask, pad_mask, via,
     )
     south = lax.ppermute(bottom, GY, ring(GY))
     north = lax.ppermute(top, GY, back(ring(GY)))
@@ -736,13 +769,11 @@
     parts = lax.all_to_all(spread, GX, 0, 0, tiled=True)
     (spread,) = call(relay_kernel, [array(n_rest, STEP, LANES)], [], 0, parts)
     parts = lax.all_to_all(spread, rest, 0, 0, tiled=True)
-    coefs, flag = call(
-        solve_kernel,
-        [array(STEP, LANES), jax.ShapeDtypeStruct((1, LANES), jnp.int32)], [], 0, parts,
-    )
-    quick = call(
-        combine_kernel, [array(2, n_rows, n_cols)] * 2, [], 1,
-        gz, coefs, drawn, inv_near, inv_far, n_0, n_0_far, n_12, n_12_far,
+    volts, left, flag = call(
+        combine_kernel,
+        [array(2, n_rows, n_cols)] * 2 + [jax.ShapeDtypeStruct((1, LANES), jnp.int32)],
+        [pltpu.VMEM((2, n_rows, n_cols), jnp.float32)] * 2 + [pltpu.SemaphoreType.DMA((4,))],
+        1, gz, parts, drawn, inv_near, inv_far, n_0, n_0_far, n_12, n_12_far, outside=2,
     )
 
     def careful():
@@ -750,7 +781,7 @@
             load_current, sink_mask, pad_mask, plane_class, via_class, plane_table, via_table
         )
 
-    return lax.cond(flag[0, 0] == 1, lambda: tuple(quick), careful)
+    return lax.cond(flag[0, 0] == 1, lambda: (volts, left), careful)
 
 
 def solution(mesh):

time: 89.2 us -> 87.7 us (0.983)
  the two profiles are of different devices: /device:TPU:1 before, /device:TPU:2 now
where the time goes in v4:
time: 87.7 us; the launch traced here: 87.3 us
  waiting for transfers between devices  24 us (27%)
  starting transfers between devices  21.9 us (25%)
  Pallas kernels  18.7 us (21%)
  blocking collectives  15.1 us (17%)
  local copies, waits for them, and re-layouts  6.37 us (7%)
  between operations  0.99 us (1%)
    pallas_call x10, Pallas kernels, call(): pl.pallas_call(kernel, in_specs=[SMEM] * n_smem + [VMEM] * (len(args) - n...  18.7 us
    all_to_all x1, blocking collectives, shards(): parts = lax.all_to_all(spread, GX, 0, 0, tiled=True)  15.1 us
    ppermute x1, waiting for transfers between devices, shards(): south = lax.ppermute(bottom, GY, ring(GY))  13.8 us
    ppermute x1, waiting for transfers between devices, shards(): via_far = lax.ppermute(via_send, 'gz', swap)  8.74 us
    unnamed x22, local copies, waits for them, and re-layouts  6.37 us
    all_to_all x1, starting transfers between devices, shards(): parts = lax.all_to_all(spread, rest, 0, 0, tiled=True)  4.82 us
    ppermute x1, starting transfers between devices, shards(): north = lax.ppermute(top, GY, back(ring(GY)))  4.37 us
    ppermute x1, starting transfers between devices, shards(): east = lax.ppermute(first, GX, back(ring(GX)))  4.16 us
  transfers between devices with their start and end apart: 11, of which 3 were waited for; matrix products, arithmetic and copies ran while one was open for 0% of the time, Pallas kernels for 8%

profile of v4, /device:TPU:2, one launch (start us, length us, event | category | flops | bytes accessed | tf_op | source)
XLA Modules:
  0.0 87.3 jit_solution(1437007090565555545)
XLA Ops:
  0.6 2.5 %shard_map.90 = (f32[2,192,512]{2,1,0:T(8,128)S(1)}, f32[2,96,512]{2,1,0:T(8,128)S(1)}, f32[96,512]{1,0:T(8,128)}) custom-call(s32[1]{0:T(128)} %bitcast.23.gz, f32[2,8]{1,0:T(2,128)} %table.2, s32[2,192,512]{2,1,0:T(8,128)} %classes.2), custom_call_target="tpu_custom_call" | custom-call | tf_op jit(solution)/shard_map/pallas_call | solution.py:683
  3.2 2.2 %collective-permute-start.29 = (f32[2,96,512]{2,1,0:T(8,128)S(1)}, f32[2,96,512]{2,1,0:T(8,128)S(1)}, u32[]{:S(2)}, u32[]{:S(2)}) collective-permute-start(f32[2,96,512]{2,1,0:T(8,128)S(1)} %get-tuple-element.69), channel_id=1, source_target_pairs={{0,1},{1,0},{2,3},{3,2},{4,5},{5,4},{6,7},{7,6},{8,9},{9,8},{10,11... | collective-permute-start | bytes 1179656 | tf_op jit(solution)/shard_map/ppermute | solution.py:720
  5.4 1.9 %shard_map.91 = (f32[3,192,512]{2,1,0:T(8,128)S(1)}, f32[192,512]{1,0:T(8,128)S(1)}, f32[2,96,512]{2,1,0:T(8,128)S(1)}, f32[24,512]{1,0:T(8,128)S(1)}, f32[24,512]{1,0:T(8,128)S(1)}) custom-call(s32[1]{0:T(128)} %bitcast.23.gz, f32[2,8]{1,0:T(2,128)} %table.3, s32[2,192,512]{2,1,0:T(8,128)S(1)} %copy-done.27, f32[192,512]{1,0:T(8,128)} %load.1, ...), custom_call_target="tpu_custom_call" | custom-call | tf_op jit(solution)/shard_map/pallas_call | solution.py:683
  7.4 1.3 %collective-permute-start.24 = (f32[24,512]{1,0:T(8,128)S(1)}, f32[24,512]{1,0:T(8,128)S(1)}, u32[]{:S(2)}, u32[]{:S(2)}) collective-permute-start(f32[24,512]{1,0:T(8,128)S(1)} %get-tuple-element.60), channel_id=1, source_target_pairs={{0,2},{2,4},{4,6},{6,8},{8,10},{10,12},{12,14},{14,0},{1,3},{3,5},... | collective-permute-start | bytes 147464 | tf_op jit(solution)/shard_map/ppermute | solution.py:727
  8.8 4.4 %collective-permute-start.25 = (f32[24,512]{1,0:T(8,128)S(1)}, f32[24,512]{1,0:T(8,128)S(1)}, u32[]{:S(2)}, u32[]{:S(2)}) collective-permute-start(f32[24,512]{1,0:T(8,128)S(1)} %get-tuple-element.61), channel_id=1, source_target_pairs={{2,0},{4,2},{6,4},{8,6},{10,8},{12,10},{14,12},{0,14},{3,1},{5,3},... | collective-permute-start | bytes 147464 | tf_op jit(solution)/shard_map/ppermute | solution.py:728
  13.1 13.8 %collective-permute-done.24.south = f32[24,512]{1,0:T(8,128)S(1)} collective-permute-done((f32[24,512]{1,0:T(8,128)S(1)}, f32[24,512]{1,0:T(8,128)S(1)}, u32[]{:S(2)}, u32[]{:S(2)}) %collective-permute-start.24) | collective-permute-done | bytes 49184 | tf_op jit(solution)/shard_map/ppermute | solution.py:727
  26.9 1.2 %shard_map.92 = (f32[24,256]{1,0:T(8,128)S(1)}, f32[24,256]{1,0:T(8,128)S(1)}) custom-call(f32[3,192,512]{2,1,0:T(8,128)S(1)} %get-tuple-element.58.plane, f32[2,192,512]{2,1,0:T(8,128)S(1)} %get-tuple-element.57.via, f32[192,512]{1,0:T(8,128)S(1)} %get-tuple-element.59.drawn.current, f32[24,512]{1,0:T(8,128)S(1)} %collective-permute-done.24.south, ...), custom_call_target="tpu_custom_call" | custom-call | tf_op jit(solution)/shard_map/pallas_call | solution.py:683
  28.2 4.2 %collective-permute-start.27 = (f32[24,256]{1,0:T(8,128)S(1)}, f32[24,256]{1,0:T(8,128)S(1)}, u32[]{:S(2)}, u32[]{:S(2)}) collective-permute-start(f32[24,256]{1,0:T(8,128)S(1)} %get-tuple-element.63), channel_id=1, source_target_pairs={{16,0},{32,16},{48,32},{64,48},{80,64},{96,80},{112,96},{128,112},... | collective-permute-start | bytes 73736 | tf_op jit(solution)/shard_map/ppermute | solution.py:735
  32.3 1.5 %collective-permute-done.26.west = f32[24,256]{1,0:T(8,128)S(1)} collective-permute-done((f32[24,256]{1,0:T(8,128)S(1)}, f32[24,256]{1,0:T(8,128)S(1)}, u32[]{:S(2)}, u32[]{:S(2)}) %collective-permute-start.26) | collective-permute-done | bytes 24608 | tf_op jit(solution)/shard_map/ppermute | solution.py:734
  33.9 1.9 %collective-permute-start.30 = (f32[48,512]{1,0:T(8,128)S(1)}, f32[48,512]{1,0:T(8,128)S(1)}, u32[]{:S(2)}, u32[]{:S(2)}) collective-permute-start(f32[48,512]{1,0:T(8,128)S(1)} %shard_map.94), channel_id=1, source_target_pairs={{0,1},{1,0},{2,3},{3,2},{4,5},{5,4},{6,7},{7,6},{8,9},{9,8},{10,11... | collective-permute-start | bytes 294920 | tf_op jit(solution)/shard_map/ppermute | solution.py:740
  35.8 2.9 %shard_map.93 = (f32[4,112,640]{2,1,0:T(8,128)S(1)}, f32[2,112,640]{2,1,0:T(8,128)S(1)}, f32[2,112,640]{2,1,0:T(8,128)S(1)}, f32[2,112,640]{2,1,0:T(8,128)S(1)}, f32[2,96,512]{2,1,0:T(8,128)S(1)}) custom-call(s32[1]{0:T(128)} %bitcast.23.gz, f32[3,192,512]{2,1,0:T(8,128)S(1)} %get-tuple-element.58.plane, f32[2,192,512]{2,1,0:T(8,128)S(1)} %get-tuple-element.57.via, ...), custom_call_target="tpu_custom_call" | custom-call | tf_op jit(solution)/shard_map/pallas_call | solution.py:683
  39.5 4.1 %shard_map.95 = (f32[2,112,640]{2,1,0:T(8,128)S(1)}, f32[2,112,640]{2,1,0:T(8,128)S(1)}, f32[112,640]{1,0:T(8,128)S(1)}, f32[6,112,640]{2,1,0:T(8,128)S(1)}, f32...) custom-call(s32[1]{0:T(128)} %bitcast.23.gz, ...), custom_call_target="tpu_custom_call" | custom-call | tf_op jit(solution)/shard_map/pallas_call | solution.py:683
  43.6 2.3 %shard_map.96 = (f32[4,96,512]{2,1,0:T(8,128)S(1)}, f32[4,96,512]{2,1,0:T(8,128)}, f32[16,8,128]{2,1,0:T(8,128)S(1)}) custom-call(f32[4,112,640]{2,1,0:T(8,128)S(1)} %get-tuple-element.70.step_1, f32[2,112,640]{2,1,0:T(8,128)S(1)} %get-tuple-element.65.near_e, f32[2,112,640]{2,1,0:T(8,128)S(1)} %get-tuple-element.66.near_n, ...), custom_call_target="tpu_custom_call" | custom-call | tf_op jit(solution)/shard_map/pallas_call | solution.py:683
  46.8 0.9 %collective-permute-start.33 = (f32[4,96,512]{2,1,0:T(8,128)}, f32[4,96,512]{2,1,0:T(8,128)}, u32[]{:S(2)}, u32[]{:S(2)}) collective-permute-start(f32[4,96,512]{2,1,0:T(8,128)} %get-tuple-element.83), channel_id=1, source_target_pairs={{0,1},{1,0},{2,3},{3,2},{4,5},{5,4},{6,7},{7,6},{8,9},{9,8},{10,11... | collective-permute-start | bytes 2359304 | tf_op jit(solution)/shard_map/ppermute | solution.py:768
  47.7 1.1 %collective-permute-start.32 = (f32[2,96,512]{2,1,0:T(8,128)}, f32[2,96,512]{2,1,0:T(8,128)}, u32[]{:S(2)}, u32[]{:S(2)}) collective-permute-start(f32[2,96,512]{2,1,0:T(8,128)} %get-tuple-element.81), channel_id=1, source_target_pairs={{0,1},{1,0},{2,3},{3,2},{4,5},{5,4},{6,7},{7,6},{8,9},{9,8},{10,11... | collective-permute-start | bytes 1179656 | tf_op jit(solution)/shard_map/ppermute | solution.py:757
  48.8 0.9 %collective-permute-start.31 = (f32[96,512]{1,0:T(8,128)}, f32[96,512]{1,0:T(8,128)S(1)}, u32[]{:S(2)}, u32[]{:S(2)}) collective-permute-start(f32[96,512]{1,0:T(8,128)} %get-tuple-element.79), channel_id=1, source_target_pairs={{0,1},{1,0},{2,3},{3,2},{4,5},{5,4},{6,7},{7,6},{8,9},{9,8},{10,11... | collective-permute-start | bytes 589832 | tf_op jit(solution)/shard_map/ppermute | solution.py:741
  49.7 15.1 %all_to_all.10.parts = f32[16,8,128]{2,1,0:T(8,128)S(1)} all-to-all(f32[16,8,128]{2,1,0:T(8,128)S(1)} %get-tuple-element.76), channel_id=1, replica_groups=mesh['gx_0'=8,'gx_1'=2,'gy_0'=2,'gy_1'=4,'gz'=2] {'gx_0','gx_1'}, dimensions={0} | all-to-all | bytes 131072 | tf_op jit(solution)/shard_map/all_to_all | solution.py:769
  65.5 4.8 %all-to-all-start.1 = ((f32[16,8,128]{2,1,0:T(8,128)}), f32[16,8,128]{2,1,0:T(8,128)}, u32[]{:S(2)}, u32[]{:S(2)}) async-start(f32[16,8,128]{2,1,0:T(8,128)} %shard_map.97), calls=%async_computation.1 | async-start | bytes 131072 | tf_op jit(solution)/shard_map/all_to_all | solution.py:771
  70.3 8.7 %collective-permute-done.31.given = f32[96,512]{1,0:T(8,128)S(1)} collective-permute-done((f32[96,512]{1,0:T(8,128)}, f32[96,512]{1,0:T(8,128)S(1)}, u32[]{:S(2)}, u32[]{:S(2)}) %collective-permute-start.31) | collective-permute-done | bytes 196640 | tf_op jit(solution)/shard_map/ppermute | solution.py:741
  79.7 1.0 %copy-done.5 = f32[2,96,512]{2,1,0:T(8,128)S(1)} copy-done((f32[2,96,512]{2,1,0:T(8,128)S(1)}, f32[2,96,512]{2,1,0:T(8,128)}, u32[]{:S(2)}) %copy-start.5) | copy-done | bytes 393240
  80.7 0.9 %copy-done.7 = f32[96,512]{1,0:T(8,128)S(1)} copy-done((f32[96,512]{1,0:T(8,128)S(1)}, f32[96,512]{1,0:T(8,128)}, u32[]{:S(2)}) %copy-start.7) | copy-done | bytes 196632
  81.8 1.1 %copy-done.1 = f32[4,96,512]{2,1,0:T(8,128)S(1)} copy-done((f32[4,96,512]{2,1,0:T(8,128)S(1)}, f32[4,96,512]{2,1,0:T(8,128)}, u32[]{:S(2)}) %copy-start.1) | copy-done | bytes 786456
  83.0 1.0 %copy-done.3 = f32[2,96,512]{2,1,0:T(8,128)S(1)} copy-done((f32[2,96,512]{2,1,0:T(8,128)S(1)}, f32[2,96,512]{2,1,0:T(8,128)}, u32[]{:S(2)}) %copy-start.3) | copy-done | bytes 393240
  84.0 2.9 %shard_map.99 = (f32[2,192,512]{2,1,0:T(8,128)}, f32[2,192,512]{2,1,0:T(8,128)}, s32[1,128]{1,0:T(1,128)S(1)}) custom-call(s32[1]{0:T(128)} %bitcast.23.gz, f32[16,8,128]{2,1,0:T(8,128)} %all-to-all-done.1.parts, f32[192,512]{1,0:T(8,128)S(1)} %get-tuple-element.59.drawn.current, f32[3,96,512]{2,1,0:T(8,128)S(1)} %get-tuple-element.77.inv_near, ...), custom_call_target="tpu_custom_call" | custom-call | tf_op jit(solution)/shard_map/pallas_call | solution.py:683
  (32 shorter events, 3.6 us)
Async XLA Ops:
  0.6 4.8 %copy-start.27 = (s32[2,192,512]{2,1,0:T(8,128)S(1)}, s32[2,192,512]{2,1,0:T(8,128)}, u32[]{:S(2)}) copy-start(s32[2,192,512]{2,1,0:T(8,128)} %classes.3) | copy-start | bytes 2359300
  3.2 36.3 %collective-permute-start.29 = (f32[2,96,512]{2,1,0:T(8,128)S(1)}, f32[2,96,512]{2,1,0:T(8,128)S(1)}, u32[]{:S(2)}, u32[]{:S(2)}) collective-permute-start(f32[2,96,512]{2,1,0:T(8,128)S(1)} %get-tuple-element.69), channel_id=1, source_target_pairs={{0,1},{1,0},{2,3},{3,2},{4,5},{5,4},{6,7},{7,6},{8,9},{9,8},{10,11... | collective-permute-start | bytes 1179656 | tf_op jit(solution)/shard_map/ppermute | solution.py:720
  7.3 32.2 %collective-permute-start.28 = (f32[2,96,512]{2,1,0:T(8,128)S(1)}, f32[2,96,512]{2,1,0:T(8,128)S(1)}, u32[]{:S(2)}, u32[]{:S(2)}) collective-permute-start(f32[2,96,512]{2,1,0:T(8,128)S(1)} %get-tuple-element.68), channel_id=1, source_target_pairs={{0,1},{1,0},{2,3},{3,2},{4,5},{5,4},{6,7},{7,6},{8,9},{9,8},{10,11... | collective-permute-start | bytes 1179656 | tf_op jit(solution)/shard_map/ppermute | solution.py:729
  7.4 19.5 %collective-permute-start.24 = (f32[24,512]{1,0:T(8,128)S(1)}, f32[24,512]{1,0:T(8,128)S(1)}, u32[]{:S(2)}, u32[]{:S(2)}) collective-permute-start(f32[24,512]{1,0:T(8,128)S(1)} %get-tuple-element.60), channel_id=1, source_target_pairs={{0,2},{2,4},{4,6},{6,8},{8,10},{10,12},{12,14},{14,0},{1,3},{3,5},... | collective-permute-start | bytes 147464 | tf_op jit(solution)/shard_map/ppermute | solution.py:727
  8.8 18.1 %collective-permute-start.25 = (f32[24,512]{1,0:T(8,128)S(1)}, f32[24,512]{1,0:T(8,128)S(1)}, u32[]{:S(2)}, u32[]{:S(2)}) collective-permute-start(f32[24,512]{1,0:T(8,128)S(1)} %get-tuple-element.61), channel_id=1, source_target_pairs={{2,0},{4,2},{6,4},{8,6},{10,8},{12,10},{14,12},{0,14},{3,1},{5,3},... | collective-permute-start | bytes 147464 | tf_op jit(solution)/shard_map/ppermute | solution.py:728
  28.1 5.7 %collective-permute-start.26 = (f32[24,256]{1,0:T(8,128)S(1)}, f32[24,256]{1,0:T(8,128)S(1)}, u32[]{:S(2)}, u32[]{:S(2)}) collective-permute-start(f32[24,256]{1,0:T(8,128)S(1)} %get-tuple-element.62), channel_id=1, source_target_pairs={{0,16},{16,32},{32,48},{48,64},{64,80},{80,96},{96,112},{112,128},... | collective-permute-start | bytes 73736 | tf_op jit(solution)/shard_map/ppermute | solution.py:734
  28.2 5.7 %collective-permute-start.27 = (f32[24,256]{1,0:T(8,128)S(1)}, f32[24,256]{1,0:T(8,128)S(1)}, u32[]{:S(2)}, u32[]{:S(2)}) collective-permute-start(f32[24,256]{1,0:T(8,128)S(1)} %get-tuple-element.63), channel_id=1, source_target_pairs={{16,0},{32,16},{48,32},{64,48},{80,64},{96,80},{112,96},{128,112},... | collective-permute-start | bytes 73736 | tf_op jit(solution)/shard_map/ppermute | solution.py:735
  33.9 5.6 %collective-permute-start.30 = (f32[48,512]{1,0:T(8,128)S(1)}, f32[48,512]{1,0:T(8,128)S(1)}, u32[]{:S(2)}, u32[]{:S(2)}) collective-permute-start(f32[48,512]{1,0:T(8,128)S(1)} %shard_map.94), channel_id=1, source_target_pairs={{0,1},{1,0},{2,3},{3,2},{4,5},{5,4},{6,7},{7,6},{8,9},{9,8},{10,11... | collective-permute-start | bytes 294920 | tf_op jit(solution)/shard_map/ppermute | solution.py:740
  38.7 0.8 copy-start.4
  43.6 2.3 %copy-start.2 = (f32[2,96,512]{2,1,0:T(8,128)}, f32[2,96,512]{2,1,0:T(8,128)S(1)}, u32[]{:S(2)}) copy-start(f32[2,96,512]{2,1,0:T(8,128)S(1)} %get-tuple-element.80.n_0) | copy-start | bytes 1179652
  45.9 0.9 %copy-start = (f32[4,96,512]{2,1,0:T(8,128)}, f32[4,96,512]{2,1,0:T(8,128)S(1)}, u32[]{:S(2)}) copy-start(f32[4,96,512]{2,1,0:T(8,128)S(1)} %get-tuple-element.82.n_12) | copy-start | bytes 2359300
  46.8 35.1 %collective-permute-start.33 = (f32[4,96,512]{2,1,0:T(8,128)}, f32[4,96,512]{2,1,0:T(8,128)}, u32[]{:S(2)}, u32[]{:S(2)}) collective-permute-start(f32[4,96,512]{2,1,0:T(8,128)} %get-tuple-element.83), channel_id=1, source_target_pairs={{0,1},{1,0},{2,3},{3,2},{4,5},{5,4},{6,7},{7,6},{8,9},{9,8},{10,11... | collective-permute-start | bytes 2359304 | tf_op jit(solution)/shard_map/ppermute | solution.py:768
  47.7 34.1 %collective-permute-start.32 = (f32[2,96,512]{2,1,0:T(8,128)}, f32[2,96,512]{2,1,0:T(8,128)}, u32[]{:S(2)}, u32[]{:S(2)}) collective-permute-start(f32[2,96,512]{2,1,0:T(8,128)} %get-tuple-element.81), channel_id=1, source_target_pairs={{0,1},{1,0},{2,3},{3,2},{4,5},{5,4},{6,7},{7,6},{8,9},{9,8},{10,11... | collective-permute-start | bytes 1179656 | tf_op jit(solution)/shard_map/ppermute | solution.py:757
  48.8 30.2 %collective-permute-start.31 = (f32[96,512]{1,0:T(8,128)}, f32[96,512]{1,0:T(8,128)S(1)}, u32[]{:S(2)}, u32[]{:S(2)}) collective-permute-start(f32[96,512]{1,0:T(8,128)} %get-tuple-element.79), channel_id=1, source_target_pairs={{0,1},{1,0},{2,3},{3,2},{4,5},{5,4},{6,7},{7,6},{8,9},{9,8},{10,11... | collective-permute-start | bytes 589832 | tf_op jit(solution)/shard_map/ppermute | solution.py:741
  65.5 16.3 %all-to-all-start.1 = ((f32[16,8,128]{2,1,0:T(8,128)}), f32[16,8,128]{2,1,0:T(8,128)}, u32[]{:S(2)}, u32[]{:S(2)}) async-start(f32[16,8,128]{2,1,0:T(8,128)} %shard_map.97), calls=%async_computation.1 | async-start | bytes 131072 | tf_op jit(solution)/shard_map/all_to_all | solution.py:771
  79.0 0.7 copy-start.6
  79.7 1.0 %copy-start.5 = (f32[2,96,512]{2,1,0:T(8,128)S(1)}, f32[2,96,512]{2,1,0:T(8,128)}, u32[]{:S(2)}) copy-start(f32[2,96,512]{2,1,0:T(8,128)} %copy-done.4) | copy-start | bytes 1179652
  80.7 0.9 %copy-start.7 = (f32[96,512]{1,0:T(8,128)S(1)}, f32[96,512]{1,0:T(8,128)}, u32[]{:S(2)}) copy-start(f32[96,512]{1,0:T(8,128)} %copy-done.6) | copy-start | bytes 589828
  81.8 1.1 %copy-start.1 = (f32[4,96,512]{2,1,0:T(8,128)S(1)}, f32[4,96,512]{2,1,0:T(8,128)}, u32[]{:S(2)}) copy-start(f32[4,96,512]{2,1,0:T(8,128)} %copy-done) | copy-start | bytes 2359300
  83.0 1.0 %copy-start.3 = (f32[2,96,512]{2,1,0:T(8,128)S(1)}, f32[2,96,512]{2,1,0:T(8,128)}, u32[]{:S(2)}) copy-start(f32[2,96,512]{2,1,0:T(8,128)} %copy-done.2) | copy-start | bytes 1179652
  84.0 2.9 %copy-start.33 = (f32[2,8]{1,0:T(2,128)S(1)}, f32[2,8]{1,0:T(2,128)}, u32[]{:S(2)}) copy-start(f32[2,8]{1,0:T(2,128)} %table.3) | copy-start | bytes 196
  84.0 2.9 %copy-start.34 = (f32[2,8]{1,0:T(2,128)S(1)}, f32[2,8]{1,0:T(2,128)}, u32[]{:S(2)}) copy-start(f32[2,8]{1,0:T(2,128)} %table.2) | copy-start | bytes 196

commit v5 on v4

--- a/solution.py
+++ b/solution.py
@@ -214,7 +214,7 @@
     )
 
 
-def via_kernel(gz, table, classes, via, pair, lone):
+def via_kernel(gz, table, classes, via, first, lone):
     group = gz[0]
     n_rows, n_cols = via.shape[1:]
     half = n_rows // 2 // STEP
@@ -231,15 +231,14 @@
     lax.fori_loop(0, n_rows // STEP, fill, 0, unroll=4)
 
     def copy(k, carry):
-        for f in range(2):
-            pair[f, block(k), :] = via[f, block(k + (1 - group) * half), :]
+        first[block(k), :] = via[0, block(k + (1 - group) * half), :]
         lone[block(k), :] = via[0, block(k + group * half), :]
         return carry
 
     lax.fori_loop(0, half, copy, 0, unroll=4)
 
 
-def plane_kernel(gz, table, classes, load, sink, pad, via, plane, drawn, pair, top, bottom):
+def plane_kernel(gz, table, classes, load, sink, pad, via, plane, drawn, three, top, bottom):
     group = gz[0]
     n_rows, n_cols = plane.shape[1:]
     half = n_rows // 2 // STEP
@@ -256,8 +255,10 @@
     lax.fori_loop(0, n_rows // STEP, fill, 0, unroll=4)
 
     def copy(k, carry):
+        rows = block(k + (1 - group) * half)
         for f in range(2):
-            pair[f, block(k), :] = plane[f, block(k + (1 - group) * half), :]
+            three[f, block(k), :] = plane[f, rows, :]
+        three[2, block(k), :] = via[1, rows, :]
         return carry
 
     lax.fori_loop(0, half, copy, 0, unroll=4)
@@ -352,10 +353,30 @@
     return jnp.where(sub == edge, outer, inner)
 
 
+def edge_loop(wide, start, count, done):
+    last = wide.shape[1] // STEP - 1
+
+    def body(k, carried):
+        kept = []
+        for layer in range(2):
+            value = wide[layer, block(start + k), :]
+            over = wide[layer, block(jnp.minimum(start + k + 1, last)), :]
+            above = joined(STEP - 1, rows_up(value), rows_up(over))
+            to_east, to_north = mean(value, eastward(value)), mean(value, above)
+            down = rows_down(to_north)
+            south = joined(0, down, carried[layer])
+            kept.append(down)
+            done(layer, k, to_east, to_north, (to_east + westward(to_east)) + (to_north + south))
+        return tuple(kept)
+
+    none = jnp.zeros((STEP, wide.shape[2]), jnp.float32)
+    lax.fori_loop(0, count, body, (none, none), unroll=2)
+
+
 def own_kernel(gz, plane, via, drawn, south, north, west, east, near, edge_e, edge_n, near_sum, far_sum, wide, flat, tall):
     group = gz[0]
     n_rows, n_cols = drawn.shape
-    half, last = n_rows // 2 // STEP, n_rows // STEP + 1
+    half = n_rows // 2 // STEP
     flat[...] = jnp.zeros(flat.shape, jnp.float32)
     for f in range(N_OWN):
         at = 2 * DEEP * f
@@ -363,55 +384,51 @@
         flat[at + DEEP : at + 2 * DEEP, :] = east[DEEP * f : DEEP * f + DEEP, :]
     tall[...] = flat[...].T
 
-    def put(rows, pick):
+    def put(target, index, rows, value, strip, f):
+        target[index, rows, :n_cols] = value
+        target[index, rows, n_cols:] = side(strip, f, 1.0 if f < N_FAR else 0.0)
+
+    def inner(k, carry):
+        rows = block(k + 1)
         strip = tall[rows, :]
         for f in range(2):
-            wide[f, rows, :n_cols] = pick(f)
-            wide[f, rows, n_cols:] = side(strip, f, 1.0)
-
-    def inner(k, carry):
-        put(block(k + 1), lambda f: plane[f, block(k), :])
+            put(wide, f, rows, plane[f, block(k), :], strip, f)
         return carry
 
-    put(pl.ds(0, STEP), lambda f: tile_of(south, f, True))
-    lax.fori_loop(0, n_rows // STEP, inner, 0, unroll=4)
-    put(pl.ds(n_rows + STEP, STEP), lambda f: tile_of(north, f, False))
-
-    def around(layer, k):
-        value = wide[layer, block(k), :]
-        over = wide[layer, block(jnp.minimum(k + 1, last)), :]
-        under = wide[layer, block(jnp.maximum(k - 1, 0)), :]
-        above = joined(STEP - 1, rows_up(value), rows_up(over))
-        below = joined(0, rows_down(value), rows_down(under))
-        to_east, to_north = mean(value, eastward(value)), mean(value, above)
-        return to_east, to_north, (to_east + westward(to_east)) + (to_north + mean(value, below))
-
-    def frame(k, carry):
-        at = k + group * half
-        for layer in range(2):
-            to_east, to_north, total = around(layer, at)
-            edge_e[layer, block(k), :] = to_east
-            edge_n[layer, block(k), :] = to_north
-            near_sum[layer, block(k), :] = total
-        strip = tall[block(at), :]
-        inside = block(jnp.clip(at - 1, 0, last - 2))
-        for place, f in enumerate((2, 3, 4, 5)):
-            core = field_rows(plane, via, drawn, f, inside)
-            core = jnp.where(at == 0, tile_of(south, f, True), core)
-            core = jnp.where(at == last, tile_of(north, f, False), core)
-            near[place, block(k), :n_cols] = core
-            near[place, block(k), n_cols:] = side(strip, f, 1.0 if f < N_FAR else 0.0)
+    ends = (pl.ds(0, STEP), south, True), (pl.ds(n_rows + STEP, STEP), north, False)
+    for rows, stack, upper in ends:
+        for f in range(2):
+            put(wide, f, rows, tile_of(stack, f, upper), tall[rows, :], f)
+    lax.fori_loop(0, n_rows // STEP, inner, 0, unroll=2)
+
+    def rest(k, carry):
+        at = block(k + group * half)
+        strip = tall[block(k + 1 + group * half), :]
+        for f in range(2, N_OWN):
+            put(near, f - 2, block(k + 1), field_rows(plane, via, drawn, f, at), strip, f)
         return carry
 
-    lax.fori_loop(0, half + 2, frame, 0, unroll=2)
-
-    def other(k, carry):
-        for layer in range(2):
-            total = around(layer, k + 1 + (1 - group) * half)[2]
-            far_sum[layer, block(k), :] = total[:, :n_cols]
-        return carry
-
-    lax.fori_loop(0, half, other, 0, unroll=2)
+    lax.fori_loop(0, half, rest, 0, unroll=2)
+    for f in range(2, N_OWN):
+        value = field_rows(plane, via, drawn, f, pl.ds((half - 1) * STEP, STEP))
+        value = jnp.where(group == 0, tile_of(south, f, True), value)
+        put(near, f - 2, pl.ds(0, STEP), value, tall[block(group * half), :], f)
+        value = field_rows(plane, via, drawn, f, pl.ds(half * STEP, STEP))
+        value = jnp.where(group == 1, tile_of(north, f, False), value)
+        strip = tall[block(half + 1 + group * half), :]
+        put(near, f - 2, pl.ds((half + 1) * STEP, STEP), value, strip, f)
+
+    def done(layer, k, to_east, to_north, total):
+        edge_e[layer, block(k), :] = to_east
+        edge_n[layer, block(k), :] = to_north
+        near_sum[layer, block(k), :] = total
+
+    edge_loop(wide, group * half, half + 2, done)
+
+    def other(layer, k, to_east, to_north, total):
+        far_sum[layer, block(jnp.maximum(k - 1, 0)), :] = total[:, :n_cols]
+
+    edge_loop(wide, (1 - group) * half, half + 1, other)
 
 
 def fold(total):
@@ -422,37 +439,41 @@
     return jnp.sum(total, axis=0, keepdims=True)
 
 
-def image_pass(field, edges, cross, blocks, done):
+PAIRS = ((0, 0, 2), (1, 2, 0))
+
+
+def image_pass(field, edges, cross, blocks, done, pairs=PAIRS):
     last = field.shape[1] // STEP - 1
 
     def at(k):
         return pl.ds(k * STEP, STEP)
 
-    for q in range(2):
+    for q, base, facing in pairs:
         east, north = edges[q]
         ups, downs = {}, {}
 
         def up(layer, k):
             if (layer, k) not in ups:
-                ups[layer, k] = rows_up(field[2 * q + layer, at(k), :])
+                ups[layer, k] = rows_up(field[base + layer, at(k), :])
             return ups[layer, k]
 
         def down(layer, k):
             if (layer, k) not in downs:
-                flux = north[layer, at(k), :] * field[2 * q + layer, at(k), :]
+                flux = north[layer, at(k), :] * field[base + layer, at(k), :]
                 downs[layer, k] = rows_down(flux)
             return downs[layer, k]
 
         for k in blocks:
             owns, outs = [], []
             for layer in range(2):
-                own, edge = field[2 * q + layer, at(k), :], east[layer, at(k), :]
+                own, edge = field[base + layer, at(k), :], east[layer, at(k), :]
                 above = joined(STEP - 1, up(layer, k), up(layer, min(k + 1, last)))
                 below = joined(0, down(layer, k), down(layer, max(k - 1, 0)))
                 across = edge * eastward(own) + westward(edge * own)
                 owns.append(own)
                 outs.append(across + (north[layer, at(k), :] * above + below))
-            outs[0] = outs[0] + cross[at(k), :] * field[2 - 2 * q, at(k), :]
+            if facing is not None:
+                outs[0] = outs[0] + cross[at(k), :] * field[facing, at(k), :]
             done(q, k, owns, outs)
 
 
@@ -483,10 +504,10 @@
     return sums
 
 
-def edge_kernel(gz, near, near_e, near_n, near_sum, big_plane, big_via, small, far_e, far_n, cross, inverse, step_1, n_own, inv_own, send, part, *scratch):
+def edge_kernel(gz, near, near_e, near_n, near_sum, three, first, small, far_e, far_n, cross, inverse, step_1, n_own, inv_own, send, part, *scratch):
     fields, step_0, flat, tall = scratch
     group = gz[0]
-    half, n_cols = big_via.shape[1:]
+    half, n_cols = first.shape
     n_blocks = half // STEP + 2
     tall_rows = tall.shape[0]
     flat[...] = jnp.zeros(flat.shape, jnp.float32)
@@ -500,7 +521,7 @@
         strip = tall[block(k + group * (half // STEP)), :]
         for f in range(N_FAR):
             if 0 < k < n_blocks - 1:
-                core = (big_plane if f < 2 else big_via)[f % 2, (k - 1) * STEP : k * STEP, :]
+                core = (first if f == 2 else three.at[min(f, 2)])[(k - 1) * STEP : k * STEP, :]
             else:
                 core = pltpu.roll(small[2 * DEEP * f : 2 * DEEP * f + STEP, :], DEEP, 0)
             fields[f, rows, :n_cols] = core
@@ -529,6 +550,7 @@
         cross[rows, :] = link
         drawn, pads = near[2, rows, :], near[3, rows, :]
         inner = pl.ds((k - 1) * STEP, STEP)
+        both = []
         for q, up_edge in ((0, near[1, rows, :]), (1, fields[3, rows, :])):
             diag_i = sums[2 * q] + up_edge + link
             diag_o = sums[2 * q + 1] + up_edge + jnp.where(group == 1 - q, pads, 0.0)
@@ -538,16 +560,46 @@
                 inverse[3 * q + e, rows, :] = found[e]
                 if q == 0 and 0 < k < n_blocks - 1:
                     inv_own[e, inner, :] = found[e][:, :n_cols]
-            here = jnp.where(group == q, drawn, 0.0)
-            one, two = found[2] * here, found[1] * here
-            step_0[2 * q, rows, :], step_0[2 * q + 1, rows, :] = one, two
-            if 0 < k < n_blocks - 1:
-                total = total + (two * here)[:, :n_cols]
+            both.append(found)
+        one = jnp.where(group == 0, both[0][2], both[1][2]) * drawn
+        two = jnp.where(group == 0, both[0][1], both[1][1]) * drawn
+        step_0[0, rows, :], step_0[1, rows, :] = one, two
+        if 0 < k < n_blocks - 1:
+            total = total + (two * drawn)[:, :n_cols]
     part[...] = jnp.zeros(part.shape, jnp.float32)
     part[0:1, :] = fold(total)
-    sums = image_step(
-        step_0, ((near_e, near_n), (far_e, far_n)), cross, inverse, step_1, (n_own, send), n_cols
-    )
+    edges, keep = ((near_e, near_n), (far_e, far_n)), (n_own, send)
+    for q in range(2):
+
+        @pl.when(group == q)
+        def _(q=q):
+            first_step(q, step_0, edges, cross, inverse, step_1, keep, part)
+
+
+def first_step(q, step_0, edges, cross, inverse, step_1, keep, part):
+    n_cols = keep[0].shape[2]
+    n_blocks, p = step_0.shape[1] // STEP, 1 - q
+    sums = [jnp.zeros((STEP, n_cols), jnp.float32)] * 2
+
+    def done(_, k, owns, outs):
+        rows = pl.ds(k * STEP, STEP)
+        news = solved(inverse, q, k, outs)
+        over = cross[rows, :] * owns[0]
+        facing = inverse[3 * p, rows, :] * over
+        for layer in range(2):
+            step_1[2 * q + layer, rows, :] = news[layer]
+        step_1[2 * p, rows, :] = facing
+        step_1[2 * p + 1, rows, :] = inverse[3 * p + 2, rows, :] * over
+        if 0 < k < n_blocks - 1:
+            inner = pl.ds((k - 1) * STEP, STEP)
+            for layer in range(2):
+                keep[q][layer, inner, :] = outs[layer][:, :n_cols]
+            keep[p][0, inner, :] = over[:, :n_cols]
+            keep[p][1, inner, :] = jnp.zeros((STEP, n_cols), jnp.float32)
+            sums[0] = sums[0] + dot(owns, outs, n_cols)
+            sums[1] = sums[1] + (dot(news, outs, n_cols) + (facing * over)[:, :n_cols])
+
+    image_pass(step_0, edges, cross, range(n_blocks), done, ((q, 0, None),))
     part[1:2, :] = fold(sums[0])
     part[2:3, :] = fold(sums[1])
 
@@ -712,21 +764,21 @@
     rest = ("gy_0", "gy_1", "gz")
     n_gx, n_rest = lax.axis_size(GX), lax.axis_size(rest)
 
-    via, pair, via_send = call(
+    via, one, via_send = call(
         via_kernel,
-        [array(2, n_rows, n_cols), array(2, half, n_cols), array(half, n_cols)],
+        [array(2, n_rows, n_cols), array(half, n_cols), array(half, n_cols)],
         [], 1, gz, via_table, via_class,
     )
-    big_via = lax.ppermute(pair, "gz", swap)
-    plane, drawn, pair, top, bottom = call(
+    big_via = lax.ppermute(one, "gz", swap)
+    plane, drawn, three, top, bottom = call(
         plane_kernel,
-        [array(3, n_rows, n_cols), array(n_rows, n_cols), array(2, half, n_cols)]
+        [array(3, n_rows, n_cols), array(n_rows, n_cols), array(3, half, n_cols)]
         + [array(DEEP * N_OWN, n_cols)] * 2,
         [], 1, gz, plane_table, plane_class, load_current, sink_mask, pad_mask, via,
     )
     south = lax.ppermute(bottom, GY, ring(GY))
     north = lax.ppermute(top, GY, back(ring(GY)))
-    big_plane = lax.ppermute(pair, "gz", swap)
+    big_plane = lax.ppermute(three, "gz", swap)
     first, last = call(
         columns_kernel, [array(DEEP * N_OWN, tall)] * 2, turn[1:], 0,
         plane, via, drawn, south, north,
@@ -742,7 +794,7 @@
     near, near_e, near_n, near_sum, far_sum = call(
         own_kernel,
         [array(4, frame, broad)] + [array(2, frame, broad)] * 3 + [array(2, half, n_cols)],
-        [pltpu.VMEM((N_OWN, n_rows + 2 * STEP, broad), jnp.float32)] + turn,
+        [pltpu.VMEM((2, n_rows + 2 * STEP, broad), jnp.float32)] + turn,
         1, gz, plane, via, drawn, south, north, west, east,
     )
     far_e, far_n, cross, inverse, step_1, n_0, inv_near, send, part = call(
@@ -750,7 +802,7 @@
         [array(2, frame, broad)] * 2
         + [array(frame, broad), array(6, frame, broad), array(4, frame, broad),
            array(2, half, n_cols), array(3, half, n_cols), array(2, half, n_cols), array(STEP, LANES)],
-        [pltpu.VMEM((N_FAR, frame, broad), jnp.float32), pltpu.VMEM((4, frame, broad), jnp.float32)]
+        [pltpu.VMEM((N_FAR, frame, broad), jnp.float32), pltpu.VMEM((2, frame, broad), jnp.float32)]
         + turn,
         1, gz, near, near_e, near_n, near_sum, big_plane, big_via, small,
     )

time: 87.7 us -> 89.8 us (1.024)
  the two profiles are of different devices: /device:TPU:2 before, /device:TPU:1 now
where the time goes in v5:
time: 89.8 us; the launch traced here: 88.7 us
  waiting for transfers between devices  27.7 us (31%)
  Pallas kernels  18.8 us (21%)
  starting transfers between devices  18.1 us (20%)
  blocking collectives  16.6 us (18%)
  local copies, waits for them, and re-layouts  6.37 us (7%)
  between operations  0.99 us (1%)
    pallas_call x10, Pallas kernels, call(): pl.pallas_call(kernel, in_specs=[SMEM] * n_smem + [VMEM] * (len(args) - n...  18.8 us
    ppermute x1, waiting for transfers between devices, shards(): south = lax.ppermute(bottom, GY, ring(GY))  17.2 us
    all_to_all x1, blocking collectives, shards(): parts = lax.all_to_all(spread, GX, 0, 0, tiled=True)  16.6 us
    ppermute x1, waiting for transfers between devices, shards(): via_far = lax.ppermute(via_send, 'gz', swap)  6.95 us
    unnamed x22, local copies, waits for them, and re-layouts  6.37 us
    all_to_all x1, starting transfers between devices, shards(): parts = lax.all_to_all(spread, rest, 0, 0, tiled=True)  4.15 us
    ppermute x1, starting transfers between devices, shards(): north = lax.ppermute(top, GY, back(ring(GY)))  3.9 us
    ppermute x1, starting transfers between devices, shards(): west = lax.ppermute(last, GX, ring(GX))  3.36 us
  transfers between devices with their start and end apart: 11, of which 4 were waited for; matrix products, arithmetic and copies ran while one was open for 0% of the time, Pallas kernels for 7%

profile of v5, /device:TPU:1, one launch (start us, length us, event | category | flops | bytes accessed | tf_op | source)
XLA Modules:
  0.0 88.7 jit_solution(1116610280568658094)
XLA Ops:
  0.6 2.5 %shard_map.90 = (f32[2,192,512]{2,1,0:T(8,128)S(1)}, f32[96,512]{1,0:T(8,128)S(1)}, f32[96,512]{1,0:T(8,128)}) custom-call(s32[1]{0:T(128)} %bitcast.23.gz, f32[2,8]{1,0:T(2,128)} %table.2, s32[2,192,512]{2,1,0:T(8,128)} %classes.2), custom_call_target="tpu_custom_call" | custom-call | tf_op jit(solution)/shard_map/pallas_call | solution.py:735
  3.2 1.9 %shard_map.91 = (f32[3,192,512]{2,1,0:T(8,128)S(1)}, f32[192,512]{1,0:T(8,128)S(1)}, f32[3,96,512]{2,1,0:T(8,128)S(1)}, f32[24,512]{1,0:T(8,128)S(1)}, f32[24,512]{1,0:T(8,128)S(1)}) custom-call(s32[1]{0:T(128)} %bitcast.23.gz, f32[2,8]{1,0:T(2,128)} %table.3, s32[2,192,512]{2,1,0:T(8,128)S(1)} %copy-done.27, f32[192,512]{1,0:T(8,128)} %load.1, ...), custom_call_target="tpu_custom_call" | custom-call | tf_op jit(solution)/shard_map/pallas_call | solution.py:735
  5.1 2.1 %collective-permute-start.28 = (f32[3,96,512]{2,1,0:T(8,128)S(1)}, f32[3,96,512]{2,1,0:T(8,128)S(1)}, u32[]{:S(2)}, u32[]{:S(2)}) collective-permute-start(f32[3,96,512]{2,1,0:T(8,128)S(1)} %get-tuple-element.68), channel_id=1, source_target_pairs={{0,1},{1,0},{2,3},{3,2},{4,5},{5,4},{6,7},{7,6},{8,9},{9,8},{10,11... | collective-permute-start | bytes 1769480 | tf_op jit(solution)/shard_map/ppermute | solution.py:781
  7.3 1.5 %collective-permute-start.24 = (f32[24,512]{1,0:T(8,128)S(1)}, f32[24,512]{1,0:T(8,128)S(1)}, u32[]{:S(2)}, u32[]{:S(2)}) collective-permute-start(f32[24,512]{1,0:T(8,128)S(1)} %get-tuple-element.60), channel_id=1, source_target_pairs={{0,2},{2,4},{4,6},{6,8},{8,10},{10,12},{12,14},{14,0},{1,3},{3,5},... | collective-permute-start | bytes 147464 | tf_op jit(solution)/shard_map/ppermute | solution.py:779
  8.8 3.9 %collective-permute-start.25 = (f32[24,512]{1,0:T(8,128)S(1)}, f32[24,512]{1,0:T(8,128)S(1)}, u32[]{:S(2)}, u32[]{:S(2)}) collective-permute-start(f32[24,512]{1,0:T(8,128)S(1)} %get-tuple-element.61), channel_id=1, source_target_pairs={{2,0},{4,2},{6,4},{8,6},{10,8},{12,10},{14,12},{0,14},{3,1},{5,3},... | collective-permute-start | bytes 147464 | tf_op jit(solution)/shard_map/ppermute | solution.py:780
  12.7 17.2 %collective-permute-done.24.south = f32[24,512]{1,0:T(8,128)S(1)} collective-permute-done((f32[24,512]{1,0:T(8,128)S(1)}, f32[24,512]{1,0:T(8,128)S(1)}, u32[]{:S(2)}, u32[]{:S(2)}) %collective-permute-start.24) | collective-permute-done | bytes 49184 | tf_op jit(solution)/shard_map/ppermute | solution.py:779
  29.8 1.2 %shard_map.92 = (f32[24,256]{1,0:T(8,128)S(1)}, f32[24,256]{1,0:T(8,128)S(1)}) custom-call(f32[3,192,512]{2,1,0:T(8,128)S(1)} %get-tuple-element.58.plane, f32[2,192,512]{2,1,0:T(8,128)S(1)} %get-tuple-element.57.via, f32[192,512]{1,0:T(8,128)S(1)} %get-tuple-element.59.drawn.current, f32[24,512]{1,0:T(8,128)S(1)} %collective-permute-done.24.south, ...), custom_call_target="tpu_custom_call" | custom-call | tf_op jit(solution)/shard_map/pallas_call | solution.py:735
  31.1 3.4 %collective-permute-start.26 = (f32[24,256]{1,0:T(8,128)S(1)}, f32[24,256]{1,0:T(8,128)S(1)}, u32[]{:S(2)}, u32[]{:S(2)}) collective-permute-start(f32[24,256]{1,0:T(8,128)S(1)} %get-tuple-element.62), channel_id=1, source_target_pairs={{0,16},{16,32},{32,48},{48,64},{64,80},{80,96},{96,112},{112,128},... | collective-permute-start | bytes 73736 | tf_op jit(solution)/shard_map/ppermute | solution.py:786
  34.4 0.9 %collective-permute-done.26.west = f32[24,256]{1,0:T(8,128)S(1)} collective-permute-done((f32[24,256]{1,0:T(8,128)S(1)}, f32[24,256]{1,0:T(8,128)S(1)}, u32[]{:S(2)}, u32[]{:S(2)}) %collective-permute-start.26) | collective-permute-done | bytes 24608 | tf_op jit(solution)/shard_map/ppermute | solution.py:786
  35.4 2.6 %collective-permute-done.27.east = f32[24,256]{1,0:T(8,128)S(1)} collective-permute-done((f32[24,256]{1,0:T(8,128)S(1)}, f32[24,256]{1,0:T(8,128)S(1)}, u32[]{:S(2)}, u32[]{:S(2)}) %collective-permute-start.27) | collective-permute-done | bytes 24608 | tf_op jit(solution)/shard_map/ppermute | solution.py:787
  38.1 4.0 %shard_map.93 = (f32[4,112,640]{2,1,0:T(8,128)S(1)}, f32[2,112,640]{2,1,0:T(8,128)S(1)}, f32[2,112,640]{2,1,0:T(8,128)S(1)}, f32[2,112,640]{2,1,0:T(8,128)S(1)}, f32[2,96,512]{2,1,0:T(8,128)S(1)}) custom-call(s32[1]{0:T(128)} %bitcast.23.gz, f32[3,192,512]{2,1,0:T(8,128)S(1)} %get-tuple-element.58.plane, f32[2,192,512]{2,1,0:T(8,128)S(1)} %get-tuple-element.57.via, ...), custom_call_target="tpu_custom_call" | custom-call | tf_op jit(solution)/shard_map/pallas_call | solution.py:735
  42.8 3.2 %shard_map.95 = (f32[2,112,640]{2,1,0:T(8,128)S(1)}, f32[2,112,640]{2,1,0:T(8,128)S(1)}, f32[112,640]{1,0:T(8,128)S(1)}, f32[6,112,640]{2,1,0:T(8,128)S(1)}, f32...) custom-call(s32[1]{0:T(128)} %bitcast.23.gz, ...), custom_call_target="tpu_custom_call" | custom-call | tf_op jit(solution)/shard_map/pallas_call | solution.py:735
  46.1 2.3 %shard_map.96 = (f32[4,96,512]{2,1,0:T(8,128)S(1)}, f32[4,96,512]{2,1,0:T(8,128)}, f32[16,8,128]{2,1,0:T(8,128)S(1)}) custom-call(f32[4,112,640]{2,1,0:T(8,128)S(1)} %get-tuple-element.70.step_1, f32[2,112,640]{2,1,0:T(8,128)S(1)} %get-tuple-element.65.near_e, f32[2,112,640]{2,1,0:T(8,128)S(1)} %get-tuple-element.66.near_n, ...), custom_call_target="tpu_custom_call" | custom-call | tf_op jit(solution)/shard_map/pallas_call | solution.py:735
  48.4 0.9 copy-done
  49.2 1.4 %collective-permute-start.33 = (f32[4,96,512]{2,1,0:T(8,128)}, f32[4,96,512]{2,1,0:T(8,128)}, u32[]{:S(2)}, u32[]{:S(2)}) collective-permute-start(f32[4,96,512]{2,1,0:T(8,128)} %get-tuple-element.83), channel_id=1, source_target_pairs={{0,1},{1,0},{2,3},{3,2},{4,5},{5,4},{6,7},{7,6},{8,9},{9,8},{10,11... | collective-permute-start | bytes 2359304 | tf_op jit(solution)/shard_map/ppermute | solution.py:820
  50.7 1.4 %collective-permute-start.31 = (f32[96,512]{1,0:T(8,128)}, f32[96,512]{1,0:T(8,128)S(1)}, u32[]{:S(2)}, u32[]{:S(2)}) collective-permute-start(f32[96,512]{1,0:T(8,128)} %get-tuple-element.79), channel_id=1, source_target_pairs={{0,1},{1,0},{2,3},{3,2},{4,5},{5,4},{6,7},{7,6},{8,9},{9,8},{10,11... | collective-permute-start | bytes 589832 | tf_op jit(solution)/shard_map/ppermute | solution.py:793
  52.1 16.6 %all_to_all.10.parts = f32[16,8,128]{2,1,0:T(8,128)S(1)} all-to-all(f32[16,8,128]{2,1,0:T(8,128)S(1)} %get-tuple-element.76), channel_id=1, replica_groups=mesh['gx_0'=8,'gx_1'=2,'gy_0'=2,'gy_1'=4,'gz'=2] {'gx_0','gx_1'}, dimensions={0} | all-to-all | bytes 131072 | tf_op jit(solution)/shard_map/all_to_all | solution.py:821
  69.4 4.1 %all-to-all-start.1 = ((f32[16,8,128]{2,1,0:T(8,128)}), f32[16,8,128]{2,1,0:T(8,128)}, u32[]{:S(2)}, u32[]{:S(2)}) async-start(f32[16,8,128]{2,1,0:T(8,128)} %shard_map.97), calls=%async_computation.1 | async-start | bytes 131072 | tf_op jit(solution)/shard_map/all_to_all | solution.py:823
  73.5 6.9 %collective-permute-done.31.given = f32[96,512]{1,0:T(8,128)S(1)} collective-permute-done((f32[96,512]{1,0:T(8,128)}, f32[96,512]{1,0:T(8,128)S(1)}, u32[]{:S(2)}, u32[]{:S(2)}) %collective-permute-start.31) | collective-permute-done | bytes 196640 | tf_op jit(solution)/shard_map/ppermute | solution.py:793
  81.1 1.0 %copy-done.5 = f32[2,96,512]{2,1,0:T(8,128)S(1)} copy-done((f32[2,96,512]{2,1,0:T(8,128)S(1)}, f32[2,96,512]{2,1,0:T(8,128)}, u32[]{:S(2)}) %copy-start.5) | copy-done | bytes 393240
  82.1 0.9 %copy-done.7 = f32[96,512]{1,0:T(8,128)S(1)} copy-done((f32[96,512]{1,0:T(8,128)S(1)}, f32[96,512]{1,0:T(8,128)}, u32[]{:S(2)}) %copy-start.7) | copy-done | bytes 196632
  83.3 1.1 %copy-done.1 = f32[4,96,512]{2,1,0:T(8,128)S(1)} copy-done((f32[4,96,512]{2,1,0:T(8,128)S(1)}, f32[4,96,512]{2,1,0:T(8,128)}, u32[]{:S(2)}) %copy-start.1) | copy-done | bytes 786456
  84.4 1.0 %copy-done.3 = f32[2,96,512]{2,1,0:T(8,128)S(1)} copy-done((f32[2,96,512]{2,1,0:T(8,128)S(1)}, f32[2,96,512]{2,1,0:T(8,128)}, u32[]{:S(2)}) %copy-start.3) | copy-done | bytes 393240
  85.4 2.9 %shard_map.99 = (f32[2,192,512]{2,1,0:T(8,128)}, f32[2,192,512]{2,1,0:T(8,128)}, s32[1,128]{1,0:T(1,128)S(1)}) custom-call(s32[1]{0:T(128)} %bitcast.23.gz, f32[16,8,128]{2,1,0:T(8,128)} %all-to-all-done.1.parts, f32[192,512]{1,0:T(8,128)S(1)} %get-tuple-element.59.drawn.current, f32[3,96,512]{2,1,0:T(8,128)S(1)} %get-tuple-element.77.inv_near, ...), custom_call_target="tpu_custom_call" | custom-call | tf_op jit(solution)/shard_map/pallas_call | solution.py:735
  (32 shorter events, 2.8 us)
Async XLA Ops:
  0.6 2.5 %copy-start.27 = (s32[2,192,512]{2,1,0:T(8,128)S(1)}, s32[2,192,512]{2,1,0:T(8,128)}, u32[]{:S(2)}) copy-start(s32[2,192,512]{2,1,0:T(8,128)} %classes.3) | copy-start | bytes 2359300
  5.1 37.8 %collective-permute-start.28 = (f32[3,96,512]{2,1,0:T(8,128)S(1)}, f32[3,96,512]{2,1,0:T(8,128)S(1)}, u32[]{:S(2)}, u32[]{:S(2)}) collective-permute-start(f32[3,96,512]{2,1,0:T(8,128)S(1)} %get-tuple-element.68), channel_id=1, source_target_pairs={{0,1},{1,0},{2,3},{3,2},{4,5},{5,4},{6,7},{7,6},{8,9},{9,8},{10,11... | collective-permute-start | bytes 1769480 | tf_op jit(solution)/shard_map/ppermute | solution.py:781
  7.2 35.6 %collective-permute-start.29 = (f32[96,512]{1,0:T(8,128)S(1)}, f32[96,512]{1,0:T(8,128)S(1)}, u32[]{:S(2)}, u32[]{:S(2)}) collective-permute-start(f32[96,512]{1,0:T(8,128)S(1)} %get-tuple-element.69), channel_id=1, source_target_pairs={{0,1},{1,0},{2,3},{3,2},{4,5},{5,4},{6,7},{7,6},{8,9},{9,8},{10,11... | collective-permute-start | bytes 589832 | tf_op jit(solution)/shard_map/ppermute | solution.py:772
  7.3 22.5 %collective-permute-start.24 = (f32[24,512]{1,0:T(8,128)S(1)}, f32[24,512]{1,0:T(8,128)S(1)}, u32[]{:S(2)}, u32[]{:S(2)}) collective-permute-start(f32[24,512]{1,0:T(8,128)S(1)} %get-tuple-element.60), channel_id=1, source_target_pairs={{0,2},{2,4},{4,6},{6,8},{8,10},{10,12},{12,14},{14,0},{1,3},{3,5},... | collective-permute-start | bytes 147464 | tf_op jit(solution)/shard_map/ppermute | solution.py:779
  8.8 21.1 %collective-permute-start.25 = (f32[24,512]{1,0:T(8,128)S(1)}, f32[24,512]{1,0:T(8,128)S(1)}, u32[]{:S(2)}, u32[]{:S(2)}) collective-permute-start(f32[24,512]{1,0:T(8,128)S(1)} %get-tuple-element.61), channel_id=1, source_target_pairs={{2,0},{4,2},{6,4},{8,6},{10,8},{12,10},{14,12},{0,14},{3,1},{5,3},... | collective-permute-start | bytes 147464 | tf_op jit(solution)/shard_map/ppermute | solution.py:780
  31.1 4.3 %collective-permute-start.26 = (f32[24,256]{1,0:T(8,128)S(1)}, f32[24,256]{1,0:T(8,128)S(1)}, u32[]{:S(2)}, u32[]{:S(2)}) collective-permute-start(f32[24,256]{1,0:T(8,128)S(1)} %get-tuple-element.62), channel_id=1, source_target_pairs={{0,16},{16,32},{32,48},{48,64},{64,80},{80,96},{96,112},{112,128},... | collective-permute-start | bytes 73736 | tf_op jit(solution)/shard_map/ppermute | solution.py:786
  34.4 3.5 %collective-permute-start.27 = (f32[24,256]{1,0:T(8,128)S(1)}, f32[24,256]{1,0:T(8,128)S(1)}, u32[]{:S(2)}, u32[]{:S(2)}) collective-permute-start(f32[24,256]{1,0:T(8,128)S(1)} %get-tuple-element.63), channel_id=1, source_target_pairs={{16,0},{32,16},{48,32},{64,48},{80,64},{96,80},{112,96},{128,112},... | collective-permute-start | bytes 73736 | tf_op jit(solution)/shard_map/ppermute | solution.py:787
  38.0 4.8 %collective-permute-start.30 = (f32[48,512]{1,0:T(8,128)S(1)}, f32[48,512]{1,0:T(8,128)S(1)}, u32[]{:S(2)}, u32[]{:S(2)}) collective-permute-start(f32[48,512]{1,0:T(8,128)S(1)} %shard_map.94), channel_id=1, source_target_pairs={{0,1},{1,0},{2,3},{3,2},{4,5},{5,4},{6,7},{7,6},{8,9},{9,8},{10,11... | collective-permute-start | bytes 294920 | tf_op jit(solution)/shard_map/ppermute | solution.py:792
  42.1 0.8 copy-start.4
  46.1 2.3 %copy-start.2 = (f32[2,96,512]{2,1,0:T(8,128)}, f32[2,96,512]{2,1,0:T(8,128)S(1)}, u32[]{:S(2)}) copy-start(f32[2,96,512]{2,1,0:T(8,128)S(1)} %get-tuple-element.80.n_0) | copy-start | bytes 1179652
  48.4 0.9 copy-start
  49.2 34.0 %collective-permute-start.33 = (f32[4,96,512]{2,1,0:T(8,128)}, f32[4,96,512]{2,1,0:T(8,128)}, u32[]{:S(2)}, u32[]{:S(2)}) collective-permute-start(f32[4,96,512]{2,1,0:T(8,128)} %get-tuple-element.83), channel_id=1, source_target_pairs={{0,1},{1,0},{2,3},{3,2},{4,5},{5,4},{6,7},{7,6},{8,9},{9,8},{10,11... | collective-permute-start | bytes 2359304 | tf_op jit(solution)/shard_map/ppermute | solution.py:820
  50.7 32.6 %collective-permute-start.32 = (f32[2,96,512]{2,1,0:T(8,128)}, f32[2,96,512]{2,1,0:T(8,128)}, u32[]{:S(2)}, u32[]{:S(2)}) collective-permute-start(f32[2,96,512]{2,1,0:T(8,128)} %get-tuple-element.81), channel_id=1, source_target_pairs={{0,1},{1,0},{2,3},{3,2},{4,5},{5,4},{6,7},{7,6},{8,9},{9,8},{10,11... | collective-permute-start | bytes 1179656 | tf_op jit(solution)/shard_map/ppermute | solution.py:809
  50.7 29.8 %collective-permute-start.31 = (f32[96,512]{1,0:T(8,128)}, f32[96,512]{1,0:T(8,128)S(1)}, u32[]{:S(2)}, u32[]{:S(2)}) collective-permute-start(f32[96,512]{1,0:T(8,128)} %get-tuple-element.79), channel_id=1, source_target_pairs={{0,1},{1,0},{2,3},{3,2},{4,5},{5,4},{6,7},{7,6},{8,9},{9,8},{10,11... | collective-permute-start | bytes 589832 | tf_op jit(solution)/shard_map/ppermute | solution.py:793
  69.4 13.9 %all-to-all-start.1 = ((f32[16,8,128]{2,1,0:T(8,128)}), f32[16,8,128]{2,1,0:T(8,128)}, u32[]{:S(2)}, u32[]{:S(2)}) async-start(f32[16,8,128]{2,1,0:T(8,128)} %shard_map.97), calls=%async_computation.1 | async-start | bytes 131072 | tf_op jit(solution)/shard_map/all_to_all | solution.py:823
  80.5 0.7 copy-start.6
  81.1 1.0 %copy-start.5 = (f32[2,96,512]{2,1,0:T(8,128)S(1)}, f32[2,96,512]{2,1,0:T(8,128)}, u32[]{:S(2)}) copy-start(f32[2,96,512]{2,1,0:T(8,128)} %copy-done.4) | copy-start | bytes 1179652
  82.1 0.9 %copy-start.7 = (f32[96,512]{1,0:T(8,128)S(1)}, f32[96,512]{1,0:T(8,128)}, u32[]{:S(2)}) copy-start(f32[96,512]{1,0:T(8,128)} %copy-done.6) | copy-start | bytes 589828
  83.3 1.1 %copy-start.1 = (f32[4,96,512]{2,1,0:T(8,128)S(1)}, f32[4,96,512]{2,1,0:T(8,128)}, u32[]{:S(2)}) copy-start(f32[4,96,512]{2,1,0:T(8,128)} %copy-done) | copy-start | bytes 2359300
  84.4 1.0 %copy-start.3 = (f32[2,96,512]{2,1,0:T(8,128)S(1)}, f32[2,96,512]{2,1,0:T(8,128)}, u32[]{:S(2)}) copy-start(f32[2,96,512]{2,1,0:T(8,128)} %copy-done.2) | copy-start | bytes 1179652
  85.4 2.9 %copy-start.33 = (f32[2,8]{1,0:T(2,128)S(1)}, f32[2,8]{1,0:T(2,128)}, u32[]{:S(2)}) copy-start(f32[2,8]{1,0:T(2,128)} %table.3) | copy-start | bytes 196
  85.4 2.9 %copy-start.34 = (f32[2,8]{1,0:T(2,128)S(1)}, f32[2,8]{1,0:T(2,128)}, u32[]{:S(2)}) copy-start(f32[2,8]{1,0:T(2,128)} %table.2) | copy-start | bytes 196

commit v6 on v5

--- a/solution.py
+++ b/solution.py
@@ -228,14 +228,14 @@
         via[1, rows, :] = mean(one, two)
         return carry
 
-    lax.fori_loop(0, n_rows // STEP, fill, 0, unroll=4)
+    lax.fori_loop(0, n_rows // STEP, fill, 0, unroll=8)
 
     def copy(k, carry):
         first[block(k), :] = via[0, block(k + (1 - group) * half), :]
         lone[block(k), :] = via[0, block(k + group * half), :]
         return carry
 
-    lax.fori_loop(0, half, copy, 0, unroll=4)
+    lax.fori_loop(0, half, copy, 0, unroll=12)
 
 
 def plane_kernel(gz, table, classes, load, sink, pad, via, plane, drawn, three, top, bottom):
@@ -252,7 +252,7 @@
         drawn[rows, :] = sink[rows, :].astype(jnp.float32) * load[rows, :]
         return carry
 
-    lax.fori_loop(0, n_rows // STEP, fill, 0, unroll=4)
+    lax.fori_loop(0, n_rows // STEP, fill, 0, unroll=8)
 
     def copy(k, carry):
         rows = block(k + (1 - group) * half)
@@ -261,7 +261,7 @@
         three[2, block(k), :] = via[1, rows, :]
         return carry
 
-    lax.fori_loop(0, half, copy, 0, unroll=4)
+    lax.fori_loop(0, half, copy, 0, unroll=12)
     for f in range(N_OWN):
         at = pl.ds(DEEP * f, DEEP)
         top[at, :] = field_rows(plane, via, drawn, f, pl.ds(0, DEEP))
@@ -302,7 +302,7 @@
         return carry
 
     put(pl.ds(0, STEP), lambda f: tile_of(south, f, True))
-    lax.fori_loop(0, n_rows // STEP, inner, 0, unroll=2)
+    lax.fori_loop(0, n_rows // STEP, inner, 0, unroll=8)
     put(pl.ds(n_rows + STEP, STEP), lambda f: tile_of(north, f, False))
     rest = n_rows + 2 * STEP
     stage[rest:, :] = jnp.zeros((stage.shape[0] - rest, LANES), jnp.float32)
@@ -353,30 +353,10 @@
     return jnp.where(sub == edge, outer, inner)
 
 
-def edge_loop(wide, start, count, done):
-    last = wide.shape[1] // STEP - 1
-
-    def body(k, carried):
-        kept = []
-        for layer in range(2):
-            value = wide[layer, block(start + k), :]
-            over = wide[layer, block(jnp.minimum(start + k + 1, last)), :]
-            above = joined(STEP - 1, rows_up(value), rows_up(over))
-            to_east, to_north = mean(value, eastward(value)), mean(value, above)
-            down = rows_down(to_north)
-            south = joined(0, down, carried[layer])
-            kept.append(down)
-            done(layer, k, to_east, to_north, (to_east + westward(to_east)) + (to_north + south))
-        return tuple(kept)
-
-    none = jnp.zeros((STEP, wide.shape[2]), jnp.float32)
-    lax.fori_loop(0, count, body, (none, none), unroll=2)
-
-
 def own_kernel(gz, plane, via, drawn, south, north, west, east, near, edge_e, edge_n, near_sum, far_sum, wide, flat, tall):
     group = gz[0]
     n_rows, n_cols = drawn.shape
-    half = n_rows // 2 // STEP
+    half, last = n_rows // 2 // STEP, n_rows // STEP + 1
     flat[...] = jnp.zeros(flat.shape, jnp.float32)
     for f in range(N_OWN):
         at = 2 * DEEP * f
@@ -384,51 +364,55 @@
         flat[at + DEEP : at + 2 * DEEP, :] = east[DEEP * f : DEEP * f + DEEP, :]
     tall[...] = flat[...].T
 
-    def put(target, index, rows, value, strip, f):
-        target[index, rows, :n_cols] = value
-        target[index, rows, n_cols:] = side(strip, f, 1.0 if f < N_FAR else 0.0)
-
-    def inner(k, carry):
-        rows = block(k + 1)
+    def put(rows, pick):
         strip = tall[rows, :]
         for f in range(2):
-            put(wide, f, rows, plane[f, block(k), :], strip, f)
+            wide[f, rows, :n_cols] = pick(f)
+            wide[f, rows, n_cols:] = side(strip, f, 1.0)
+
+    def inner(k, carry):
+        put(block(k + 1), lambda f: plane[f, block(k), :])
         return carry
 
-    ends = (pl.ds(0, STEP), south, True), (pl.ds(n_rows + STEP, STEP), north, False)
-    for rows, stack, upper in ends:
-        for f in range(2):
-            put(wide, f, rows, tile_of(stack, f, upper), tall[rows, :], f)
-    lax.fori_loop(0, n_rows // STEP, inner, 0, unroll=2)
-
-    def rest(k, carry):
-        at = block(k + group * half)
-        strip = tall[block(k + 1 + group * half), :]
-        for f in range(2, N_OWN):
-            put(near, f - 2, block(k + 1), field_rows(plane, via, drawn, f, at), strip, f)
+    put(pl.ds(0, STEP), lambda f: tile_of(south, f, True))
+    lax.fori_loop(0, n_rows // STEP, inner, 0, unroll=8)
+    put(pl.ds(n_rows + STEP, STEP), lambda f: tile_of(north, f, False))
+
+    def around(layer, k):
+        value = wide[layer, block(k), :]
+        over = wide[layer, block(jnp.minimum(k + 1, last)), :]
+        under = wide[layer, block(jnp.maximum(k - 1, 0)), :]
+        above = joined(STEP - 1, rows_up(value), rows_up(over))
+        below = joined(0, rows_down(value), rows_down(under))
+        to_east, to_north = mean(value, eastward(value)), mean(value, above)
+        return to_east, to_north, (to_east + westward(to_east)) + (to_north + mean(value, below))
+
+    def frame(k, carry):
+        at = k + group * half
+        for layer in range(2):
+            to_east, to_north, total = around(layer, at)
+            edge_e[layer, block(k), :] = to_east
+            edge_n[layer, block(k), :] = to_north
+            near_sum[layer, block(k), :] = total
+        strip = tall[block(at), :]
+        inside = block(jnp.clip(at - 1, 0, last - 2))
+        for place, f in enumerate((2, 3, 4, 5)):
+            core = field_rows(plane, via, drawn, f, inside)
+            core = jnp.where(at == 0, tile_of(south, f, True), core)
+            core = jnp.where(at == last, tile_of(north, f, False), core)
+            near[place, block(k), :n_cols] = core
+            near[place, block(k), n_cols:] = side(strip, f, 1.0 if f < N_FAR else 0.0)
         return carry
 
-    lax.fori_loop(0, half, rest, 0, unroll=2)
-    for f in range(2, N_OWN):
-        value = field_rows(plane, via, drawn, f, pl.ds((half - 1) * STEP, STEP))
-        value = jnp.where(group == 0, tile_of(south, f, True), value)
-        put(near, f - 2, pl.ds(0, STEP), value, tall[block(group * half), :], f)
-        value = field_rows(plane, via, drawn, f, pl.ds(half * STEP, STEP))
-        value = jnp.where(group == 1, tile_of(north, f, False), value)
-        strip = tall[block(half + 1 + group * half), :]
-        put(near, f - 2, pl.ds((half + 1) * STEP, STEP), value, strip, f)
-
-    def done(layer, k, to_east, to_north, total):
-        edge_e[layer, block(k), :] = to_east
-        edge_n[layer, block(k), :] = to_north
-        near_sum[layer, block(k), :] = total
-
-    edge_loop(wide, group * half, half + 2, done)
-
-    def other(layer, k, to_east, to_north, total):
-        far_sum[layer, block(jnp.maximum(k - 1, 0)), :] = total[:, :n_cols]
-
-    edge_loop(wide, (1 - group) * half, half + 1, other)
+    lax.fori_loop(0, half + 2, frame, 0, unroll=7)
+
+    def other(k, carry):
+        for layer in range(2):
+            total = around(layer, k + 1 + (1 - group) * half)[2]
+            far_sum[layer, block(k), :] = total[:, :n_cols]
+        return carry
+
+    lax.fori_loop(0, half, other, 0, unroll=6)
 
 
 def fold(total):
@@ -624,8 +608,11 @@
     part = before[...]
     for j in range(3):
         part = jnp.where(row == 3 + j, fold(sums[j]), part)
+    sums = jnp.sum(part, axis=1, keepdims=True)
+    lane = lax.broadcasted_iota(jnp.int32, part.shape, 1)
+    line = jnp.sum(jnp.where(lane == row, sums, 0.0), axis=0, keepdims=True)
     for k in range(spread.shape[0]):
-        spread[k] = part
+        spread[k] = line
 
 
 def inverse_kernel(gz, plane, via, sums, given, inverse):
@@ -660,8 +647,8 @@
 
 
 def solve(parts):
-    sums = jnp.sum(tree(parts), axis=1, keepdims=True)
-    g = [jnp.broadcast_to(sums[k : k + 1, :], (1, LANES)) for k in range(6)]
+    sums = tree(parts)
+    g = [jnp.broadcast_to(sums[:, k : k + 1], (1, LANES)) for k in range(6)]
     step = [g[k] - g[k + 1] for k in range(5)]
     scale = [lax.rsqrt(g[0]), lax.rsqrt(g[2]), lax.rsqrt(g[4])]
 
@@ -685,9 +672,11 @@
     return (c0, c1, c2, 1.0 - c0, c0 - c1, c1 - c2), good
 
 
-def combine_kernel(gz, parts, current, inv_near, inv_far, n_0, n_0_far, n_12, n_12_far, volts, left, flag, volts_here, left_here, sems):
+def combine_kernel(gz, far_0, parts, current, inv_near, inv_far, n_0, n_12, n_12_far, volts, left, flag, volts_here, left_here, n_0_far, sems):
     group = gz[0]
     half, n_cols = n_0.shape[1:]
+    bring = pltpu.make_async_copy(far_0, n_0_far, sems.at[4])
+    bring.start()
     values, good = solve(parts)
     flag[...] = jnp.where(good, 1, 0)
     c = [jnp.broadcast_to(value[:, 0:1], (STEP, n_cols)) for value in values]
@@ -707,34 +696,32 @@
             left_here[group, at, :] = c[3] * drawn + c[4] * n0o + c[5] * n1o + c[2] * n2o
             return carry
 
-        lax.fori_loop(0, half // STEP, body, 0, unroll=2)
+        lax.fori_loop(0, half // STEP, body, 0, unroll=6)
 
     copies = []
-    for part in range(2):
-
-        @pl.when(group == part)
-        def _(part=part):
-            fill(part, inv_near, n_0, n_12)
-
-        @pl.when(group != part)
-        def _(part=part):
-            fill(part, inv_far, n_0_far, n_12_far)
-
+
+    def put_out(part, first_sem):
+        rows = pl.ds(pl.multiple_of(part * half, STEP), half)
         for j, (source, target) in enumerate(((volts_here, volts), (left_here, left))):
-            rows = pl.ds(part * half, half)
             copy = pltpu.make_async_copy(
-                source.at[:, rows, :], target.at[:, rows, :], sems.at[2 * part + j]
+                source.at[:, rows, :], target.at[:, rows, :], sems.at[first_sem + j]
             )
             copy.start()
             copies.append(copy)
+
+    fill(group, inv_near, n_0, n_12)
+    put_out(group, 0)
+    bring.wait()
+    fill(1 - group, inv_far, n_0_far, n_12_far)
+    put_out(1 - group, 2)
     for copy in copies:
         copy.wait()
 
 
-def call(kernel, outs, scratch, n_smem, *args, outside=0):
+def call(kernel, outs, scratch, n_smem, *args, outside=0, far=0):
     return pl.pallas_call(
         kernel,
-        in_specs=[SMEM] * n_smem + [VMEM] * (len(args) - n_smem),
+        in_specs=[SMEM] * n_smem + [OUTSIDE] * far + [VMEM] * (len(args) - n_smem - far),
         out_specs=[OUTSIDE] * outside + [VMEM] * (len(outs) - outside),
         out_shape=outs,
         scratch_shapes=scratch,
@@ -813,19 +800,20 @@
     )
     n_12, send, spread = call(
         steps_kernel,
-        [array(4, half, n_cols), array(4, half, n_cols), array(n_gx, STEP, LANES)],
+        [array(4, half, n_cols), array(4, half, n_cols), array(n_gx, 1, LANES)],
         [pltpu.VMEM((4, frame, broad), jnp.float32)],
         0, step_1, near_e, near_n, far_e, far_n, cross, inverse, part,
     )
     n_12_far = lax.ppermute(send, "gz", swap)
     parts = lax.all_to_all(spread, GX, 0, 0, tiled=True)
-    (spread,) = call(relay_kernel, [array(n_rest, STEP, LANES)], [], 0, parts)
+    (spread,) = call(relay_kernel, [array(n_rest, 1, LANES)], [], 0, parts)
     parts = lax.all_to_all(spread, rest, 0, 0, tiled=True)
     volts, left, flag = call(
         combine_kernel,
         [array(2, n_rows, n_cols)] * 2 + [jax.ShapeDtypeStruct((1, LANES), jnp.int32)],
-        [pltpu.VMEM((2, n_rows, n_cols), jnp.float32)] * 2 + [pltpu.SemaphoreType.DMA((4,))],
-        1, gz, parts, drawn, inv_near, inv_far, n_0, n_0_far, n_12, n_12_far, outside=2,
+        [pltpu.VMEM((2, n_rows, n_cols), jnp.float32)] * 2
+        + [pltpu.VMEM((2, half, n_cols), jnp.float32), pltpu.SemaphoreType.DMA((5,))],
+        1, gz, n_0_far, parts, drawn, inv_near, inv_far, n_0, n_12, n_12_far, outside=2, far=1,
     )
 
     def careful():

time: 89.8 us -> 88.2 us (0.982)
  the two profiles are of different devices: /device:TPU:1 before, /device:TPU:97 now
where the time goes in v6:
time: 88.2 us; the launch traced here: 87.8 us
  waiting for transfers between devices  36.6 us (41%)
  starting transfers between devices  17 us (19%)
  Pallas kernels  16.5 us (19%)
  blocking collectives  10.1 us (11%)
  local copies, waits for them, and re-layouts  6.38 us (7%)
  between operations  0.97 us (1%)
    ppermute x1, waiting for transfers between devices, shards(): south = lax.ppermute(bottom, GY, ring(GY))  17.2 us
    pallas_call x10, Pallas kernels, call(): pl.pallas_call(kernel, in_specs=[SMEM] * n_smem + [OUTSIDE] * far + [VMEM...  16.5 us
    ppermute x1, waiting for transfers between devices, shards(): via_far = lax.ppermute(via_send, 'gz', swap)  14.2 us
    all_to_all x1, blocking collectives, shards(): parts = lax.all_to_all(spread, GX, 0, 0, tiled=True)  10.1 us
    unnamed x22, local copies, waits for them, and re-layouts  6.38 us
    ppermute x1, starting transfers between devices, shards(): west = lax.ppermute(last, GX, ring(GX))  4.57 us
    ppermute x1, starting transfers between devices, shards(): north = lax.ppermute(top, GY, back(ring(GY)))  3.9 us
    ppermute x1, waiting for transfers between devices, shards(): east = lax.ppermute(first, GX, back(ring(GX)))  3.52 us
  transfers between devices with their start and end apart: 11, of which 5 were waited for; matrix products, arithmetic and copies ran while one was open for 0% of the time, Pallas kernels for 4%

profile of v6, /device:TPU:97, one launch (start us, length us, event | category | flops | bytes accessed | tf_op | source)
XLA Modules:
  0.0 87.8 jit_solution(7520122170854762712)
XLA Ops:
  0.6 2.5 %shard_map.90 = (f32[2,192,512]{2,1,0:T(8,128)S(1)}, f32[96,512]{1,0:T(8,128)S(1)}, f32[96,512]{1,0:T(8,128)}) custom-call(s32[1]{0:T(128)} %bitcast.23.gz, f32[2,8]{1,0:T(2,128)} %table.2, s32[2,192,512]{2,1,0:T(8,128)} %classes.2), custom_call_target="tpu_custom_call" | custom-call | tf_op jit(solution)/shard_map/pallas_call | solution.py:722
  3.1 1.9 %shard_map.91 = (f32[3,192,512]{2,1,0:T(8,128)S(1)}, f32[192,512]{1,0:T(8,128)S(1)}, f32[3,96,512]{2,1,0:T(8,128)S(1)}, f32[24,512]{1,0:T(8,128)S(1)}, f32[24,512]{1,0:T(8,128)S(1)}) custom-call(s32[1]{0:T(128)} %bitcast.23.gz, f32[2,8]{1,0:T(2,128)} %table.3, s32[2,192,512]{2,1,0:T(8,128)S(1)} %copy-done.27, f32[192,512]{1,0:T(8,128)} %load.1, ...), custom_call_target="tpu_custom_call" | custom-call | tf_op jit(solution)/shard_map/pallas_call | solution.py:722
  5.0 1.3 %collective-permute-start.28 = (f32[3,96,512]{2,1,0:T(8,128)S(1)}, f32[3,96,512]{2,1,0:T(8,128)S(1)}, u32[]{:S(2)}, u32[]{:S(2)}) collective-permute-start(f32[3,96,512]{2,1,0:T(8,128)S(1)} %get-tuple-element.68), channel_id=1, source_target_pairs={{0,1},{1,0},{2,3},{3,2},{4,5},{5,4},{6,7},{7,6},{8,9},{9,8},{10,11... | collective-permute-start | bytes 1769480 | tf_op jit(solution)/shard_map/ppermute | solution.py:768
  6.5 1.3 %collective-permute-start.24 = (f32[24,512]{1,0:T(8,128)S(1)}, f32[24,512]{1,0:T(8,128)S(1)}, u32[]{:S(2)}, u32[]{:S(2)}) collective-permute-start(f32[24,512]{1,0:T(8,128)S(1)} %get-tuple-element.60), channel_id=1, source_target_pairs={{0,2},{2,4},{4,6},{6,8},{8,10},{10,12},{12,14},{14,0},{1,3},{3,5},... | collective-permute-start | bytes 147464 | tf_op jit(solution)/shard_map/ppermute | solution.py:766
  7.8 3.9 %collective-permute-start.25 = (f32[24,512]{1,0:T(8,128)S(1)}, f32[24,512]{1,0:T(8,128)S(1)}, u32[]{:S(2)}, u32[]{:S(2)}) collective-permute-start(f32[24,512]{1,0:T(8,128)S(1)} %get-tuple-element.61), channel_id=1, source_target_pairs={{2,0},{4,2},{6,4},{8,6},{10,8},{12,10},{14,12},{0,14},{3,1},{5,3},... | collective-permute-start | bytes 147464 | tf_op jit(solution)/shard_map/ppermute | solution.py:767
  11.7 17.2 %collective-permute-done.24.south = f32[24,512]{1,0:T(8,128)S(1)} collective-permute-done((f32[24,512]{1,0:T(8,128)S(1)}, f32[24,512]{1,0:T(8,128)S(1)}, u32[]{:S(2)}, u32[]{:S(2)}) %collective-permute-start.24) | collective-permute-done | bytes 49184 | tf_op jit(solution)/shard_map/ppermute | solution.py:766
  29.6 4.6 %collective-permute-start.26 = (f32[24,256]{1,0:T(8,128)S(1)}, f32[24,256]{1,0:T(8,128)S(1)}, u32[]{:S(2)}, u32[]{:S(2)}) collective-permute-start(f32[24,256]{1,0:T(8,128)S(1)} %get-tuple-element.62), channel_id=1, source_target_pairs={{0,16},{16,32},{32,48},{48,64},{64,80},{80,96},{96,112},{112,128},... | collective-permute-start | bytes 73736 | tf_op jit(solution)/shard_map/ppermute | solution.py:773
  34.1 0.9 %collective-permute-done.26.west = f32[24,256]{1,0:T(8,128)S(1)} collective-permute-done((f32[24,256]{1,0:T(8,128)S(1)}, f32[24,256]{1,0:T(8,128)S(1)}, u32[]{:S(2)}, u32[]{:S(2)}) %collective-permute-start.26) | collective-permute-done | bytes 24608 | tf_op jit(solution)/shard_map/ppermute | solution.py:773
  35.1 3.5 %collective-permute-done.27.east = f32[24,256]{1,0:T(8,128)S(1)} collective-permute-done((f32[24,256]{1,0:T(8,128)S(1)}, f32[24,256]{1,0:T(8,128)S(1)}, u32[]{:S(2)}, u32[]{:S(2)}) %collective-permute-start.27) | collective-permute-done | bytes 24608 | tf_op jit(solution)/shard_map/ppermute | solution.py:774
  38.7 1.9 %shard_map.93 = (f32[4,112,640]{2,1,0:T(8,128)S(1)}, f32[2,112,640]{2,1,0:T(8,128)S(1)}, f32[2,112,640]{2,1,0:T(8,128)S(1)}, f32[2,112,640]{2,1,0:T(8,128)S(1)}, f32[2,96,512]{2,1,0:T(8,128)S(1)}) custom-call(s32[1]{0:T(128)} %bitcast.23.gz, f32[3,192,512]{2,1,0:T(8,128)S(1)} %get-tuple-element.58.plane, f32[2,192,512]{2,1,0:T(8,128)S(1)} %get-tuple-element.57.via, ...), custom_call_target="tpu_custom_call" | custom-call | tf_op jit(solution)/shard_map/pallas_call | solution.py:722
  40.6 0.8 copy-done.4
  41.4 0.8 collective-permute-done.30.small
  42.2 3.2 %shard_map.95 = (f32[2,112,640]{2,1,0:T(8,128)S(1)}, f32[2,112,640]{2,1,0:T(8,128)S(1)}, f32[112,640]{1,0:T(8,128)S(1)}, f32[6,112,640]{2,1,0:T(8,128)S(1)}, f32...) custom-call(s32[1]{0:T(128)} %bitcast.23.gz, ...), custom_call_target="tpu_custom_call" | custom-call | tf_op jit(solution)/shard_map/pallas_call | solution.py:722
  45.4 2.3 %shard_map.96 = (f32[4,96,512]{2,1,0:T(8,128)S(1)}, f32[4,96,512]{2,1,0:T(8,128)}, f32[16,1,128]{2,1,0:T(1,128)S(1)}) custom-call(f32[4,112,640]{2,1,0:T(8,128)S(1)} %get-tuple-element.71.step_1, f32[2,112,640]{2,1,0:T(8,128)S(1)} %get-tuple-element.65.near_e, f32[2,112,640]{2,1,0:T(8,128)S(1)} %get-tuple-element.66.near_n, ...), custom_call_target="tpu_custom_call" | custom-call | tf_op jit(solution)/shard_map/pallas_call | solution.py:722
  47.7 0.9 copy-done
  49.2 0.8 collective-permute-start.31
  50.7 10.1 %all_to_all.10.parts = f32[16,1,128]{2,1,0:T(1,128)S(1)} all-to-all(f32[16,1,128]{2,1,0:T(1,128)S(1)} %get-tuple-element.77), channel_id=1, replica_groups=mesh['gx_0'=8,'gx_1'=2,'gy_0'=2,'gy_1'=4,'gz'=2] {'gx_0','gx_1'}, dimensions={0} | all-to-all | bytes 16384 | tf_op jit(solution)/shard_map/all_to_all | solution.py:808
  61.4 3.5 %all-to-all-start.1 = ((f32[16,1,128]{2,1,0:T(1,128)}), f32[16,1,128]{2,1,0:T(1,128)S(1)}, u32[]{:S(2)}, u32[]{:S(2)}) async-start(f32[16,1,128]{2,1,0:T(1,128)} %shard_map.97), calls=%async_computation.1 | async-start | bytes 16384 | tf_op jit(solution)/shard_map/all_to_all | solution.py:810
  64.9 14.2 %collective-permute-done.32.given = f32[96,512]{1,0:T(8,128)S(1)} collective-permute-done((f32[96,512]{1,0:T(8,128)}, f32[96,512]{1,0:T(8,128)S(1)}, u32[]{:S(2)}, u32[]{:S(2)}) %collective-permute-start.32) | collective-permute-done | bytes 196640 | tf_op jit(solution)/shard_map/ppermute | solution.py:780
  79.8 1.0 %copy-done.5 = f32[2,96,512]{2,1,0:T(8,128)S(1)} copy-done((f32[2,96,512]{2,1,0:T(8,128)S(1)}, f32[2,96,512]{2,1,0:T(8,128)}, u32[]{:S(2)}) %copy-start.5) | copy-done | bytes 393240
  80.8 0.9 %copy-done.7 = f32[96,512]{1,0:T(8,128)S(1)} copy-done((f32[96,512]{1,0:T(8,128)S(1)}, f32[96,512]{1,0:T(8,128)}, u32[]{:S(2)}) %copy-start.7) | copy-done | bytes 196632
  81.9 1.1 %copy-done.1 = f32[4,96,512]{2,1,0:T(8,128)S(1)} copy-done((f32[4,96,512]{2,1,0:T(8,128)S(1)}, f32[4,96,512]{2,1,0:T(8,128)}, u32[]{:S(2)}) %copy-start.1) | copy-done | bytes 786456
  83.0 1.0 %copy-done.3 = f32[2,96,512]{2,1,0:T(8,128)S(1)} copy-done((f32[2,96,512]{2,1,0:T(8,128)S(1)}, f32[2,96,512]{2,1,0:T(8,128)}, u32[]{:S(2)}) %copy-start.3) | copy-done | bytes 393240
  84.0 3.3 %shard_map.99 = (f32[2,192,512]{2,1,0:T(8,128)}, f32[2,192,512]{2,1,0:T(8,128)}, s32[1,128]{1,0:T(1,128)S(1)}) custom-call(s32[1]{0:T(128)} %bitcast.23.gz, f32[2,96,512]{2,1,0:T(8,128)} %collective-permute-done.31.far_0, f32[16,1,128]{2,1,0:T(1,128)S(1)} %all-to-all-done.1.parts, f32[192,512]{1,0:T(8,128)S(1)} %get-tuple-element.59.drawn.current, ...), custom_call_target="tpu_custom_call" | custom-call | tf_op jit(solution)/shard_map/pallas_call | solution.py:722
  (32 shorter events, 4.1 us)
Async XLA Ops:
  0.6 2.5 %copy-start.27 = (s32[2,192,512]{2,1,0:T(8,128)S(1)}, s32[2,192,512]{2,1,0:T(8,128)}, u32[]{:S(2)}) copy-start(s32[2,192,512]{2,1,0:T(8,128)} %classes.3) | copy-start | bytes 2359300
  5.0 37.2 %collective-permute-start.28 = (f32[3,96,512]{2,1,0:T(8,128)S(1)}, f32[3,96,512]{2,1,0:T(8,128)S(1)}, u32[]{:S(2)}, u32[]{:S(2)}) collective-permute-start(f32[3,96,512]{2,1,0:T(8,128)S(1)} %get-tuple-element.68), channel_id=1, source_target_pairs={{0,1},{1,0},{2,3},{3,2},{4,5},{5,4},{6,7},{7,6},{8,9},{9,8},{10,11... | collective-permute-start | bytes 1769480 | tf_op jit(solution)/shard_map/ppermute | solution.py:768
  6.3 35.9 %collective-permute-start.29 = (f32[96,512]{1,0:T(8,128)S(1)}, f32[96,512]{1,0:T(8,128)S(1)}, u32[]{:S(2)}, u32[]{:S(2)}) collective-permute-start(f32[96,512]{1,0:T(8,128)S(1)} %get-tuple-element.69), channel_id=1, source_target_pairs={{0,1},{1,0},{2,3},{3,2},{4,5},{5,4},{6,7},{7,6},{8,9},{9,8},{10,11... | collective-permute-start | bytes 589832 | tf_op jit(solution)/shard_map/ppermute | solution.py:759
  6.5 22.4 %collective-permute-start.24 = (f32[24,512]{1,0:T(8,128)S(1)}, f32[24,512]{1,0:T(8,128)S(1)}, u32[]{:S(2)}, u32[]{:S(2)}) collective-permute-start(f32[24,512]{1,0:T(8,128)S(1)} %get-tuple-element.60), channel_id=1, source_target_pairs={{0,2},{2,4},{4,6},{6,8},{8,10},{10,12},{12,14},{14,0},{1,3},{3,5},... | collective-permute-start | bytes 147464 | tf_op jit(solution)/shard_map/ppermute | solution.py:766
  7.8 21.1 %collective-permute-start.25 = (f32[24,512]{1,0:T(8,128)S(1)}, f32[24,512]{1,0:T(8,128)S(1)}, u32[]{:S(2)}, u32[]{:S(2)}) collective-permute-start(f32[24,512]{1,0:T(8,128)S(1)} %get-tuple-element.61), channel_id=1, source_target_pairs={{2,0},{4,2},{6,4},{8,6},{10,8},{12,10},{14,12},{0,14},{3,1},{5,3},... | collective-permute-start | bytes 147464 | tf_op jit(solution)/shard_map/ppermute | solution.py:767
  29.6 5.5 %collective-permute-start.26 = (f32[24,256]{1,0:T(8,128)S(1)}, f32[24,256]{1,0:T(8,128)S(1)}, u32[]{:S(2)}, u32[]{:S(2)}) collective-permute-start(f32[24,256]{1,0:T(8,128)S(1)} %get-tuple-element.62), channel_id=1, source_target_pairs={{0,16},{16,32},{32,48},{48,64},{64,80},{80,96},{96,112},{112,128},... | collective-permute-start | bytes 73736 | tf_op jit(solution)/shard_map/ppermute | solution.py:773
  34.1 4.5 %collective-permute-start.27 = (f32[24,256]{1,0:T(8,128)S(1)}, f32[24,256]{1,0:T(8,128)S(1)}, u32[]{:S(2)}, u32[]{:S(2)}) collective-permute-start(f32[24,256]{1,0:T(8,128)S(1)} %get-tuple-element.63), channel_id=1, source_target_pairs={{16,0},{32,16},{48,32},{64,48},{80,64},{96,80},{112,96},{128,112},... | collective-permute-start | bytes 73736 | tf_op jit(solution)/shard_map/ppermute | solution.py:774
  38.6 3.6 %collective-permute-start.30 = (f32[48,512]{1,0:T(8,128)S(1)}, f32[48,512]{1,0:T(8,128)S(1)}, u32[]{:S(2)}, u32[]{:S(2)}) collective-permute-start(f32[48,512]{1,0:T(8,128)S(1)} %shard_map.94), channel_id=1, source_target_pairs={{0,1},{1,0},{2,3},{3,2},{4,5},{5,4},{6,7},{7,6},{8,9},{9,8},{10,11... | collective-permute-start | bytes 294920 | tf_op jit(solution)/shard_map/ppermute | solution.py:779
  40.6 0.8 copy-start.4
  45.4 2.3 %copy-start.2 = (f32[2,96,512]{2,1,0:T(8,128)}, f32[2,96,512]{2,1,0:T(8,128)S(1)}, u32[]{:S(2)}) copy-start(f32[2,96,512]{2,1,0:T(8,128)S(1)} %get-tuple-element.81.n_0) | copy-start | bytes 1179652
  47.7 0.9 %copy-start = (f32[4,96,512]{2,1,0:T(8,128)}, f32[4,96,512]{2,1,0:T(8,128)S(1)}, u32[]{:S(2)}) copy-start(f32[4,96,512]{2,1,0:T(8,128)S(1)} %get-tuple-element.82.n_12) | copy-start | bytes 2359300
  48.6 33.3 %collective-permute-start.33 = (f32[4,96,512]{2,1,0:T(8,128)}, f32[4,96,512]{2,1,0:T(8,128)}, u32[]{:S(2)}, u32[]{:S(2)}) collective-permute-start(f32[4,96,512]{2,1,0:T(8,128)} %get-tuple-element.83), channel_id=1, source_target_pairs={{0,1},{1,0},{2,3},{3,2},{4,5},{5,4},{6,7},{7,6},{8,9},{9,8},{10,11... | collective-permute-start | bytes 2359304 | tf_op jit(solution)/shard_map/ppermute | solution.py:807
  49.2 32.6 %collective-permute-start.31 = (f32[2,96,512]{2,1,0:T(8,128)}, f32[2,96,512]{2,1,0:T(8,128)}, u32[]{:S(2)}, u32[]{:S(2)}) collective-permute-start(f32[2,96,512]{2,1,0:T(8,128)} %get-tuple-element.70), channel_id=1, source_target_pairs={{0,1},{1,0},{2,3},{3,2},{4,5},{5,4},{6,7},{7,6},{8,9},{9,8},{10,11... | collective-permute-start | bytes 1179656 | tf_op jit(solution)/shard_map/ppermute | solution.py:796
  50.0 29.0 %collective-permute-start.32 = (f32[96,512]{1,0:T(8,128)}, f32[96,512]{1,0:T(8,128)S(1)}, u32[]{:S(2)}, u32[]{:S(2)}) collective-permute-start(f32[96,512]{1,0:T(8,128)} %get-tuple-element.80), channel_id=1, source_target_pairs={{0,1},{1,0},{2,3},{3,2},{4,5},{5,4},{6,7},{7,6},{8,9},{9,8},{10,11... | collective-permute-start | bytes 589832 | tf_op jit(solution)/shard_map/ppermute | solution.py:780
  61.4 20.5 %all-to-all-start.1 = ((f32[16,1,128]{2,1,0:T(1,128)}), f32[16,1,128]{2,1,0:T(1,128)S(1)}, u32[]{:S(2)}, u32[]{:S(2)}) async-start(f32[16,1,128]{2,1,0:T(1,128)} %shard_map.97), calls=%async_computation.1 | async-start | bytes 16384 | tf_op jit(solution)/shard_map/all_to_all | solution.py:810
  79.1 0.7 copy-start.6
  79.8 1.0 %copy-start.5 = (f32[2,96,512]{2,1,0:T(8,128)S(1)}, f32[2,96,512]{2,1,0:T(8,128)}, u32[]{:S(2)}) copy-start(f32[2,96,512]{2,1,0:T(8,128)} %copy-done.4) | copy-start | bytes 1179652
  80.8 0.9 %copy-start.7 = (f32[96,512]{1,0:T(8,128)S(1)}, f32[96,512]{1,0:T(8,128)}, u32[]{:S(2)}) copy-start(f32[96,512]{1,0:T(8,128)} %copy-done.6) | copy-start | bytes 589828
  81.9 1.1 %copy-start.1 = (f32[4,96,512]{2,1,0:T(8,128)S(1)}, f32[4,96,512]{2,1,0:T(8,128)}, u32[]{:S(2)}) copy-start(f32[4,96,512]{2,1,0:T(8,128)} %copy-done) | copy-start | bytes 2359300
  83.0 1.0 %copy-start.3 = (f32[2,96,512]{2,1,0:T(8,128)S(1)}, f32[2,96,512]{2,1,0:T(8,128)}, u32[]{:S(2)}) copy-start(f32[2,96,512]{2,1,0:T(8,128)} %copy-done.2) | copy-start | bytes 1179652
  84.0 3.3 %copy-start.33 = (f32[2,8]{1,0:T(2,128)S(1)}, f32[2,8]{1,0:T(2,128)}, u32[]{:S(2)}) copy-start(f32[2,8]{1,0:T(2,128)} %table.3) | copy-start | bytes 196
  84.0 3.3 %copy-start.34 = (f32[2,8]{1,0:T(2,128)S(1)}, f32[2,8]{1,0:T(2,128)}, u32[]{:S(2)}) copy-start(f32[2,8]{1,0:T(2,128)} %table.2) | copy-start | bytes 196

commit v7 on v6

--- a/solution.py
+++ b/solution.py
@@ -230,12 +230,13 @@
 
     lax.fori_loop(0, n_rows // STEP, fill, 0, unroll=8)
 
-    def copy(k, carry):
-        first[block(k), :] = via[0, block(k + (1 - group) * half), :]
-        lone[block(k), :] = via[0, block(k + group * half), :]
-        return carry
-
-    lax.fori_loop(0, half, copy, 0, unroll=12)
+    head = first.shape[0] // STEP - half
+    for k in range(half):
+        first[k * STEP : k * STEP + STEP, :] = via[0, block(k + (1 - group) * half), :]
+        lone[k * STEP : k * STEP + STEP, :] = via[0, block(k + group * half), :]
+    for k in range(head):
+        rows = pl.ds((half + k) * STEP, STEP)
+        first[rows, :] = via[1, block(k + (1 - group) * half), :]
 
 
 def plane_kernel(gz, table, classes, load, sink, pad, via, plane, drawn, three, top, bottom):
@@ -254,14 +255,13 @@
 
     lax.fori_loop(0, n_rows // STEP, fill, 0, unroll=8)
 
-    def copy(k, carry):
+    head = 3 * half - three.shape[0] // STEP
+    for k in range(half):
         rows = block(k + (1 - group) * half)
         for f in range(2):
-            three[f, block(k), :] = plane[f, rows, :]
-        three[2, block(k), :] = via[1, rows, :]
-        return carry
-
-    lax.fori_loop(0, half, copy, 0, unroll=12)
+            three[pl.ds((f * half + k) * STEP, STEP), :] = plane[f, rows, :]
+        if k >= head:
+            three[pl.ds((2 * half + k - head) * STEP, STEP), :] = via[1, rows, :]
     for f in range(N_OWN):
         at = pl.ds(DEEP * f, DEEP)
         top[at, :] = field_rows(plane, via, drawn, f, pl.ds(0, DEEP))
@@ -491,7 +491,9 @@
 def edge_kernel(gz, near, near_e, near_n, near_sum, three, first, small, far_e, far_n, cross, inverse, step_1, n_own, inv_own, send, part, *scratch):
     fields, step_0, flat, tall = scratch
     group = gz[0]
-    half, n_cols = first.shape
+    n_cols = first.shape[1]
+    half = (first.shape[0] + three.shape[0]) // N_FAR
+    head = first.shape[0] - half
     n_blocks = half // STEP + 2
     tall_rows = tall.shape[0]
     flat[...] = jnp.zeros(flat.shape, jnp.float32)
@@ -505,7 +507,14 @@
         strip = tall[block(k + group * (half // STEP)), :]
         for f in range(N_FAR):
             if 0 < k < n_blocks - 1:
-                core = (first if f == 2 else three.at[min(f, 2)])[(k - 1) * STEP : k * STEP, :]
+                r = (k - 1) * STEP
+                stack, r = {
+                    0: (three, r),
+                    1: (three, half + r),
+                    2: (first, r),
+                    3: (first, half + r) if r < head else (three, 2 * half + r - head),
+                }[f]
+                core = stack[r : r + STEP, :]
             else:
                 core = pltpu.roll(small[2 * DEEP * f : 2 * DEEP * f + STEP, :], DEEP, 0)
             fields[f, rows, :n_cols] = core
@@ -734,6 +743,7 @@
     half, frame = n_rows // 2, n_rows // 2 + 2 * STEP
     tall = -(-(n_rows + 2 * STEP) // LANES) * LANES
     broad = n_cols + LANES
+    head = half * 6 // 12
 
     def array(*shape):
         return jax.ShapeDtypeStruct(shape, jnp.float32)
@@ -753,13 +763,13 @@
 
     via, one, via_send = call(
         via_kernel,
-        [array(2, n_rows, n_cols), array(half, n_cols), array(half, n_cols)],
+        [array(2, n_rows, n_cols), array(half + head, n_cols), array(half, n_cols)],
         [], 1, gz, via_table, via_class,
     )
     big_via = lax.ppermute(one, "gz", swap)
     plane, drawn, three, top, bottom = call(
         plane_kernel,
-        [array(3, n_rows, n_cols), array(n_rows, n_cols), array(3, half, n_cols)]
+        [array(3, n_rows, n_cols), array(n_rows, n_cols), array(3 * half - head, n_cols)]
         + [array(DEEP * N_OWN, n_cols)] * 2,
         [], 1, gz, plane_table, plane_class, load_current, sink_mask, pad_mask, via,
     )

time: 88.2 us -> 88.2 us (level)
  no operation moved by 1% of the time
where the time goes in v7:
time: 88.2 us; the launch traced here: 87.8 us
  waiting for transfers between devices  36.6 us (41%)
  starting transfers between devices  17 us (19%)
  Pallas kernels  16.5 us (19%)
  blocking collectives  10.1 us (11%)
  local copies, waits for them, and re-layouts  6.38 us (7%)
  between operations  0.97 us (1%)
    ppermute x1, waiting for transfers between devices, shards(): south = lax.ppermute(bottom, GY, ring(GY))  17.2 us
    pallas_call x10, Pallas kernels, call(): pl.pallas_call(kernel, in_specs=[SMEM] * n_smem + [OUTSIDE] * far + [VMEM...  16.5 us
    ppermute x1, waiting for transfers between devices, shards(): via_far = lax.ppermute(via_send, 'gz', swap)  14.2 us
    all_to_all x1, blocking collectives, shards(): parts = lax.all_to_all(spread, GX, 0, 0, tiled=True)  10.1 us
    unnamed x22, local copies, waits for them, and re-layouts  6.38 us
    ppermute x1, starting transfers between devices, shards(): west = lax.ppermute(last, GX, ring(GX))  4.57 us
    ppermute x1, starting transfers between devices, shards(): north = lax.ppermute(top, GY, back(ring(GY)))  3.9 us
    ppermute x1, waiting for transfers between devices, shards(): east = lax.ppermute(first, GX, back(ring(GX)))  3.52 us
  transfers between devices with their start and end apart: 11, of which 5 were waited for; matrix products, arithmetic and copies ran while one was open for 0% of the time, Pallas kernels for 4%

profile of v7, /device:TPU:97, one launch (start us, length us, event | category | flops | bytes accessed | tf_op | source)
XLA Modules:
  0.0 87.8 jit_solution(3835681233250477705)
XLA Ops:
  0.6 2.5 %shard_map.90 = (f32[2,192,512]{2,1,0:T(8,128)S(1)}, f32[144,512]{1,0:T(8,128)S(1)}, f32[96,512]{1,0:T(8,128)}) custom-call(s32[1]{0:T(128)} %bitcast.23.gz, f32[2,8]{1,0:T(2,128)} %table.2, s32[2,192,512]{2,1,0:T(8,128)} %classes.2), custom_call_target="tpu_custom_call" | custom-call | tf_op jit(solution)/shard_map/pallas_call | solution.py:731
  3.1 1.9 %shard_map.91 = (f32[3,192,512]{2,1,0:T(8,128)S(1)}, f32[192,512]{1,0:T(8,128)S(1)}, f32[240,512]{1,0:T(8,128)S(1)}, f32[24,512]{1,0:T(8,128)S(1)}, f32[24,512]{1,0:T(8,128)S(1)}) custom-call(s32[1]{0:T(128)} %bitcast.23.gz, f32[2,8]{1,0:T(2,128)} %table.3, s32[2,192,512]{2,1,0:T(8,128)S(1)} %copy-done.27, f32[192,512]{1,0:T(8,128)} %load.1, ...), custom_call_target="tpu_custom_call" | custom-call | tf_op jit(solution)/shard_map/pallas_call | solution.py:731
  5.0 1.3 %collective-permute-start.28 = (f32[240,512]{1,0:T(8,128)S(1)}, f32[240,512]{1,0:T(8,128)S(1)}, u32[]{:S(2)}, u32[]{:S(2)}) collective-permute-start(f32[240,512]{1,0:T(8,128)S(1)} %get-tuple-element.68), channel_id=1, source_target_pairs={{0,1},{1,0},{2,3},{3,2},{4,5},{5,4},{6,7},{7,6},{8,9},{9,8},{10,11... | collective-permute-start | bytes 1474568 | tf_op jit(solution)/shard_map/ppermute | solution.py:778
  6.5 1.3 %collective-permute-start.24 = (f32[24,512]{1,0:T(8,128)S(1)}, f32[24,512]{1,0:T(8,128)S(1)}, u32[]{:S(2)}, u32[]{:S(2)}) collective-permute-start(f32[24,512]{1,0:T(8,128)S(1)} %get-tuple-element.60), channel_id=1, source_target_pairs={{0,2},{2,4},{4,6},{6,8},{8,10},{10,12},{12,14},{14,0},{1,3},{3,5},... | collective-permute-start | bytes 147464 | tf_op jit(solution)/shard_map/ppermute | solution.py:776
  7.8 3.9 %collective-permute-start.25 = (f32[24,512]{1,0:T(8,128)S(1)}, f32[24,512]{1,0:T(8,128)S(1)}, u32[]{:S(2)}, u32[]{:S(2)}) collective-permute-start(f32[24,512]{1,0:T(8,128)S(1)} %get-tuple-element.61), channel_id=1, source_target_pairs={{2,0},{4,2},{6,4},{8,6},{10,8},{12,10},{14,12},{0,14},{3,1},{5,3},... | collective-permute-start | bytes 147464 | tf_op jit(solution)/shard_map/ppermute | solution.py:777
  11.7 17.2 %collective-permute-done.24.south = f32[24,512]{1,0:T(8,128)S(1)} collective-permute-done((f32[24,512]{1,0:T(8,128)S(1)}, f32[24,512]{1,0:T(8,128)S(1)}, u32[]{:S(2)}, u32[]{:S(2)}) %collective-permute-start.24) | collective-permute-done | bytes 49184 | tf_op jit(solution)/shard_map/ppermute | solution.py:776
  29.6 4.6 %collective-permute-start.26 = (f32[24,256]{1,0:T(8,128)S(1)}, f32[24,256]{1,0:T(8,128)S(1)}, u32[]{:S(2)}, u32[]{:S(2)}) collective-permute-start(f32[24,256]{1,0:T(8,128)S(1)} %get-tuple-element.62), channel_id=1, source_target_pairs={{0,16},{16,32},{32,48},{48,64},{64,80},{80,96},{96,112},{112,128},... | collective-permute-start | bytes 73736 | tf_op jit(solution)/shard_map/ppermute | solution.py:783
  34.1 0.9 %collective-permute-done.26.west = f32[24,256]{1,0:T(8,128)S(1)} collective-permute-done((f32[24,256]{1,0:T(8,128)S(1)}, f32[24,256]{1,0:T(8,128)S(1)}, u32[]{:S(2)}, u32[]{:S(2)}) %collective-permute-start.26) | collective-permute-done | bytes 24608 | tf_op jit(solution)/shard_map/ppermute | solution.py:783
  35.1 3.5 %collective-permute-done.27.east = f32[24,256]{1,0:T(8,128)S(1)} collective-permute-done((f32[24,256]{1,0:T(8,128)S(1)}, f32[24,256]{1,0:T(8,128)S(1)}, u32[]{:S(2)}, u32[]{:S(2)}) %collective-permute-start.27) | collective-permute-done | bytes 24608 | tf_op jit(solution)/shard_map/ppermute | solution.py:784
  38.7 1.9 %shard_map.93 = (f32[4,112,640]{2,1,0:T(8,128)S(1)}, f32[2,112,640]{2,1,0:T(8,128)S(1)}, f32[2,112,640]{2,1,0:T(8,128)S(1)}, f32[2,112,640]{2,1,0:T(8,128)S(1)}, f32[2,96,512]{2,1,0:T(8,128)S(1)}) custom-call(s32[1]{0:T(128)} %bitcast.23.gz, f32[3,192,512]{2,1,0:T(8,128)S(1)} %get-tuple-element.58.plane, f32[2,192,512]{2,1,0:T(8,128)S(1)} %get-tuple-element.57.via, ...), custom_call_target="tpu_custom_call" | custom-call | tf_op jit(solution)/shard_map/pallas_call | solution.py:731
  40.6 0.8 copy-done.4
  41.4 0.8 collective-permute-done.30.small
  42.2 3.2 %shard_map.95 = (f32[2,112,640]{2,1,0:T(8,128)S(1)}, f32[2,112,640]{2,1,0:T(8,128)S(1)}, f32[112,640]{1,0:T(8,128)S(1)}, f32[6,112,640]{2,1,0:T(8,128)S(1)}, f32...) custom-call(s32[1]{0:T(128)} %bitcast.23.gz, ...), custom_call_target="tpu_custom_call" | custom-call | tf_op jit(solution)/shard_map/pallas_call | solution.py:731
  45.4 2.3 %shard_map.96 = (f32[4,96,512]{2,1,0:T(8,128)S(1)}, f32[4,96,512]{2,1,0:T(8,128)}, f32[16,1,128]{2,1,0:T(1,128)S(1)}) custom-call(f32[4,112,640]{2,1,0:T(8,128)S(1)} %get-tuple-element.71.step_1, f32[2,112,640]{2,1,0:T(8,128)S(1)} %get-tuple-element.65.near_e, f32[2,112,640]{2,1,0:T(8,128)S(1)} %get-tuple-element.66.near_n, ...), custom_call_target="tpu_custom_call" | custom-call | tf_op jit(solution)/shard_map/pallas_call | solution.py:731
  47.7 0.9 copy-done
  49.2 0.8 collective-permute-start.31
  50.7 10.1 %all_to_all.10.parts = f32[16,1,128]{2,1,0:T(1,128)S(1)} all-to-all(f32[16,1,128]{2,1,0:T(1,128)S(1)} %get-tuple-element.77), channel_id=1, replica_groups=mesh['gx_0'=8,'gx_1'=2,'gy_0'=2,'gy_1'=4,'gz'=2] {'gx_0','gx_1'}, dimensions={0} | all-to-all | bytes 16384 | tf_op jit(solution)/shard_map/all_to_all | solution.py:818
  61.4 3.5 %all-to-all-start.1 = ((f32[16,1,128]{2,1,0:T(1,128)}), f32[16,1,128]{2,1,0:T(1,128)S(1)}, u32[]{:S(2)}, u32[]{:S(2)}) async-start(f32[16,1,128]{2,1,0:T(1,128)} %shard_map.97), calls=%async_computation.1 | async-start | bytes 16384 | tf_op jit(solution)/shard_map/all_to_all | solution.py:820
  64.9 14.2 %collective-permute-done.32.given = f32[96,512]{1,0:T(8,128)S(1)} collective-permute-done((f32[96,512]{1,0:T(8,128)}, f32[96,512]{1,0:T(8,128)S(1)}, u32[]{:S(2)}, u32[]{:S(2)}) %collective-permute-start.32) | collective-permute-done | bytes 196640 | tf_op jit(solution)/shard_map/ppermute | solution.py:790
  79.8 1.0 %copy-done.5 = f32[2,96,512]{2,1,0:T(8,128)S(1)} copy-done((f32[2,96,512]{2,1,0:T(8,128)S(1)}, f32[2,96,512]{2,1,0:T(8,128)}, u32[]{:S(2)}) %copy-start.5) | copy-done | bytes 393240
  80.8 0.9 %copy-done.7 = f32[96,512]{1,0:T(8,128)S(1)} copy-done((f32[96,512]{1,0:T(8,128)S(1)}, f32[96,512]{1,0:T(8,128)}, u32[]{:S(2)}) %copy-start.7) | copy-done | bytes 196632
  81.9 1.1 %copy-done.1 = f32[4,96,512]{2,1,0:T(8,128)S(1)} copy-done((f32[4,96,512]{2,1,0:T(8,128)S(1)}, f32[4,96,512]{2,1,0:T(8,128)}, u32[]{:S(2)}) %copy-start.1) | copy-done | bytes 786456
  83.0 1.0 %copy-done.3 = f32[2,96,512]{2,1,0:T(8,128)S(1)} copy-done((f32[2,96,512]{2,1,0:T(8,128)S(1)}, f32[2,96,512]{2,1,0:T(8,128)}, u32[]{:S(2)}) %copy-start.3) | copy-done | bytes 393240
  84.0 3.3 %shard_map.99 = (f32[2,192,512]{2,1,0:T(8,128)}, f32[2,192,512]{2,1,0:T(8,128)}, s32[1,128]{1,0:T(1,128)S(1)}) custom-call(s32[1]{0:T(128)} %bitcast.23.gz, f32[2,96,512]{2,1,0:T(8,128)} %collective-permute-done.31.far_0, f32[16,1,128]{2,1,0:T(1,128)S(1)} %all-to-all-done.1.parts, f32[192,512]{1,0:T(8,128)S(1)} %get-tuple-element.59.drawn.current, ...), custom_call_target="tpu_custom_call" | custom-call | tf_op jit(solution)/shard_map/pallas_call | solution.py:731
  (32 shorter events, 4.1 us)
Async XLA Ops:
  0.6 2.5 %copy-start.27 = (s32[2,192,512]{2,1,0:T(8,128)S(1)}, s32[2,192,512]{2,1,0:T(8,128)}, u32[]{:S(2)}) copy-start(s32[2,192,512]{2,1,0:T(8,128)} %classes.3) | copy-start | bytes 2359300
  5.0 37.2 %collective-permute-start.28 = (f32[240,512]{1,0:T(8,128)S(1)}, f32[240,512]{1,0:T(8,128)S(1)}, u32[]{:S(2)}, u32[]{:S(2)}) collective-permute-start(f32[240,512]{1,0:T(8,128)S(1)} %get-tuple-element.68), channel_id=1, source_target_pairs={{0,1},{1,0},{2,3},{3,2},{4,5},{5,4},{6,7},{7,6},{8,9},{9,8},{10,11... | collective-permute-start | bytes 1474568 | tf_op jit(solution)/shard_map/ppermute | solution.py:778
  6.3 35.9 %collective-permute-start.29 = (f32[144,512]{1,0:T(8,128)S(1)}, f32[144,512]{1,0:T(8,128)S(1)}, u32[]{:S(2)}, u32[]{:S(2)}) collective-permute-start(f32[144,512]{1,0:T(8,128)S(1)} %get-tuple-element.69), channel_id=1, source_target_pairs={{0,1},{1,0},{2,3},{3,2},{4,5},{5,4},{6,7},{7,6},{8,9},{9,8},{10,11... | collective-permute-start | bytes 884744 | tf_op jit(solution)/shard_map/ppermute | solution.py:769
  6.5 22.4 %collective-permute-start.24 = (f32[24,512]{1,0:T(8,128)S(1)}, f32[24,512]{1,0:T(8,128)S(1)}, u32[]{:S(2)}, u32[]{:S(2)}) collective-permute-start(f32[24,512]{1,0:T(8,128)S(1)} %get-tuple-element.60), channel_id=1, source_target_pairs={{0,2},{2,4},{4,6},{6,8},{8,10},{10,12},{12,14},{14,0},{1,3},{3,5},... | collective-permute-start | bytes 147464 | tf_op jit(solution)/shard_map/ppermute | solution.py:776
  7.8 21.1 %collective-permute-start.25 = (f32[24,512]{1,0:T(8,128)S(1)}, f32[24,512]{1,0:T(8,128)S(1)}, u32[]{:S(2)}, u32[]{:S(2)}) collective-permute-start(f32[24,512]{1,0:T(8,128)S(1)} %get-tuple-element.61), channel_id=1, source_target_pairs={{2,0},{4,2},{6,4},{8,6},{10,8},{12,10},{14,12},{0,14},{3,1},{5,3},... | collective-permute-start | bytes 147464 | tf_op jit(solution)/shard_map/ppermute | solution.py:777
  29.6 5.5 %collective-permute-start.26 = (f32[24,256]{1,0:T(8,128)S(1)}, f32[24,256]{1,0:T(8,128)S(1)}, u32[]{:S(2)}, u32[]{:S(2)}) collective-permute-start(f32[24,256]{1,0:T(8,128)S(1)} %get-tuple-element.62), channel_id=1, source_target_pairs={{0,16},{16,32},{32,48},{48,64},{64,80},{80,96},{96,112},{112,128},... | collective-permute-start | bytes 73736 | tf_op jit(solution)/shard_map/ppermute | solution.py:783
  34.1 4.5 %collective-permute-start.27 = (f32[24,256]{1,0:T(8,128)S(1)}, f32[24,256]{1,0:T(8,128)S(1)}, u32[]{:S(2)}, u32[]{:S(2)}) collective-permute-start(f32[24,256]{1,0:T(8,128)S(1)} %get-tuple-element.63), channel_id=1, source_target_pairs={{16,0},{32,16},{48,32},{64,48},{80,64},{96,80},{112,96},{128,112},... | collective-permute-start | bytes 73736 | tf_op jit(solution)/shard_map/ppermute | solution.py:784
  38.6 3.6 %collective-permute-start.30 = (f32[48,512]{1,0:T(8,128)S(1)}, f32[48,512]{1,0:T(8,128)S(1)}, u32[]{:S(2)}, u32[]{:S(2)}) collective-permute-start(f32[48,512]{1,0:T(8,128)S(1)} %shard_map.94), channel_id=1, source_target_pairs={{0,1},{1,0},{2,3},{3,2},{4,5},{5,4},{6,7},{7,6},{8,9},{9,8},{10,11... | collective-permute-start | bytes 294920 | tf_op jit(solution)/shard_map/ppermute | solution.py:789
  40.6 0.8 copy-start.4
  45.4 2.3 %copy-start.2 = (f32[2,96,512]{2,1,0:T(8,128)}, f32[2,96,512]{2,1,0:T(8,128)S(1)}, u32[]{:S(2)}) copy-start(f32[2,96,512]{2,1,0:T(8,128)S(1)} %get-tuple-element.81.n_0) | copy-start | bytes 1179652
  47.7 0.9 %copy-start = (f32[4,96,512]{2,1,0:T(8,128)}, f32[4,96,512]{2,1,0:T(8,128)S(1)}, u32[]{:S(2)}) copy-start(f32[4,96,512]{2,1,0:T(8,128)S(1)} %get-tuple-element.82.n_12) | copy-start | bytes 2359300
  48.6 33.3 %collective-permute-start.33 = (f32[4,96,512]{2,1,0:T(8,128)}, f32[4,96,512]{2,1,0:T(8,128)}, u32[]{:S(2)}, u32[]{:S(2)}) collective-permute-start(f32[4,96,512]{2,1,0:T(8,128)} %get-tuple-element.83), channel_id=1, source_target_pairs={{0,1},{1,0},{2,3},{3,2},{4,5},{5,4},{6,7},{7,6},{8,9},{9,8},{10,11... | collective-permute-start | bytes 2359304 | tf_op jit(solution)/shard_map/ppermute | solution.py:817
  49.2 32.6 %collective-permute-start.31 = (f32[2,96,512]{2,1,0:T(8,128)}, f32[2,96,512]{2,1,0:T(8,128)}, u32[]{:S(2)}, u32[]{:S(2)}) collective-permute-start(f32[2,96,512]{2,1,0:T(8,128)} %get-tuple-element.70), channel_id=1, source_target_pairs={{0,1},{1,0},{2,3},{3,2},{4,5},{5,4},{6,7},{7,6},{8,9},{9,8},{10,11... | collective-permute-start | bytes 1179656 | tf_op jit(solution)/shard_map/ppermute | solution.py:806
  50.0 29.0 %collective-permute-start.32 = (f32[96,512]{1,0:T(8,128)}, f32[96,512]{1,0:T(8,128)S(1)}, u32[]{:S(2)}, u32[]{:S(2)}) collective-permute-start(f32[96,512]{1,0:T(8,128)} %get-tuple-element.80), channel_id=1, source_target_pairs={{0,1},{1,0},{2,3},{3,2},{4,5},{5,4},{6,7},{7,6},{8,9},{9,8},{10,11... | collective-permute-start | bytes 589832 | tf_op jit(solution)/shard_map/ppermute | solution.py:790
  61.4 20.5 %all-to-all-start.1 = ((f32[16,1,128]{2,1,0:T(1,128)}), f32[16,1,128]{2,1,0:T(1,128)S(1)}, u32[]{:S(2)}, u32[]{:S(2)}) async-start(f32[16,1,128]{2,1,0:T(1,128)} %shard_map.97), calls=%async_computation.1 | async-start | bytes 16384 | tf_op jit(solution)/shard_map/all_to_all | solution.py:820
  79.1 0.7 copy-start.6
  79.8 1.0 %copy-start.5 = (f32[2,96,512]{2,1,0:T(8,128)S(1)}, f32[2,96,512]{2,1,0:T(8,128)}, u32[]{:S(2)}) copy-start(f32[2,96,512]{2,1,0:T(8,128)} %copy-done.4) | copy-start | bytes 1179652
  80.8 0.9 %copy-start.7 = (f32[96,512]{1,0:T(8,128)S(1)}, f32[96,512]{1,0:T(8,128)}, u32[]{:S(2)}) copy-start(f32[96,512]{1,0:T(8,128)} %copy-done.6) | copy-start | bytes 589828
  81.9 1.1 %copy-start.1 = (f32[4,96,512]{2,1,0:T(8,128)S(1)}, f32[4,96,512]{2,1,0:T(8,128)}, u32[]{:S(2)}) copy-start(f32[4,96,512]{2,1,0:T(8,128)} %copy-done) | copy-start | bytes 2359300
  83.0 1.0 %copy-start.3 = (f32[2,96,512]{2,1,0:T(8,128)S(1)}, f32[2,96,512]{2,1,0:T(8,128)}, u32[]{:S(2)}) copy-start(f32[2,96,512]{2,1,0:T(8,128)} %copy-done.2) | copy-start | bytes 1179652
  84.0 3.3 %copy-start.33 = (f32[2,8]{1,0:T(2,128)S(1)}, f32[2,8]{1,0:T(2,128)}, u32[]{:S(2)}) copy-start(f32[2,8]{1,0:T(2,128)} %table.3) | copy-start | bytes 196
  84.0 3.3 %copy-start.34 = (f32[2,8]{1,0:T(2,128)S(1)}, f32[2,8]{1,0:T(2,128)}, u32[]{:S(2)}) copy-start(f32[2,8]{1,0:T(2,128)} %table.2) | copy-start | bytes 196

commit v8 on v7

--- a/solution.py
+++ b/solution.py
@@ -423,7 +423,7 @@
     return jnp.sum(total, axis=0, keepdims=True)
 
 
-PAIRS = ((0, 0, 2), (1, 2, 0))
+PAIRS = ((1, 2, 0), (0, 0, 2))
 
 
 def image_pass(field, edges, cross, blocks, done, pairs=PAIRS):
@@ -488,8 +488,8 @@
     return sums
 
 
-def edge_kernel(gz, near, near_e, near_n, near_sum, three, first, small, far_e, far_n, cross, inverse, step_1, n_own, inv_own, send, part, *scratch):
-    fields, step_0, flat, tall = scratch
+def edge_kernel(gz, near, near_e, near_n, near_sum, three, first, small, out, far_e, far_n, cross, inverse, step_1, n_own, inv_own, part, *scratch):
+    fields, step_0, flat, tall, send, sems = scratch
     group = gz[0]
     n_cols = first.shape[1]
     half = (first.shape[0] + three.shape[0]) // N_FAR
@@ -562,14 +562,24 @@
     part[...] = jnp.zeros(part.shape, jnp.float32)
     part[0:1, :] = fold(total)
     edges, keep = ((near_e, near_n), (far_e, far_n)), (n_own, send)
-    for q in range(2):
-
-        @pl.when(group == q)
-        def _(q=q):
-            first_step(q, step_0, edges, cross, inverse, step_1, keep, part)
-
-
-def first_step(q, step_0, edges, cross, inverse, step_1, keep, part):
+    copies = []
+    for piece in range(2):
+        blocks = range(piece * n_blocks // 2, (piece + 1) * n_blocks // 2)
+        for q in range(2):
+
+            @pl.when(group == q)
+            def _(q=q, blocks=blocks):
+                first_step(q, blocks, step_0, edges, cross, inverse, step_1, keep, part)
+
+        rows = pl.ds(piece * (half // 2), half // 2)
+        copy = pltpu.make_async_copy(send.at[:, rows, :], out.at[:, rows, :], sems.at[piece])
+        copy.start()
+        copies.append(copy)
+    for copy in copies:
+        copy.wait()
+
+
+def first_step(q, blocks, step_0, edges, cross, inverse, step_1, keep, part):
     n_cols = keep[0].shape[2]
     n_blocks, p = step_0.shape[1] // STEP, 1 - q
     sums = [jnp.zeros((STEP, n_cols), jnp.float32)] * 2
@@ -592,18 +602,24 @@
             sums[0] = sums[0] + dot(owns, outs, n_cols)
             sums[1] = sums[1] + (dot(news, outs, n_cols) + (facing * over)[:, :n_cols])
 
-    image_pass(step_0, edges, cross, range(n_blocks), done, ((q, 0, None),))
-    part[1:2, :] = fold(sums[0])
-    part[2:3, :] = fold(sums[1])
-
-
-def steps_kernel(step_1, near_e, near_n, far_e, far_n, cross, inverse, before, n_own, send, spread, step_2):
+    image_pass(step_0, edges, cross, blocks, done, ((q, 0, None),))
+    part[1:2, :] = part[1:2, :] + fold(sums[0])
+    part[2:3, :] = part[2:3, :] + fold(sums[1])
+
+
+def steps_kernel(step_1, near_e, near_n, far_e, far_n, cross, inverse, before, out, n_own, spread, step_2, send, sems):
     n_cols = n_own.shape[2]
     edges = ((near_e, near_n), (far_e, far_n))
     first, second = pl.ds(0, 2), pl.ds(2, 2)
+    copies = [
+        pltpu.make_async_copy(send.at[part], out.at[part], sems.at[j])
+        for j, part in enumerate((first, second))
+    ]
+    last = step_1.shape[1] // STEP - 2
     sums = image_step(
         step_1, edges, cross, inverse, step_2, (n_own.at[first], send.at[first]), n_cols
     )
+    copies[0].start()
     keep = (n_own.at[second], send.at[second])
     sums.append(jnp.zeros((STEP, n_cols), jnp.float32))
 
@@ -611,8 +627,10 @@
         for layer in range(2):
             keep[q][layer, pl.ds((k - 1) * STEP, STEP), :] = outs[layer][:, :n_cols]
         sums[2] = sums[2] + dot(owns, outs, n_cols)
-
-    image_pass(step_2, edges, cross, range(1, step_1.shape[1] // STEP - 1), done)
+        if q == 1 and k == last:
+            copies[1].start()
+
+    image_pass(step_2, edges, cross, range(1, last + 1), done)
     row = lax.broadcasted_iota(jnp.int32, before.shape, 0)
     part = before[...]
     for j in range(3):
@@ -622,6 +640,8 @@
     line = jnp.sum(jnp.where(lane == row, sums, 0.0), axis=0, keepdims=True)
     for k in range(spread.shape[0]):
         spread[k] = line
+    for copy in copies:
+        copy.wait()
 
 
 def inverse_kernel(gz, plane, via, sums, given, inverse):
@@ -743,7 +763,7 @@
     half, frame = n_rows // 2, n_rows // 2 + 2 * STEP
     tall = -(-(n_rows + 2 * STEP) // LANES) * LANES
     broad = n_cols + LANES
-    head = half * 6 // 12
+    head = half * 4 // 12
 
     def array(*shape):
         return jax.ShapeDtypeStruct(shape, jnp.float32)
@@ -794,25 +814,26 @@
         [pltpu.VMEM((2, n_rows + 2 * STEP, broad), jnp.float32)] + turn,
         1, gz, plane, via, drawn, south, north, west, east,
     )
-    far_e, far_n, cross, inverse, step_1, n_0, inv_near, send, part = call(
+    send, far_e, far_n, cross, inverse, step_1, n_0, inv_near, part = call(
         edge_kernel,
-        [array(2, frame, broad)] * 2
+        [array(2, half, n_cols)] + [array(2, frame, broad)] * 2
         + [array(frame, broad), array(6, frame, broad), array(4, frame, broad),
-           array(2, half, n_cols), array(3, half, n_cols), array(2, half, n_cols), array(STEP, LANES)],
+           array(2, half, n_cols), array(3, half, n_cols), array(STEP, LANES)],
         [pltpu.VMEM((N_FAR, frame, broad), jnp.float32), pltpu.VMEM((2, frame, broad), jnp.float32)]
-        + turn,
-        1, gz, near, near_e, near_n, near_sum, big_plane, big_via, small,
+        + turn + [pltpu.VMEM((2, half, n_cols), jnp.float32), pltpu.SemaphoreType.DMA((2,))],
+        1, gz, near, near_e, near_n, near_sum, big_plane, big_via, small, outside=1,
     )
     n_0_far = lax.ppermute(send, "gz", swap)
     (inv_far,) = call(
         inverse_kernel, [array(3, half, n_cols)], [], 1,
         gz, plane, via, far_sum, via_far,
     )
-    n_12, send, spread = call(
+    send, n_12, spread = call(
         steps_kernel,
         [array(4, half, n_cols), array(4, half, n_cols), array(n_gx, 1, LANES)],
-        [pltpu.VMEM((4, frame, broad), jnp.float32)],
-        0, step_1, near_e, near_n, far_e, far_n, cross, inverse, part,
+        [pltpu.VMEM((4, frame, broad), jnp.float32), pltpu.VMEM((4, half, n_cols), jnp.float32),
+         pltpu.SemaphoreType.DMA((2,))],
+        0, step_1, near_e, near_n, far_e, far_n, cross, inverse, part, outside=1,
     )
     n_12_far = lax.ppermute(send, "gz", swap)
     parts = lax.all_to_all(spread, GX, 0, 0, tiled=True)

time: 88.2 us -> 87.8 us (level)
  no operation moved by 1% of the time
where the time goes in v8:
time: 87.8 us; the launch traced here: 87.4 us
  waiting for transfers between devices  36.6 us (42%)
  starting transfers between devices  17 us (19%)
  Pallas kernels  16 us (18%)
  blocking collectives  10.1 us (12%)
  local copies, waits for them, and re-layouts  6.38 us (7%)
  between operations  1 us (1%)
    ppermute x1, waiting for transfers between devices, shards(): south = lax.ppermute(bottom, GY, ring(GY))  17.2 us
    pallas_call x10, Pallas kernels, call(): pl.pallas_call(kernel, in_specs=[SMEM] * n_smem + [OUTSIDE] * far + [VMEM...  16 us
    ppermute x1, waiting for transfers between devices, shards(): via_far = lax.ppermute(via_send, 'gz', swap)  14.2 us
    all_to_all x1, blocking collectives, shards(): parts = lax.all_to_all(spread, GX, 0, 0, tiled=True)  10.1 us
    unnamed x22, local copies, waits for them, and re-layouts  6.38 us
    ppermute x1, starting transfers between devices, shards(): west = lax.ppermute(last, GX, ring(GX))  4.57 us
    ppermute x1, starting transfers between devices, shards(): north = lax.ppermute(top, GY, back(ring(GY)))  3.9 us
    ppermute x1, waiting for transfers between devices, shards(): east = lax.ppermute(first, GX, back(ring(GX)))  3.52 us
  transfers between devices with their start and end apart: 11, of which 5 were waited for; matrix products, arithmetic and copies ran while one was open for 0% of the time, Pallas kernels for 4%

profile of v8, /device:TPU:97, one launch (start us, length us, event | category | flops | bytes accessed | tf_op | source)
XLA Modules:
  0.0 87.4 jit_solution(10606157560755410622)
XLA Ops:
  0.6 2.5 %shard_map.90 = (f32[2,192,512]{2,1,0:T(8,128)S(1)}, f32[128,512]{1,0:T(8,128)S(1)}, f32[96,512]{1,0:T(8,128)}) custom-call(s32[1]{0:T(128)} %bitcast.23.gz, f32[2,8]{1,0:T(2,128)} %table.2, s32[2,192,512]{2,1,0:T(8,128)} %classes.2), custom_call_target="tpu_custom_call" | custom-call | tf_op jit(solution)/shard_map/pallas_call | solution.py:751
  3.1 1.9 %shard_map.91 = (f32[3,192,512]{2,1,0:T(8,128)S(1)}, f32[192,512]{1,0:T(8,128)S(1)}, f32[256,512]{1,0:T(8,128)S(1)}, f32[24,512]{1,0:T(8,128)S(1)}, f32[24,512]{1,0:T(8,128)S(1)}) custom-call(s32[1]{0:T(128)} %bitcast.23.gz, f32[2,8]{1,0:T(2,128)} %table.3, s32[2,192,512]{2,1,0:T(8,128)S(1)} %copy-done.27, f32[192,512]{1,0:T(8,128)} %load.1, ...), custom_call_target="tpu_custom_call" | custom-call | tf_op jit(solution)/shard_map/pallas_call | solution.py:751
  5.0 1.3 %collective-permute-start.28 = (f32[256,512]{1,0:T(8,128)S(1)}, f32[256,512]{1,0:T(8,128)S(1)}, u32[]{:S(2)}, u32[]{:S(2)}) collective-permute-start(f32[256,512]{1,0:T(8,128)S(1)} %get-tuple-element.68), channel_id=1, source_target_pairs={{0,1},{1,0},{2,3},{3,2},{4,5},{5,4},{6,7},{7,6},{8,9},{9,8},{10,11... | collective-permute-start | bytes 1572872 | tf_op jit(solution)/shard_map/ppermute | solution.py:798
  6.5 1.3 %collective-permute-start.24 = (f32[24,512]{1,0:T(8,128)S(1)}, f32[24,512]{1,0:T(8,128)S(1)}, u32[]{:S(2)}, u32[]{:S(2)}) collective-permute-start(f32[24,512]{1,0:T(8,128)S(1)} %get-tuple-element.60), channel_id=1, source_target_pairs={{0,2},{2,4},{4,6},{6,8},{8,10},{10,12},{12,14},{14,0},{1,3},{3,5},... | collective-permute-start | bytes 147464 | tf_op jit(solution)/shard_map/ppermute | solution.py:796
  7.8 3.9 %collective-permute-start.25 = (f32[24,512]{1,0:T(8,128)S(1)}, f32[24,512]{1,0:T(8,128)S(1)}, u32[]{:S(2)}, u32[]{:S(2)}) collective-permute-start(f32[24,512]{1,0:T(8,128)S(1)} %get-tuple-element.61), channel_id=1, source_target_pairs={{2,0},{4,2},{6,4},{8,6},{10,8},{12,10},{14,12},{0,14},{3,1},{5,3},... | collective-permute-start | bytes 147464 | tf_op jit(solution)/shard_map/ppermute | solution.py:797
  11.7 17.2 %collective-permute-done.24.south = f32[24,512]{1,0:T(8,128)S(1)} collective-permute-done((f32[24,512]{1,0:T(8,128)S(1)}, f32[24,512]{1,0:T(8,128)S(1)}, u32[]{:S(2)}, u32[]{:S(2)}) %collective-permute-start.24) | collective-permute-done | bytes 49184 | tf_op jit(solution)/shard_map/ppermute | solution.py:796
  29.6 4.6 %collective-permute-start.26 = (f32[24,256]{1,0:T(8,128)S(1)}, f32[24,256]{1,0:T(8,128)S(1)}, u32[]{:S(2)}, u32[]{:S(2)}) collective-permute-start(f32[24,256]{1,0:T(8,128)S(1)} %get-tuple-element.62), channel_id=1, source_target_pairs={{0,16},{16,32},{32,48},{48,64},{64,80},{80,96},{96,112},{112,128},... | collective-permute-start | bytes 73736 | tf_op jit(solution)/shard_map/ppermute | solution.py:803
  34.1 0.9 %collective-permute-done.26.west = f32[24,256]{1,0:T(8,128)S(1)} collective-permute-done((f32[24,256]{1,0:T(8,128)S(1)}, f32[24,256]{1,0:T(8,128)S(1)}, u32[]{:S(2)}, u32[]{:S(2)}) %collective-permute-start.26) | collective-permute-done | bytes 24608 | tf_op jit(solution)/shard_map/ppermute | solution.py:803
  35.1 3.5 %collective-permute-done.27.east = f32[24,256]{1,0:T(8,128)S(1)} collective-permute-done((f32[24,256]{1,0:T(8,128)S(1)}, f32[24,256]{1,0:T(8,128)S(1)}, u32[]{:S(2)}, u32[]{:S(2)}) %collective-permute-start.27) | collective-permute-done | bytes 24608 | tf_op jit(solution)/shard_map/ppermute | solution.py:804
  38.7 1.9 %shard_map.93 = (f32[4,112,640]{2,1,0:T(8,128)S(1)}, f32[2,112,640]{2,1,0:T(8,128)S(1)}, f32[2,112,640]{2,1,0:T(8,128)S(1)}, f32[2,112,640]{2,1,0:T(8,128)S(1)}, f32[2,96,512]{2,1,0:T(8,128)S(1)}) custom-call(s32[1]{0:T(128)} %bitcast.23.gz, f32[3,192,512]{2,1,0:T(8,128)S(1)} %get-tuple-element.58.plane, f32[2,192,512]{2,1,0:T(8,128)S(1)} %get-tuple-element.57.via, ...), custom_call_target="tpu_custom_call" | custom-call | tf_op jit(solution)/shard_map/pallas_call | solution.py:751
  40.6 0.8 copy-done.4
  41.4 0.8 collective-permute-done.30.small
  42.2 3.2 %shard_map.95 = (f32[2,96,512]{2,1,0:T(8,128)}, f32[2,112,640]{2,1,0:T(8,128)S(1)}, f32[2,112,640]{2,1,0:T(8,128)S(1)}, f32[112,640]{1,0:T(8,128)S(1)}, f32[6,11...) custom-call(s32[1]{0:T(128)} %bitcast.23.gz, ...), custom_call_target="tpu_custom_call" | custom-call | tf_op jit(solution)/shard_map/pallas_call | solution.py:751
  45.4 1.9 %shard_map.96 = (f32[4,96,512]{2,1,0:T(8,128)}, f32[4,96,512]{2,1,0:T(8,128)S(1)}, f32[16,1,128]{2,1,0:T(1,128)S(1)}) custom-call(f32[4,112,640]{2,1,0:T(8,128)S(1)} %get-tuple-element.71.step_1, f32[2,112,640]{2,1,0:T(8,128)S(1)} %get-tuple-element.65.near_e, f32[2,112,640]{2,1,0:T(8,128)S(1)} %get-tuple-element.66.near_n, ...), custom_call_target="tpu_custom_call" | custom-call | tf_op jit(solution)/shard_map/pallas_call | solution.py:751
  47.3 0.9 copy-done
  48.8 0.8 collective-permute-start.31
  50.3 10.1 %all_to_all.10.parts = f32[16,1,128]{2,1,0:T(1,128)S(1)} all-to-all(f32[16,1,128]{2,1,0:T(1,128)S(1)} %get-tuple-element.77), channel_id=1, replica_groups=mesh['gx_0'=8,'gx_1'=2,'gy_0'=2,'gy_1'=4,'gz'=2] {'gx_0','gx_1'}, dimensions={0} | all-to-all | bytes 16384 | tf_op jit(solution)/shard_map/all_to_all | solution.py:839
  61.0 3.5 %all-to-all-start.1 = ((f32[16,1,128]{2,1,0:T(1,128)}), f32[16,1,128]{2,1,0:T(1,128)S(1)}, u32[]{:S(2)}, u32[]{:S(2)}) async-start(f32[16,1,128]{2,1,0:T(1,128)} %shard_map.97), calls=%async_computation.1 | async-start | bytes 16384 | tf_op jit(solution)/shard_map/all_to_all | solution.py:841
  64.4 14.2 %collective-permute-done.32.given = f32[96,512]{1,0:T(8,128)S(1)} collective-permute-done((f32[96,512]{1,0:T(8,128)}, f32[96,512]{1,0:T(8,128)S(1)}, u32[]{:S(2)}, u32[]{:S(2)}) %collective-permute-start.32) | collective-permute-done | bytes 196640 | tf_op jit(solution)/shard_map/ppermute | solution.py:810
  79.3 1.0 %copy-done.5 = f32[2,96,512]{2,1,0:T(8,128)S(1)} copy-done((f32[2,96,512]{2,1,0:T(8,128)S(1)}, f32[2,96,512]{2,1,0:T(8,128)}, u32[]{:S(2)}) %copy-start.5) | copy-done | bytes 393240
  80.3 0.9 %copy-done.7 = f32[96,512]{1,0:T(8,128)S(1)} copy-done((f32[96,512]{1,0:T(8,128)S(1)}, f32[96,512]{1,0:T(8,128)}, u32[]{:S(2)}) %copy-start.7) | copy-done | bytes 196632
  81.5 1.1 %copy-done.1 = f32[4,96,512]{2,1,0:T(8,128)S(1)} copy-done((f32[4,96,512]{2,1,0:T(8,128)S(1)}, f32[4,96,512]{2,1,0:T(8,128)}, u32[]{:S(2)}) %copy-start.1) | copy-done | bytes 786456
  82.6 1.0 %copy-done.3 = f32[2,96,512]{2,1,0:T(8,128)S(1)} copy-done((f32[2,96,512]{2,1,0:T(8,128)S(1)}, f32[2,96,512]{2,1,0:T(8,128)}, u32[]{:S(2)}) %copy-start.3) | copy-done | bytes 393240
  83.6 3.3 %shard_map.99 = (f32[2,192,512]{2,1,0:T(8,128)}, f32[2,192,512]{2,1,0:T(8,128)}, s32[1,128]{1,0:T(1,128)S(1)}) custom-call(s32[1]{0:T(128)} %bitcast.23.gz, f32[2,96,512]{2,1,0:T(8,128)} %collective-permute-done.31.far_0, f32[16,1,128]{2,1,0:T(1,128)S(1)} %all-to-all-done.1.parts, f32[192,512]{1,0:T(8,128)S(1)} %get-tuple-element.59.drawn.current, ...), custom_call_target="tpu_custom_call" | custom-call | tf_op jit(solution)/shard_map/pallas_call | solution.py:751
  (32 shorter events, 4.1 us)
Async XLA Ops:
  0.6 2.5 %copy-start.27 = (s32[2,192,512]{2,1,0:T(8,128)S(1)}, s32[2,192,512]{2,1,0:T(8,128)}, u32[]{:S(2)}) copy-start(s32[2,192,512]{2,1,0:T(8,128)} %classes.3) | copy-start | bytes 2359300
  5.0 37.2 %collective-permute-start.28 = (f32[256,512]{1,0:T(8,128)S(1)}, f32[256,512]{1,0:T(8,128)S(1)}, u32[]{:S(2)}, u32[]{:S(2)}) collective-permute-start(f32[256,512]{1,0:T(8,128)S(1)} %get-tuple-element.68), channel_id=1, source_target_pairs={{0,1},{1,0},{2,3},{3,2},{4,5},{5,4},{6,7},{7,6},{8,9},{9,8},{10,11... | collective-permute-start | bytes 1572872 | tf_op jit(solution)/shard_map/ppermute | solution.py:798
  6.3 35.9 %collective-permute-start.29 = (f32[128,512]{1,0:T(8,128)S(1)}, f32[128,512]{1,0:T(8,128)S(1)}, u32[]{:S(2)}, u32[]{:S(2)}) collective-permute-start(f32[128,512]{1,0:T(8,128)S(1)} %get-tuple-element.69), channel_id=1, source_target_pairs={{0,1},{1,0},{2,3},{3,2},{4,5},{5,4},{6,7},{7,6},{8,9},{9,8},{10,11... | collective-permute-start | bytes 786440 | tf_op jit(solution)/shard_map/ppermute | solution.py:789
  6.5 22.4 %collective-permute-start.24 = (f32[24,512]{1,0:T(8,128)S(1)}, f32[24,512]{1,0:T(8,128)S(1)}, u32[]{:S(2)}, u32[]{:S(2)}) collective-permute-start(f32[24,512]{1,0:T(8,128)S(1)} %get-tuple-element.60), channel_id=1, source_target_pairs={{0,2},{2,4},{4,6},{6,8},{8,10},{10,12},{12,14},{14,0},{1,3},{3,5},... | collective-permute-start | bytes 147464 | tf_op jit(solution)/shard_map/ppermute | solution.py:796
  7.8 21.1 %collective-permute-start.25 = (f32[24,512]{1,0:T(8,128)S(1)}, f32[24,512]{1,0:T(8,128)S(1)}, u32[]{:S(2)}, u32[]{:S(2)}) collective-permute-start(f32[24,512]{1,0:T(8,128)S(1)} %get-tuple-element.61), channel_id=1, source_target_pairs={{2,0},{4,2},{6,4},{8,6},{10,8},{12,10},{14,12},{0,14},{3,1},{5,3},... | collective-permute-start | bytes 147464 | tf_op jit(solution)/shard_map/ppermute | solution.py:797
  29.6 5.5 %collective-permute-start.26 = (f32[24,256]{1,0:T(8,128)S(1)}, f32[24,256]{1,0:T(8,128)S(1)}, u32[]{:S(2)}, u32[]{:S(2)}) collective-permute-start(f32[24,256]{1,0:T(8,128)S(1)} %get-tuple-element.62), channel_id=1, source_target_pairs={{0,16},{16,32},{32,48},{48,64},{64,80},{80,96},{96,112},{112,128},... | collective-permute-start | bytes 73736 | tf_op jit(solution)/shard_map/ppermute | solution.py:803
  34.1 4.5 %collective-permute-start.27 = (f32[24,256]{1,0:T(8,128)S(1)}, f32[24,256]{1,0:T(8,128)S(1)}, u32[]{:S(2)}, u32[]{:S(2)}) collective-permute-start(f32[24,256]{1,0:T(8,128)S(1)} %get-tuple-element.63), channel_id=1, source_target_pairs={{16,0},{32,16},{48,32},{64,48},{80,64},{96,80},{112,96},{128,112},... | collective-permute-start | bytes 73736 | tf_op jit(solution)/shard_map/ppermute | solution.py:804
  38.6 3.6 %collective-permute-start.30 = (f32[48,512]{1,0:T(8,128)S(1)}, f32[48,512]{1,0:T(8,128)S(1)}, u32[]{:S(2)}, u32[]{:S(2)}) collective-permute-start(f32[48,512]{1,0:T(8,128)S(1)} %shard_map.94), channel_id=1, source_target_pairs={{0,1},{1,0},{2,3},{3,2},{4,5},{5,4},{6,7},{7,6},{8,9},{9,8},{10,11... | collective-permute-start | bytes 294920 | tf_op jit(solution)/shard_map/ppermute | solution.py:809
  40.6 0.8 copy-start.4
  45.4 1.9 %copy-start.2 = (f32[2,96,512]{2,1,0:T(8,128)}, f32[2,96,512]{2,1,0:T(8,128)S(1)}, u32[]{:S(2)}) copy-start(f32[2,96,512]{2,1,0:T(8,128)S(1)} %get-tuple-element.81.n_0) | copy-start | bytes 1179652
  47.3 0.9 %copy-start = (f32[4,96,512]{2,1,0:T(8,128)}, f32[4,96,512]{2,1,0:T(8,128)S(1)}, u32[]{:S(2)}) copy-start(f32[4,96,512]{2,1,0:T(8,128)S(1)} %get-tuple-element.82.n_12) | copy-start | bytes 2359300
  48.1 33.3 %collective-permute-start.33 = (f32[4,96,512]{2,1,0:T(8,128)}, f32[4,96,512]{2,1,0:T(8,128)}, u32[]{:S(2)}, u32[]{:S(2)}) collective-permute-start(f32[4,96,512]{2,1,0:T(8,128)} %get-tuple-element.83), channel_id=1, source_target_pairs={{0,1},{1,0},{2,3},{3,2},{4,5},{5,4},{6,7},{7,6},{8,9},{9,8},{10,11... | collective-permute-start | bytes 2359304 | tf_op jit(solution)/shard_map/ppermute | solution.py:838
  48.8 32.6 %collective-permute-start.31 = (f32[2,96,512]{2,1,0:T(8,128)}, f32[2,96,512]{2,1,0:T(8,128)}, u32[]{:S(2)}, u32[]{:S(2)}) collective-permute-start(f32[2,96,512]{2,1,0:T(8,128)} %get-tuple-element.70), channel_id=1, source_target_pairs={{0,1},{1,0},{2,3},{3,2},{4,5},{5,4},{6,7},{7,6},{8,9},{9,8},{10,11... | collective-permute-start | bytes 1179656 | tf_op jit(solution)/shard_map/ppermute | solution.py:826
  49.6 29.0 %collective-permute-start.32 = (f32[96,512]{1,0:T(8,128)}, f32[96,512]{1,0:T(8,128)S(1)}, u32[]{:S(2)}, u32[]{:S(2)}) collective-permute-start(f32[96,512]{1,0:T(8,128)} %get-tuple-element.80), channel_id=1, source_target_pairs={{0,1},{1,0},{2,3},{3,2},{4,5},{5,4},{6,7},{7,6},{8,9},{9,8},{10,11... | collective-permute-start | bytes 589832 | tf_op jit(solution)/shard_map/ppermute | solution.py:810
  61.0 20.5 %all-to-all-start.1 = ((f32[16,1,128]{2,1,0:T(1,128)}), f32[16,1,128]{2,1,0:T(1,128)S(1)}, u32[]{:S(2)}, u32[]{:S(2)}) async-start(f32[16,1,128]{2,1,0:T(1,128)} %shard_map.97), calls=%async_computation.1 | async-start | bytes 16384 | tf_op jit(solution)/shard_map/all_to_all | solution.py:841
  78.7 0.7 copy-start.6
  79.3 1.0 %copy-start.5 = (f32[2,96,512]{2,1,0:T(8,128)S(1)}, f32[2,96,512]{2,1,0:T(8,128)}, u32[]{:S(2)}) copy-start(f32[2,96,512]{2,1,0:T(8,128)} %copy-done.4) | copy-start | bytes 1179652
  80.3 0.9 %copy-start.7 = (f32[96,512]{1,0:T(8,128)S(1)}, f32[96,512]{1,0:T(8,128)}, u32[]{:S(2)}) copy-start(f32[96,512]{1,0:T(8,128)} %copy-done.6) | copy-start | bytes 589828
  81.5 1.1 %copy-start.1 = (f32[4,96,512]{2,1,0:T(8,128)S(1)}, f32[4,96,512]{2,1,0:T(8,128)}, u32[]{:S(2)}) copy-start(f32[4,96,512]{2,1,0:T(8,128)} %copy-done) | copy-start | bytes 2359300
  82.6 1.0 %copy-start.3 = (f32[2,96,512]{2,1,0:T(8,128)S(1)}, f32[2,96,512]{2,1,0:T(8,128)}, u32[]{:S(2)}) copy-start(f32[2,96,512]{2,1,0:T(8,128)} %copy-done.2) | copy-start | bytes 1179652
  83.6 3.3 %copy-start.33 = (f32[2,8]{1,0:T(2,128)S(1)}, f32[2,8]{1,0:T(2,128)}, u32[]{:S(2)}) copy-start(f32[2,8]{1,0:T(2,128)} %table.3) | copy-start | bytes 196
  83.6 3.3 %copy-start.34 = (f32[2,8]{1,0:T(2,128)S(1)}, f32[2,8]{1,0:T(2,128)}, u32[]{:S(2)}) copy-start(f32[2,8]{1,0:T(2,128)} %table.2) | copy-start | bytes 196
